TPU v7x, 32 devices: a whole 2x2x4 slice. The times are simulated.
32 devices in a mesh: cfg: 2 (over y), tm: 4 (over z), space: 2 (over x), spin: 2 (over core).
Axes of the slice: x: 2, y: 2, z: 4, core: 2. Of those that a mesh axis runs over, the one named last changes fastest.
Arguments:
- eigenvectors: bfloat16 [16, 2048, 3, 128], P(('cfg', 'tm'), ('space', 'spin')), parts along dimension 0, may hold values from -1.25 to 1.25
- momenta: int32 [8, 3], replicated, may hold values from -2 to 2, as said below
- time_pairs: int32 [32, 2], P(('cfg', 'tm')), parts along dimension 0, may hold values from 0 to 7
- slot_map: int32 [8], replicated, may hold values from 0 to 7, each once
- perambulators: bfloat16 [32, 64, 2048], P(('cfg', 'tm')), parts along dimension 0, may hold values from -0.046875 to 0.046875
Outputs:
- meson_loops: bfloat16 [32, 8, 64, 16, 128], P(('cfg', 'tm'), None, ('space', 'spin')), parts along dimension 0
There are 2 independent parts, one for each index of `cfg`. A program takes and returns all parts, laid end to end along the dimension named above; an argument that names none is the same for every part. Nothing has to cross between parts.
Inputs may be any that keep to these rules, and one draw needn't show every extreme that they name: `momenta`: every momentum row has a component that is not zero. slot_map is a permutation of the 8 stored rows.
All inputs are finite; a program needn't handle non-finite values.
Results may differ from a plain program's by a relative error of at most 0.0074.
Values may be sent and summed in bfloat16 or wider, within the bound.
No kernel may reach another device: no remote copies, remote signals or barrier semaphores. Data moves between devices by JAX's collectives and lax.ppermute only.
A program may use at most 64 MiB of HBM per device.

v0:
```python
import jax
import jax.numpy as jnp
from jax import lax
from jax.sharding import PartitionSpec as P

LAT = 32


TURN = 6.283185307179586


def elemental(time_slab, momenta, first_site):
    site_count = time_slab.shape[0]
    vectors = time_slab.shape[2] // 2
    site_ids = first_site + lax.iota(jnp.int32, site_count)
    coord_x = site_ids % LAT
    coord_y = site_ids // LAT % LAT
    coord_z = site_ids // (LAT * LAT)
    real_part = time_slab[:, :, :vectors].astype(jnp.float32)
    imag_part = time_slab[:, :, vectors:].astype(jnp.float32)
    conj_left = time_slab.reshape(site_count * 6, vectors)
    results = []
    for momentum_row in range(momenta.shape[0]):
        wavenum = jnp.mod(
            momenta[momentum_row, 0] * coord_x
            + momenta[momentum_row, 1] * coord_y
            + momenta[momentum_row, 2] * coord_z,
            LAT,
        )
        angles = wavenum.astype(jnp.float32) * (TURN / LAT)
        cosine = jnp.cos(angles)[:, None, None]
        sines = jnp.sin(angles)[:, None, None]
        turned_real = cosine * real_part - sines * imag_part
        turned_imag = sines * real_part + cosine * imag_part
        upper_rows = jnp.concatenate([turned_real, turned_imag], axis=-1)
        lower_rows = jnp.concatenate([turned_imag, -turned_real], axis=-1)
        phased = (
            jnp.stack([upper_rows, lower_rows], axis=2)
            .reshape(site_count * 6, 2 * vectors)
            .astype(jnp.bfloat16)
        )
        results.append(
            lax.dot_general(
                conj_left, phased, (((0,), (0,)), ((), ())), preferred_element_type=jnp.float32
            )
        )
    return jnp.stack(results)


def contract(sink_rows, source_full, perambulators):
    pair_count, moms, share_rows, width = sink_rows.shape
    vectors = width // 2
    parts = perambulators.reshape(pair_count, vectors, 16, 2, vectors)
    lower = jnp.stack([-parts[:, :, :, 1], parts[:, :, :, 0]], axis=3).reshape(
        pair_count, vectors, 32 * vectors
    )
    right_side = jnp.concatenate([perambulators, lower], axis=1)
    left_side = sink_rows.reshape(pair_count, moms * share_rows, width)
    halfway = jnp.einsum(
        "kmx,kxc->kmc", left_side, right_side, preferred_element_type=jnp.float32
    ).astype(jnp.bfloat16)
    halfway = halfway.reshape(pair_count, moms, share_rows * 16, width)
    source_parts = source_full.reshape(pair_count, moms, vectors, 2, vectors)
    swapped = jnp.stack([-source_parts[:, :, :, 1], source_parts[:, :, :, 0]], axis=3).reshape(
        pair_count, moms, vectors, width
    )
    conjugate = jnp.stack([source_full, swapped], axis=2).reshape(pair_count, moms, width, width)
    loops = jnp.einsum("kpmx,kpnx->kpmn", halfway, conjugate, preferred_element_type=jnp.float32)
    return loops.astype(jnp.bfloat16).reshape(pair_count, moms, share_rows, 16, width)


def picker(targets, offset, number):
    return (targets[:, None] == offset + lax.iota(jnp.int32, number)[None, :]).astype(jnp.bfloat16)


def per_device(eigenvectors, momenta, time_pairs, slot_map, perambulators):
    groups = lax.axis_size(("space", "spin"))
    position = lax.axis_index(("space", "spin"))
    site_count = eigenvectors.shape[1]
    vectors = perambulators.shape[1]
    share_rows = vectors // groups
    pair_count = time_pairs.shape[0]
    moms = momenta.shape[0]
    width = 2 * vectors
    partial_value = lax.map(
        lambda time_slab: elemental(time_slab, momenta, position * site_count), eigenvectors
    )
    sink_slot = slot_map[time_pairs[:, 0]]
    source_slot = slot_map[time_pairs[:, 1]]
    row_share = lax.psum_scatter(
        partial_value, ("space", "spin"), scatter_dimension=2, tiled=True
    ).astype(jnp.bfloat16)
    initial = (
        jnp.zeros((pair_count, moms * share_rows * width), jnp.float32),
        jnp.zeros((pair_count, moms * share_rows * width), jnp.float32),
    )
    arrived = jax.tree.map(lambda part: lax.all_gather(part, "tm", axis=0, tiled=True), row_share)
    anchor = jnp.int32(0)
    number = arrived.shape[0]
    flat = arrived.reshape(number, -1)
    sink_acc = initial[0] + jnp.dot(
        picker(sink_slot, anchor, number), flat, preferred_element_type=jnp.float32
    )
    source_acc = initial[1] + jnp.dot(
        picker(source_slot, anchor, number), flat, preferred_element_type=jnp.float32
    )
    sink_rows = sink_acc.astype(jnp.bfloat16).reshape(pair_count, moms, share_rows, width)
    source_share = source_acc.astype(jnp.bfloat16).reshape(pair_count, moms, share_rows, width)
    source_full = lax.all_gather(source_share, ("space", "spin"), axis=2, tiled=True)
    return contract(sink_rows, source_full, perambulators)


def solution(mesh):
    placed = (
        P(("cfg", "tm"), ("space", "spin"), None, None),
        P(),
        P(("cfg", "tm"), None),
        P(),
        P(("cfg", "tm"), None, None),
    )
    return jax.shard_map(
        per_device,
        mesh=mesh,
        in_specs=placed,
        out_specs=P(("cfg", "tm"), None, ("space", "spin"), None, None),
        check_vma=False,
    )
```

profile of v0, /device:TPU:0, one launch (start us, length us, event | category | flops | bytes accessed | tf_op | source)
XLA Modules:
  0.0 155.6 jit_solution(13972722888859161238)
XLA Ops:
  6.5 77.3 %while.13 = (s32[]{:T(128)}, f32[2,8,64,128]{3,2,1,0:T(8,128)}, bf16[2,512,3,128]{3,1,2,0:T(8,128)(2,1)}, s32[8,3]{0,1:T(4,128)}, s32[]{:T(128)}, /*index=5*/s32[]{:T(128)}) while((s32[]{:T(128)}, f32[2,8,64,128]{3,2,1,0:T(8,128)}, bf16[2,512,3,128]{3,1,2,0:T(8,128)(2,1)}, s32[8,3]{0,1:T(4,128)}, s32[]{:T(128)}, /*index=5*/s32[]{:T(128)}) %tuple.147), condition=%wide.region_1.2_spmd, body=%wide.region_0.1_spmd.sunk | while | flops 427274240 | bytes 61539204 | solution.py:85
  6.5 1.0 constant_dynamic-slice_fusion.2
  9.8 2.0 %fusion.177 = (f32[512]{0:T(512)S(1)}, f32[512]{0:T(512)S(1)}) fusion(s32[]{:T(128)} %bitcast.241, s32[]{:T(128)} %bitcast.242, s32[]{:T(128)} %get-tuple-element.440, s32[]{:T(128)} %bitcast.243), kind=kLoop, calls=%fused_computation.193.clone.1 | loop fusion | flops 30208 | bytes 4112 | tf_op jit(solution)/shard_map/while/body/eval_jaxpr/sin | solution.py:32
  12.0 1.9 %fusion.178 = (f32[512]{0:T(512)S(1)}, f32[512]{0:T(512)S(1)}) fusion(s32[]{:T(128)} %bitcast.245, s32[]{:T(128)} %bitcast.246, s32[]{:T(128)} %get-tuple-element.440, s32[]{:T(128)} %bitcast.247), kind=kLoop, calls=%fused_computation.195.clone.1 | loop fusion | flops 30208 | bytes 4112 | tf_op jit(solution)/shard_map/while/body/eval_jaxpr/sin | solution.py:32
  14.3 1.1 copy.82
  15.5 1.0 fusion.180
  16.6 1.1 copy.83
  17.8 1.0 fusion.181
  18.7 1.9 %fusion.182 = (f32[512]{0:T(512)S(1)}, f32[512]{0:T(512)S(1)}) fusion(s32[]{:T(128)} %bitcast.250, s32[]{:T(128)} %bitcast.251, s32[]{:T(128)} %get-tuple-element.440, s32[]{:T(128)} %bitcast.252), kind=kLoop, calls=%fused_computation.189.clone.1 | loop fusion | flops 30208 | bytes 4112 | tf_op jit(solution)/shard_map/while/body/eval_jaxpr/sin | solution.py:32
  20.7 1.9 %fusion.183 = (f32[512]{0:T(512)S(1)}, f32[512]{0:T(512)S(1)}) fusion(s32[]{:T(128)} %bitcast.253, s32[]{:T(128)} %bitcast.254, s32[]{:T(128)} %get-tuple-element.440, s32[]{:T(128)} %bitcast.255), kind=kLoop, calls=%fused_computation.191.clone.1 | loop fusion | flops 30208 | bytes 4112 | tf_op jit(solution)/shard_map/while/body/eval_jaxpr/sin | solution.py:32
  23.1 1.1 copy.84
  24.2 1.0 fusion.185
  25.3 1.1 copy.85
  26.5 1.0 fusion.186
  27.5 1.9 %fusion.187 = (f32[512]{0:T(512)S(1)}, f32[512]{0:T(512)S(1)}) fusion(s32[]{:T(128)} %bitcast.258, s32[]{:T(128)} %bitcast.259, s32[]{:T(128)} %get-tuple-element.440, s32[]{:T(128)} %bitcast.260), kind=kLoop, calls=%fused_computation.185.clone.1 | loop fusion | flops 30208 | bytes 4112 | tf_op jit(solution)/shard_map/while/body/eval_jaxpr/sin | solution.py:32
  29.4 2.0 %fusion.188 = (f32[512]{0:T(512)S(1)}, f32[512]{0:T(512)S(1)}) fusion(s32[]{:T(128)} %bitcast.261, s32[]{:T(128)} %bitcast.262, s32[]{:T(128)} %get-tuple-element.440, s32[]{:T(128)} %bitcast.263), kind=kLoop, calls=%fused_computation.187.clone.1 | loop fusion | flops 30208 | bytes 4112 | tf_op jit(solution)/shard_map/while/body/eval_jaxpr/sin | solution.py:32
  31.8 1.1 copy.86
  32.9 1.0 fusion.190
  34.1 1.1 copy.87
  35.2 1.0 fusion.191
  36.2 1.9 %fusion.192 = (f32[512]{0:T(512)S(1)}, f32[512]{0:T(512)S(1)}) fusion(s32[]{:T(128)} %bitcast.266, s32[]{:T(128)} %bitcast.267, s32[]{:T(128)} %get-tuple-element.440, s32[]{:T(128)} %bitcast.268), kind=kLoop, calls=%fused_computation.181.clone.1 | loop fusion | flops 30208 | bytes 4112 | tf_op jit(solution)/shard_map/while/body/eval_jaxpr/sin | solution.py:32
  38.2 1.9 %fusion.193 = (f32[512]{0:T(512)S(1)}, f32[512]{0:T(512)S(1)}) fusion(s32[]{:T(128)} %bitcast.269, s32[]{:T(128)} %bitcast.270, s32[]{:T(128)} %get-tuple-element.440, s32[]{:T(128)} %bitcast.271), kind=kLoop, calls=%fused_computation.183.clone.1 | loop fusion | flops 30208 | bytes 4112 | tf_op jit(solution)/shard_map/while/body/eval_jaxpr/sin | solution.py:32
  40.5 1.1 copy.88
  41.7 1.0 fusion.195
  42.8 1.1 copy.89
  45.2 1.0 constant_dynamic-slice_fusion.2
  48.4 2.0 %fusion.177 = (f32[512]{0:T(512)S(1)}, f32[512]{0:T(512)S(1)}) fusion(s32[]{:T(128)} %bitcast.241, s32[]{:T(128)} %bitcast.242, s32[]{:T(128)} %get-tuple-element.440, s32[]{:T(128)} %bitcast.243), kind=kLoop, calls=%fused_computation.193.clone.1 | loop fusion | flops 30208 | bytes 4112 | tf_op jit(solution)/shard_map/while/body/eval_jaxpr/sin | solution.py:32
  50.6 1.9 %fusion.178 = (f32[512]{0:T(512)S(1)}, f32[512]{0:T(512)S(1)}) fusion(s32[]{:T(128)} %bitcast.245, s32[]{:T(128)} %bitcast.246, s32[]{:T(128)} %get-tuple-element.440, s32[]{:T(128)} %bitcast.247), kind=kLoop, calls=%fused_computation.195.clone.1 | loop fusion | flops 30208 | bytes 4112 | tf_op jit(solution)/shard_map/while/body/eval_jaxpr/sin | solution.py:32
  53.0 1.1 copy.82
  54.1 1.0 fusion.180
  55.3 1.1 copy.83
  56.4 1.0 fusion.181
  57.4 1.9 %fusion.182 = (f32[512]{0:T(512)S(1)}, f32[512]{0:T(512)S(1)}) fusion(s32[]{:T(128)} %bitcast.250, s32[]{:T(128)} %bitcast.251, s32[]{:T(128)} %get-tuple-element.440, s32[]{:T(128)} %bitcast.252), kind=kLoop, calls=%fused_computation.189.clone.1 | loop fusion | flops 30208 | bytes 4112 | tf_op jit(solution)/shard_map/while/body/eval_jaxpr/sin | solution.py:32
  59.3 1.9 %fusion.183 = (f32[512]{0:T(512)S(1)}, f32[512]{0:T(512)S(1)}) fusion(s32[]{:T(128)} %bitcast.253, s32[]{:T(128)} %bitcast.254, s32[]{:T(128)} %get-tuple-element.440, s32[]{:T(128)} %bitcast.255), kind=kLoop, calls=%fused_computation.191.clone.1 | loop fusion | flops 30208 | bytes 4112 | tf_op jit(solution)/shard_map/while/body/eval_jaxpr/sin | solution.py:32
  61.7 1.1 copy.84
  62.8 1.0 fusion.185
  64.0 1.1 copy.85
  65.1 1.0 fusion.186
  66.1 1.9 %fusion.187 = (f32[512]{0:T(512)S(1)}, f32[512]{0:T(512)S(1)}) fusion(s32[]{:T(128)} %bitcast.258, s32[]{:T(128)} %bitcast.259, s32[]{:T(128)} %get-tuple-element.440, s32[]{:T(128)} %bitcast.260), kind=kLoop, calls=%fused_computation.185.clone.1 | loop fusion | flops 30208 | bytes 4112 | tf_op jit(solution)/shard_map/while/body/eval_jaxpr/sin | solution.py:32
  68.0 2.0 %fusion.188 = (f32[512]{0:T(512)S(1)}, f32[512]{0:T(512)S(1)}) fusion(s32[]{:T(128)} %bitcast.261, s32[]{:T(128)} %bitcast.262, s32[]{:T(128)} %get-tuple-element.440, s32[]{:T(128)} %bitcast.263), kind=kLoop, calls=%fused_computation.187.clone.1 | loop fusion | flops 30208 | bytes 4112 | tf_op jit(solution)/shard_map/while/body/eval_jaxpr/sin | solution.py:32
  70.5 1.1 copy.86
  71.6 1.0 fusion.190
  72.7 1.1 copy.87
  73.9 1.0 fusion.191
  74.9 1.9 %fusion.192 = (f32[512]{0:T(512)S(1)}, f32[512]{0:T(512)S(1)}) fusion(s32[]{:T(128)} %bitcast.266, s32[]{:T(128)} %bitcast.267, s32[]{:T(128)} %get-tuple-element.440, s32[]{:T(128)} %bitcast.268), kind=kLoop, calls=%fused_computation.181.clone.1 | loop fusion | flops 30208 | bytes 4112 | tf_op jit(solution)/shard_map/while/body/eval_jaxpr/sin | solution.py:32
  76.8 1.9 %fusion.193 = (f32[512]{0:T(512)S(1)}, f32[512]{0:T(512)S(1)}) fusion(s32[]{:T(128)} %bitcast.269, s32[]{:T(128)} %bitcast.270, s32[]{:T(128)} %get-tuple-element.440, s32[]{:T(128)} %bitcast.271), kind=kLoop, calls=%fused_computation.183.clone.1 | loop fusion | flops 30208 | bytes 4112 | tf_op jit(solution)/shard_map/while/body/eval_jaxpr/sin | solution.py:32
  79.2 1.1 copy.88
  80.3 1.0 fusion.195
  81.5 1.1 copy.89
  83.9 4.4 %reshape.323 = bf16[4,64,16,2,64]{4,3,2,1,0:T(2,128)(2,1)S(1)} reshape(bf16[4,64,2048]{2,1,0:T(8,128)(2,1)} %param.11) | data formatting | bytes 2097152 | tf_op jit(solution)/shard_map/reshape | solution.py:53
  88.3 4.8 %slice_negate_fusion = (bf16[4,64,16,1,64]{4,3,2,1,0:T(2,128)(2,1)S(1)}, bf16[4,64,16,1,64]{4,3,2,1,0:T(2,128)(2,1)S(1)}) fusion(bf16[4,64,16,2,64]{4,3,2,1,0:T(2,128)(2,1)S(1)} %reshape.323), kind=kLoop, calls=%fused_computation.201 | loop fusion | flops 262144 | bytes 2097152 | tf_op jit(solution)/shard_map/neg | solution.py:54
  93.2 5.6 %pad_maximum_fusion.8 = bf16[4,64,16,2,64]{4,3,2,1,0:T(2,128)(2,1)S(1)} fusion(bf16[4,64,16,1,64]{4,3,2,1,0:T(2,128)(2,1)S(1)} %get-tuple-element.226, bf16[4,64,16,1,64]{4,3,2,1,0:T(2,128)(2,1)S(1)} %get-tuple-element.225), kind=kLoop, calls=%fused_computation.202 | loop fusion | flops 2097152 | bytes 2097152 | tf_op jit(solution)/shard_map/stack | solution.py:54
  98.8 2.5 %reshape.324 = bf16[4,64,2048]{2,1,0:T(8,128)(2,1)} reshape(bf16[4,64,16,2,64]{4,3,2,1,0:T(2,128)(2,1)S(1)} %pad_maximum_fusion.8) | data formatting | bytes 2097152 | tf_op jit(solution)/shard_map/reshape | solution.py:54
  102.6 5.8 %reduce-scatter.2.cloned.1.call-done = f32[2,8,16,128]{3,2,1,0:T(8,128)} async-done(((f32[2,8,64,128]{3,2,1,0:T(8,128)}), f32[2,8,16,128]{3,2,1,0:T(8,128)}) %reduce-scatter.2.cloned.1.call-update) | async-done | bytes 131088 | tf_op jit(solution)/shard_map/reduce_scatter | solution.py:90
  108.4 0.9 convert_element_type.279
  109.3 13.9 %all_gather.6 = bf16[8,8,16,128]{3,2,1,0:T(8,128)(2,1)S(1)} all-gather(bf16[2,8,16,128]{3,2,1,0:T(8,128)(2,1)S(1)} %convert_element_type.279), channel_id=1, replica_groups=mesh['cfg'=2,'tm'=4,'space'=2,'spin'=2] {'tm'}, dimensions={0}, use_global_device_ids=true | all-gather | bytes 327680 | tf_op jit(solution)/shard_map/all_gather | solution.py:97
  123.5 2.0 %convolution_convert_fusion.2 = bf16[4,128,2048]{2,1,0:T(8,128)(2,1)} fusion(bf16[4,64,2048]{2,1,0:T(8,128)(2,1)S(1)} %copy-done.4, bf16[4,64,2048]{2,1,0:T(8,128)(2,1)S(1)} %copy-done.3, bf16[1,4,128,128]{3,1,2,0:T(4,128)(2,1)S(1)} %fusion.88), kind=kOutput, calls=%fused_computation.200 | convolution fusion | flops 273678336 | bytes 4325376 | tf_op jit(solution)/shard_map/kmx,kxc->kmc/dot_general | solution.py:59
  125.5 2.9 %reshape.325 = bf16[4,8,256,128]{3,2,1,0:T(8,128)(2,1)S(1)} reshape(bf16[4,128,2048]{2,1,0:T(8,128)(2,1)} %convolution_convert_fusion.2) | data formatting | bytes 4194304 | tf_op jit(solution)/shard_map/reshape | solution.py:62
  128.7 7.0 %all_gather.7 = bf16[4,8,64,128]{3,2,1,0:T(8,128)(2,1)} all-gather(bf16[4,8,16,128]{3,2,1,0:T(8,128)(2,1)S(1)} %bitcast.290), channel_id=1, replica_groups=mesh['cfg'=2,'tm'=4,'space'=2,'spin'=2] {'space','spin'}, dimensions={2}, use_global_device_ids=true | all-gather | bytes 655360 | tf_op jit(solution)/shard_map/all_gather | solution.py:109
  135.7 2.4 %reshape.327 = bf16[4,8,64,2,64]{4,3,2,1,0:T(2,128)(2,1)S(1)} reshape(bf16[4,8,64,128]{3,2,1,0:T(8,128)(2,1)} %all_gather.7) | data formatting | bytes 1048576 | tf_op jit(solution)/shard_map/reshape | solution.py:63
  138.1 2.3 %slice_negate_fusion.1 = (bf16[4,8,64,1,64]{4,3,2,1,0:T(2,128)(2,1)S(1)}, bf16[4,8,64,1,64]{4,3,2,1,0:T(2,128)(2,1)S(1)}) fusion(bf16[4,8,64,2,64]{4,3,2,1,0:T(2,128)(2,1)S(1)} %reshape.327), kind=kLoop, calls=%fused_computation.209 | loop fusion | flops 131072 | bytes 1048576 | tf_op jit(solution)/shard_map/neg | solution.py:64
  140.5 3.6 %pad_maximum_fusion.9 = bf16[4,8,64,2,64]{4,3,2,1,0:T(2,128)(2,1)} fusion(bf16[4,8,64,1,64]{4,3,2,1,0:T(2,128)(2,1)S(1)} %get-tuple-element.228, bf16[4,8,64,1,64]{4,3,2,1,0:T(2,128)(2,1)S(1)} %get-tuple-element.227), kind=kLoop, calls=%fused_computation.210 | loop fusion | flops 1048576 | bytes 1048576 | tf_op jit(solution)/shard_map/stack | solution.py:64
  144.1 2.4 %stack_reshape.3 = bf16[4,8,1,64,128]{4,3,1,0,2:T(8,128)(2,1)S(1)} reshape(bf16[4,8,64,2,64]{4,3,2,1,0:T(2,128)(2,1)} %pad_maximum_fusion.9) | data formatting | bytes 1048576 | tf_op jit(solution)/shard_map/stack;reshape | solution.py:67
  146.7 2.0 %convolution_convert_fusion.3 = bf16[4,8,256,128]{3,2,1,0:T(8,128)(2,1)} fusion(bf16[4,8,256,128]{3,2,1,0:T(8,128)(2,1)S(1)} %reshape.325, bf16[4,8,128,128]{3,2,1,0:T(8,128)(2,1)S(1)} %bitcast.287), kind=kOutput, calls=%fused_computation.206 | convolution fusion | flops 269484032 | bytes 5242880 | tf_op jit(solution)/shard_map/kpmx,kpnx->kpmn/dot_general | solution.py:68
  (92 shorter events, 13.7 us)
Async XLA Ops:
  6.5 94.8 %copy-start = (s32[8]{0:T(128)S(1)}, s32[8]{0:T(128)}, u32[]{:S(2)}) copy-start(s32[8]{0:T(128)} %param.10) | copy-start | bytes 100
  6.5 101.9 %reduce-scatter.2.cloned.1.call-start = ((), (), s32[]{:S(2)}) async-start(), calls=%async_computation.1 | async-start | bytes 655360 | tf_op jit(solution)/shard_map/reduce_scatter | solution.py:90
  6.5 1.9 %copy-start.5 = (s32[8,3]{0,1:T(4,128)S(1)}, s32[8,3]{0,1:T(4,128)}, u32[]{:S(2)}) copy-start(s32[8,3]{0,1:T(4,128)} %get-tuple-element.439) | copy-start | bytes 292 | tf_op jit(solution)/shard_map/while
  42.7 1.3 copy-start.1
  42.7 1.6 %copy-start.6 = (f32[2,8,64,128]{3,2,1,0:T(8,128)S(1)}, f32[2,8,64,128]{3,2,1,0:T(8,128)}, u32[]{:S(2)}) copy-start(f32[2,8,64,128]{3,2,1,0:T(8,128)} %get-tuple-element.431) | copy-start | bytes 1572868 | tf_op jit(solution)/shard_map/while
  44.4 0.8 copy-start.7
  45.2 1.9 %copy-start.5 = (s32[8,3]{0,1:T(4,128)S(1)}, s32[8,3]{0,1:T(4,128)}, u32[]{:S(2)}) copy-start(s32[8,3]{0,1:T(4,128)} %get-tuple-element.439) | copy-start | bytes 292 | tf_op jit(solution)/shard_map/while
  81.3 1.3 copy-start.1
  81.4 1.6 %copy-start.6 = (f32[2,8,64,128]{3,2,1,0:T(8,128)S(1)}, f32[2,8,64,128]{3,2,1,0:T(8,128)}, u32[]{:S(2)}) copy-start(f32[2,8,64,128]{3,2,1,0:T(8,128)} %get-tuple-element.431) | copy-start | bytes 1572868 | tf_op jit(solution)/shard_map/while
  83.0 0.8 copy-start.7
  98.8 2.5 %copy-start.8 = (s32[4,2]{0,1:T(2,128)S(1)}, s32[4,2]{0,1:T(2,128)}, u32[]{:S(2)}) copy-start(s32[4,2]{0,1:T(2,128)} %param.9) | copy-start | bytes 100
  98.8 24.7 %copy-start.3 = (bf16[4,64,2048]{2,1,0:T(8,128)(2,1)S(1)}, bf16[4,64,2048]{2,1,0:T(8,128)(2,1)}, u32[]{:S(2)}) copy-start(bf16[4,64,2048]{2,1,0:T(8,128)(2,1)} %param.11) | copy-start | bytes 3145732
  101.3 22.2 %copy-start.4 = (bf16[4,64,2048]{2,1,0:T(8,128)(2,1)S(1)}, bf16[4,64,2048]{2,1,0:T(8,128)(2,1)}, u32[]{:S(2)}) copy-start(bf16[4,64,2048]{2,1,0:T(8,128)(2,1)} %reshape.324) | copy-start | bytes 3145732
  140.5 6.0 %copy-start.2 = (bf16[4,8,64,128]{3,2,1,0:T(8,128)(2,1)S(1)}, bf16[4,8,64,128]{3,2,1,0:T(8,128)(2,1)}, u32[]{:S(2)}) copy-start(bf16[4,8,64,128]{3,2,1,0:T(8,128)(2,1)} %all_gather.7) | copy-start | bytes 1572868
Sparse Core Ops, SparseCore 0:
  84.0 24.3 reduce-scatter.1
where the time goes:
time: 156 us
  other arithmetic  52.9 us (34%)
  local copies, waits for them, and re-layouts  42.6 us (27%)
  blocking collectives  20.8 us (13%)
  matrix products  19.3 us (12%)
  between operations  13.6 us (9%)
  waiting for transfers between devices  5.82 us (4%)
    sin x16, other arithmetic, elemental(): sines = jnp.sin(angles)[:, None, None]  31 us
    another operation x16, local copies, waits for them, and re-layouts, elemental(): jnp.stack([upper_rows, lower_rows], axis=2)  18 us
    dot_general x16, matrix products, elemental(): lax.dot_general(conj_left, phased, (((0,), (0,)), ((), ())), preferred_el...  14.7 us
    all_gather x1, blocking collectives, per_device(): lax.all_gather(part, 'tm', axis=0, tiled=True)  13.9 us
    all_gather x1, blocking collectives, per_device(): lax.all_gather(source_share, ('space', 'spin'), axis=2, tiled=True)  6.95 us
    reduce_scatter x1, waiting for transfers between devices, per_device(): lax.psum_scatter(partial_value, ('space', 'spin'), scatter_dimension=2, t...  5.81 us
    another operation x1, other arithmetic, contract(): jnp.stack([-parts[:, :, :, 1], parts[:, :, :, 0]], axis=3)  5.6 us
    neg x1, other arithmetic, contract(): -parts[:, :, :, 1]  4.85 us
  transfers between devices with their start and end apart: 1, of which 1 were waited for; matrix products, arithmetic and copies ran while one was open for 12% of the time, Pallas kernels for 0%

commit v1 on v0

v1 whole, which is shorter than its diff:
```python
import functools

import jax
import jax.numpy as jnp
from jax import lax
from jax.experimental import pallas as pl
from jax.experimental.pallas import tpu as pltpu
from jax.sharding import PartitionSpec as P

LAT = 32
TURN = 6.283185307179586
SPINS = 16
SHARE = ("space", "spin")
SMEM = pl.BlockSpec(memory_space=pltpu.SMEM)
VMEM = pl.BlockSpec(memory_space=pltpu.VMEM)


def swapped(value, first, second):
    half = value.shape[1] // 2
    lane = lax.broadcasted_iota(jnp.int32, value.shape, 1)
    sign = jnp.where(lane < half, first, second).astype(jnp.float32)
    return pltpu.roll(value.astype(jnp.float32), half, 1) * sign


def elementals_kernel(pos_ref, mom_ref, x_hbm, *rest, groups, chunk):
    outs = rest[:groups]
    x_ref, table_ref, phased_ref, part_ref, sems = rest[groups:]
    slots, colours, sites, width = x_ref.shape
    half = width // 2
    moms = mom_ref.shape[1]
    rows = half // groups
    copies = [pltpu.make_async_copy(x_hbm.at[s], x_ref.at[s], sems.at[s]) for s in range(slots)]
    for copy in copies:
        copy.start()
    pos = pos_ref[0]
    row = lax.broadcasted_iota(jnp.int32, (moms, sites), 0)
    site = lax.broadcasted_iota(jnp.int32, (moms, sites), 1) + pos * sites
    coords = (site % LAT, site // LAT % LAT, site // (LAT * LAT))
    wave = jnp.zeros((moms, sites), jnp.int32)
    for d in range(3):
        value = jnp.zeros((moms, sites), jnp.int32)
        for m in range(moms):
            value = jnp.where(row == m, mom_ref[d, m], value)
        wave = wave + value * coords[d]
    angle = (wave & (LAT - 1)).astype(jnp.float32) * (TURN / LAT)
    table_ref[...] = jnp.concatenate([jnp.cos(angle), jnp.sin(angle)], axis=0).T
    for copy in copies:
        copy.wait()

    def step(i, carry):
        at = pl.ds(pl.multiple_of(i * chunk, chunk), chunk)
        table = table_ref[at, :]
        blocks = [(s, c) for s in range(slots) for c in range(colours)]
        plain = [x_ref[s, c, at, :].astype(jnp.float32) for s, c in blocks]
        turned = [swapped(value, -1.0, 1.0) for value in plain]
        for m in range(moms):
            cosine = jnp.broadcast_to(table[:, m : m + 1], (chunk, width))
            sine = jnp.broadcast_to(table[:, moms + m : moms + m + 1], (chunk, width))
            for n, (s, c) in enumerate(blocks):
                phased_ref[s, c, at, m * width : (m + 1) * width] = (
                    cosine * plain[n] + sine * turned[n]
                ).astype(jnp.bfloat16)
        return carry

    lax.fori_loop(0, sites // chunk, step, 0)
    for s in range(slots):
        products = lax.dot_general(
            x_ref[s].reshape(colours * sites, width),
            phased_ref[s].reshape(colours * sites, moms * width),
            (((0,), (0,)), ((), ())),
            preferred_element_type=jnp.float32,
        )
        for m in range(moms):
            block = products[:, m * width : (m + 1) * width]
            value = block[:half] + swapped(block[half:], 1.0, -1.0)
            for r in range(groups):
                part_ref[r, s, m] = value[r * rows : (r + 1) * rows]
    for j in range(groups):
        outs[j][...] = part_ref[lax.rem(pos + j, groups)].astype(outs[j].dtype)


def elementals(pos, mom_t, x, groups, chunk=16):
    slots, colours, sites, width = x.shape
    moms = mom_t.shape[1]
    rows = width // 2 // groups
    shape = (slots, moms, rows, width)
    return pl.pallas_call(
        functools.partial(elementals_kernel, groups=groups, chunk=chunk),
        out_shape=[jax.ShapeDtypeStruct(shape, jnp.float32)]
        + [jax.ShapeDtypeStruct(shape, jnp.bfloat16)] * (groups - 1),
        in_specs=[SMEM, SMEM, pl.BlockSpec(memory_space=pl.ANY)],
        out_specs=[VMEM] * groups,
        scratch_shapes=[
            pltpu.VMEM((slots, colours, sites, width), jnp.bfloat16),
            pltpu.VMEM((sites, 2 * moms), jnp.float32),
            pltpu.VMEM((slots, colours, sites, moms * width), jnp.bfloat16),
            pltpu.VMEM((groups, slots, moms, rows, width), jnp.float32),
            pltpu.SemaphoreType.DMA((slots,)),
        ],
        compiler_params=pltpu.CompilerParams(vmem_limit_bytes=40 * 1024 * 1024),
        name="elementals",
    )(pos, mom_t, x)


def pick(place_ref, pairs_ref, map_ref, side, k, arrived, store):
    members = len(arrived)
    slots = arrived[0].shape[0]
    slot = map_ref[pairs_ref[side, k]]
    shift = lax.rem(place_ref[1] + members - slot // slots, members)
    for s in range(members):

        @pl.when(shift == s)
        def _():
            store(arrived[s][lax.rem(slot, slots)])


def choose_kernel(place_ref, pairs_ref, map_ref, *rest):
    arrived, out_ref = rest[:-1], rest[-1]
    for k in range(out_ref.shape[0]):

        def store(block):
            out_ref[k] = block

        pick(place_ref, pairs_ref, map_ref, 1, k, arrived, store)


def choose(place, pairs_t, slot_map, arrived):
    shape = (pairs_t.shape[1],) + arrived[0].shape[1:]
    return pl.pallas_call(
        choose_kernel,
        out_shape=jax.ShapeDtypeStruct(shape, arrived[0].dtype),
        in_specs=[SMEM] * 3 + [VMEM] * len(arrived),
        out_specs=VMEM,
        name="choose",
    )(place, pairs_t, slot_map, *arrived)


def halfway_kernel(place_ref, pairs_ref, map_ref, tau_ref, *rest, members):
    arrived = rest[:members]
    out_ref, sink_ref, right_ref, turn_ref = rest[members:]
    k = pl.program_id(0)
    moms, rows, width = sink_ref.shape
    vectors = tau_ref.shape[1]

    def store(block):
        sink_ref[...] = block

    pick(place_ref, pairs_ref, map_ref, 0, k, arrived, store)
    right_ref[:vectors] = tau_ref[0]
    for g in range(SPINS):
        at = slice(g * width, (g + 1) * width)
        right_ref[vectors:, at] = swapped(tau_ref[0, :, at], -1.0, 1.0).astype(jnp.bfloat16)
    product = jnp.dot(
        sink_ref[...].reshape(moms * rows, width),
        right_ref[...],
        preferred_element_type=jnp.float32,
    )
    for g in range(SPINS):
        turn_ref[pl.ds(g, moms * rows, stride=SPINS), :] = product[:, g * width : (g + 1) * width]
    out_ref[0] = turn_ref[...].astype(jnp.bfloat16)


def halfway(place, pairs_t, slot_map, perambulators, arrived):
    pairs, vectors, wide = perambulators.shape
    _, moms, rows, width = arrived[0].shape
    count = moms * rows * SPINS
    return pl.pallas_call(
        functools.partial(halfway_kernel, members=len(arrived)),
        grid=(pairs,),
        out_shape=jax.ShapeDtypeStruct((pairs, count, width), jnp.bfloat16),
        in_specs=[SMEM] * 3
        + [pl.BlockSpec((1, vectors, wide), lambda k: (k, 0, 0))]
        + [VMEM] * len(arrived),
        out_specs=pl.BlockSpec((1, count, width), lambda k: (k, 0, 0)),
        scratch_shapes=[
            pltpu.VMEM((moms, rows, width), jnp.bfloat16),
            pltpu.VMEM((2 * vectors, wide), jnp.bfloat16),
            pltpu.VMEM((count, width), jnp.float32),
        ],
        name="halfway",
    )(place, pairs_t, slot_map, perambulators, *arrived)


def loops_kernel(place_ref, half_ref, *rest, groups):
    sources = rest[:groups]
    out_ref, full_ref = rest[groups:]
    moms, _, rows, width = full_ref.shape
    for j in range(groups):
        full_ref[:, lax.rem(place_ref[0] + groups - j, groups)] = sources[j][0]
    count = rows * SPINS
    for m in range(moms):
        source = full_ref[m].reshape(groups * rows, width)
        right = jnp.concatenate([source, swapped(source, -1.0, 1.0).astype(jnp.bfloat16)], axis=0)
        product = lax.dot_general(
            half_ref[0, m * count : (m + 1) * count],
            right,
            (((1,), (1,)), ((), ())),
            preferred_element_type=jnp.float32,
        )
        out_ref[0, m] = product.astype(jnp.bfloat16).reshape(rows, SPINS, width)


def loops(place, half, sources):
    pairs, count, width = half.shape
    groups = len(sources)
    _, moms, rows, _ = sources[0].shape
    return pl.pallas_call(
        functools.partial(loops_kernel, groups=groups),
        grid=(pairs,),
        out_shape=jax.ShapeDtypeStruct((pairs, moms, rows, SPINS, width), jnp.bfloat16),
        in_specs=[SMEM, pl.BlockSpec((1, count, width), lambda k: (k, 0, 0))]
        + [pl.BlockSpec((1, moms, rows, width), lambda k: (k, 0, 0, 0))] * groups,
        out_specs=pl.BlockSpec((1, moms, rows, SPINS, width), lambda k: (k, 0, 0, 0, 0)),
        scratch_shapes=[pltpu.VMEM((moms, groups, rows, width), jnp.bfloat16)],
        name="loops",
    )(place, half, *sources)


def shifted(value, axes, by):
    size = lax.axis_size(axes)
    return lax.ppermute(value, axes, [(i, (i + by) % size) for i in range(size)])


def per_device(eigenvectors, momenta, time_pairs, slot_map, perambulators):
    groups = lax.axis_size(SHARE)
    members = lax.axis_size("tm")
    place = jnp.stack([lax.axis_index(SHARE), lax.axis_index("tm")]).astype(jnp.int32)
    pairs_t = time_pairs.T
    parts = elementals(place, momenta.T, jnp.transpose(eigenvectors, (0, 2, 1, 3)), groups)
    received = [shifted(parts[j], SHARE, j) for j in range(1, groups)]
    row_share = parts[0]
    for part in received:
        row_share = row_share + part.astype(jnp.float32)
    row_share = row_share.astype(jnp.bfloat16)
    arrived = [row_share] + [shifted(row_share, "tm", j) for j in range(1, members)]
    source_share = choose(place, pairs_t, slot_map, arrived)
    sources = [source_share] + [shifted(source_share, SHARE, j) for j in range(1, groups)]
    half = halfway(place, pairs_t, slot_map, perambulators, arrived)
    return loops(place, half, sources)


def solution(mesh):
    placed = (
        P(("cfg", "tm"), ("space", "spin"), None, None),
        P(),
        P(("cfg", "tm"), None),
        P(),
        P(("cfg", "tm"), None, None),
    )
    return jax.shard_map(
        per_device,
        mesh=mesh,
        in_specs=placed,
        out_specs=P(("cfg", "tm"), None, ("space", "spin"), None, None),
        check_vma=False,
    )
```

time: 156 us -> 44 us (0.28)
  other arithmetic: 52.9 us -> 0.11 us
  local copies, waits for them, and re-layouts: 42.6 us -> 3.72 us
  blocking collectives: 20.8 us -> 0 us
  matrix products: 19.3 us -> 0 us
  Pallas kernels: 0 us -> 18.3 us
  between operations: 13.6 us -> 0.06 us
  starting transfers between devices: 0.01 us -> 10.9 us
  waiting for transfers between devices: 5.82 us -> 10.5 us
    sin x16 -> x0, other arithmetic: 31 us -> none  [elemental(): sines = jnp.sin(angles)[:, None, None]]
    all_gather x2 -> x0, blocking collectives: 20.8 us -> none  [the longest x1 13.9 us: per_device(): lax.all_gather(part, 'tm', axis=0, tiled=True)]
    another operation x18 -> x0, local copies, waits for them, and re-layouts: 20.5 us -> none  [the longest x16 18 us: elemental(): jnp.stack([upper_rows, lower_rows], axis=2)]
    dot_general x20 -> x0, matrix products: 19.3 us -> none  [the longest x16 14.7 us: elemental(): lax.dot_general(conj_left, phased, (((0,), (0,)), ((), ())), preferred_el...]
    pallas_call x0 -> x4, Pallas kernels: none -> 18.3 us  [the longest x1 7.02 us: elementals(): pl.pallas_call(functools.partial(elementals_kernel, groups=groups, chunk=...]
    another operation x43 -> x1, other arithmetic: 13.7 us -> 0.07 us  [per_device(): jnp.stack([lax.axis_index(SHARE), lax.axis_index('tm')]).astype(jnp.int32)]
    reshape x6 -> x0, local copies, waits for them, and re-layouts: 13.2 us -> none  [the longest x1 4.43 us: contract(): parts = perambulators.reshape(pair_count, vectors, 16, 2, vectors)]
    ppermute x0 -> x9, starting transfers between devices: none -> 10.9 us  [shifted(): lax.ppermute(value, axes, [(i, (i + by) % size) for i in range(size)])]
  transfers between devices with their start and end apart: 1 -> 9, of which waited for: 1 -> 5; matrix products, arithmetic and copies ran while one was open for 12% -> 0% of each run, Pallas kernels for 0% -> 11%
where the time goes in v1:
time: 44 us; the launch traced here: 43.6 us
  Pallas kernels  18.3 us (42%)
  starting transfers between devices  10.9 us (25%)
  waiting for transfers between devices  10.5 us (24%)
  local copies, waits for them, and re-layouts  3.72 us (8%)
    ppermute x9, starting transfers between devices, shifted(): lax.ppermute(value, axes, [(i, (i + by) % size) for i in range(size)])  10.9 us
    ppermute x9, waiting for transfers between devices, shifted(): lax.ppermute(value, axes, [(i, (i + by) % size) for i in range(size)])  10.5 us
    pallas_call x1, Pallas kernels, elementals(): pl.pallas_call(functools.partial(elementals_kernel, groups=groups, chunk=...  7.02 us
    pallas_call x1, Pallas kernels, halfway(): pl.pallas_call(functools.partial(halfway_kernel, members=len(arrived)), g...  4.96 us
    pallas_call x1, Pallas kernels, loops(): pl.pallas_call(functools.partial(loops_kernel, groups=groups), grid=(pair...  4.59 us
    unnamed x20, local copies, waits for them, and re-layouts  3.72 us
    pallas_call x1, Pallas kernels, choose(): pl.pallas_call(choose_kernel, out_shape=jax.ShapeDtypeStruct(shape, arriv...  1.73 us
  transfers between devices with their start and end apart: 9, of which 5 were waited for; matrix products, arithmetic and copies ran while one was open for 0% of the time, Pallas kernels for 11%

profile of v1, /device:TPU:0, one launch (start us, length us, event | category | flops | bytes accessed | tf_op | source)
XLA Modules:
  0.0 43.6 jit_solution(8156083707248046971)
XLA Ops:
  0.0 0.1 pad_add_fusion.pos_ref.place_ref
  0.1 0.0 copy-start.1
  0.1 0.0 copy-start
  0.1 1.1 %copy-done = bf16[2,512,3,128]{3,1,2,0:T(8,128)(2,1)S(1)} copy-done((bf16[2,512,3,128]{3,1,2,0:T(8,128)(2,1)S(1)}, bf16[2,512,3,128]{3,1,2,0:T(8,128)(2,1)}, u32[]{:S(2)}) %copy-start) | copy-done | bytes 786456
  1.2 0.0 copy-start.2
  1.2 0.7 %copy-done.2 = s32[8,3]{0,1:T(4,128)S(1)} copy-done((s32[8,3]{0,1:T(4,128)S(1)}, s32[8,3]{0,1:T(4,128)}, u32[]{:S(2)}) %copy-start.2) | copy-done | bytes 120
  1.9 7.0 %elementals.1 = (f32[2,8,16,128]{3,2,1,0:T(8,128)S(1)}, bf16[2,8,16,128]{3,2,1,0:T(8,128)(2,1)S(1)}, bf16[2,8,16,128]{3,2,1,0:T(8,128)(2,1)S(1)}, bf16[2,8,16,128]{3,2,1,0:T(8,128)(2,1)S(1)}) custom-call(s32[2]{0:T(128)S(1)} %pad_add_fusion.pos_ref.place_ref, s32[3,8]{1,0:T(4,128)S(1)} %bitcast.6, bf16[2,3,512,128]{3,2,1,0:T(8,128)(2,1)S(1)} %bitcast.5), custom_call_target="tpu_custom_call" | custom-call | tf_op jit(solution)/shard_map/elementals/pallas_call | solution.py:87
  8.9 0.5 %collective-permute-start = (bf16[2,8,16,128]{3,2,1,0:T(8,128)(2,1)S(1)}, bf16[2,8,16,128]{3,2,1,0:T(8,128)(2,1)S(1)}, u32[]{:S(2)}, u32[]{:S(2)}) collective-permute-start(bf16[2,8,16,128]{3,2,1,0:T(8,128)(2,1)S(1)} %get-tuple-element.10), channel_id=1, source_target_pairs={{0,1},{1,2},{2,3},{3,0},{4,5},{5,6},{6,7},{7,4},{8,9},{9,10},{10,1... | collective-permute-start | bytes 196616 | tf_op jit(solution)/shard_map/ppermute | solution.py:221
  9.5 2.5 %collective-permute-start.1 = (bf16[2,8,16,128]{3,2,1,0:T(8,128)(2,1)S(1)}, bf16[2,8,16,128]{3,2,1,0:T(8,128)(2,1)S(1)}, u32[]{:S(2)}, u32[]{:S(2)}) collective-permute-start(bf16[2,8,16,128]{3,2,1,0:T(8,128)(2,1)S(1)} %get-tuple-element.11), channel_id=1, source_target_pairs={{0,2},{1,3},{2,0},{3,1},{4,6},{5,7},{6,4},{7,5},{8,10},{9,11},{10,... | collective-permute-start | bytes 196616 | tf_op jit(solution)/shard_map/ppermute | solution.py:221
  12.0 1.4 %collective-permute-start.2 = (bf16[2,8,16,128]{3,2,1,0:T(8,128)(2,1)S(1)}, bf16[2,8,16,128]{3,2,1,0:T(8,128)(2,1)S(1)}, u32[]{:S(2)}, u32[]{:S(2)}) collective-permute-start(bf16[2,8,16,128]{3,2,1,0:T(8,128)(2,1)S(1)} %get-tuple-element.12), channel_id=1, source_target_pairs={{0,3},{1,0},{2,1},{3,2},{4,7},{5,4},{6,5},{7,6},{8,11},{9,8},{10,9... | collective-permute-start | bytes 196616 | tf_op jit(solution)/shard_map/ppermute | solution.py:221
  13.4 0.0 collective-permute-done
  13.4 1.1 %collective-permute-done.1 = bf16[2,8,16,128]{3,2,1,0:T(8,128)(2,1)S(1)} collective-permute-done((bf16[2,8,16,128]{3,2,1,0:T(8,128)(2,1)S(1)}, bf16[2,8,16,128]{3,2,1,0:T(8,128)(2,1)S(1)}, u32[]{:S(2)}, u32[]{:S(2)}) %collective-permute-start.1) | collective-permute-done | bytes 65568 | tf_op jit(solution)/shard_map/ppermute | solution.py:221
  14.5 0.8 %collective-permute-done.2 = bf16[2,8,16,128]{3,2,1,0:T(8,128)(2,1)S(1)} collective-permute-done((bf16[2,8,16,128]{3,2,1,0:T(8,128)(2,1)S(1)}, bf16[2,8,16,128]{3,2,1,0:T(8,128)(2,1)S(1)}, u32[]{:S(2)}, u32[]{:S(2)}) %collective-permute-start.2) | collective-permute-done | bytes 65568 | tf_op jit(solution)/shard_map/ppermute | solution.py:221
  15.3 0.0 copy-start.3
  15.4 3.7 %collective-permute-start.5 = (bf16[2,8,16,128]{3,2,1,0:T(8,128)(2,1)S(1)}, bf16[2,8,16,128]{3,2,1,0:T(8,128)(2,1)S(1)}, u32[]{:S(2)}, u32[]{:S(2)}) collective-permute-start(bf16[2,8,16,128]{3,2,1,0:T(8,128)(2,1)S(1)} %add_convert_fusion.rest_0_), channel_id=1, source_target_pairs={{0,12},{4,0},{8,4},{12,8},{1,13},{5,1},{9,5},{13,9},{2,14},{6,2},{... | collective-permute-start | bytes 196616 | tf_op jit(solution)/shard_map/ppermute | solution.py:221
  19.0 0.0 collective-permute-start.4
  19.0 1.0 %collective-permute-start.3 = (bf16[2,8,16,128]{3,2,1,0:T(8,128)(2,1)S(1)}, bf16[2,8,16,128]{3,2,1,0:T(8,128)(2,1)S(1)}, u32[]{:S(2)}, u32[]{:S(2)}) collective-permute-start(bf16[2,8,16,128]{3,2,1,0:T(8,128)(2,1)S(1)} %add_convert_fusion.rest_0_), channel_id=1, source_target_pairs={{0,4},{4,8},{8,12},{12,0},{1,5},{5,9},{9,13},{13,1},{2,6},{6,10},{... | collective-permute-start | bytes 196616 | tf_op jit(solution)/shard_map/ppermute | solution.py:221
  20.0 1.5 %collective-permute-done.5.rest_3_ = bf16[2,8,16,128]{3,2,1,0:T(8,128)(2,1)S(1)} collective-permute-done((bf16[2,8,16,128]{3,2,1,0:T(8,128)(2,1)S(1)}, bf16[2,8,16,128]{3,2,1,0:T(8,128)(2,1)S(1)}, u32[]{:S(2)}, u32[]{:S(2)}) %collective-permute-start.5) | collective-permute-done | bytes 65568 | tf_op jit(solution)/shard_map/ppermute | solution.py:221
  21.6 0.0 copy-start.4
  21.6 4.9 %collective-permute-done.4.rest_2_ = bf16[2,8,16,128]{3,2,1,0:T(8,128)(2,1)S(1)} collective-permute-done((bf16[2,8,16,128]{3,2,1,0:T(8,128)(2,1)S(1)}, bf16[2,8,16,128]{3,2,1,0:T(8,128)(2,1)S(1)}, u32[]{:S(2)}, u32[]{:S(2)}) %collective-permute-start.4) | collective-permute-done | bytes 65568 | tf_op jit(solution)/shard_map/ppermute | solution.py:221
  26.4 0.0 copy-start.5
  26.4 0.0 collective-permute-done.3.rest_1_
  26.4 0.0 copy-start.6
  26.4 0.0 copy-done.1
  26.4 0.0 copy-done.3
  26.4 0.0 copy-done.4
  26.4 0.6 %copy-done.5 = bf16[2,8,16,128]{3,2,1,0:T(8,128)(2,1)} copy-done((bf16[2,8,16,128]{3,2,1,0:T(8,128)(2,1)}, bf16[2,8,16,128]{3,2,1,0:T(8,128)(2,1)S(1)}, u32[]{:S(2)}) %copy-start.5) | copy-done | bytes 65560
  27.0 0.0 copy-done.6
  27.1 1.7 %choose.1.rest_0_ = bf16[4,8,16,128]{3,2,1,0:T(8,128)(2,1)} custom-call(s32[2]{0:T(128)} %copy-done.1, s32[2,4]{1,0:T(2,128)} %bitcast.7, s32[8]{0:T(128)} %map_ref.3, bf16[2,8,16,128]{3,2,1,0:T(8,128)(2,1)} %copy-done.3, bf16[2,8,16,128]{3,2,1,0:T(8,128)(2,1)} %copy-done.6, bf16[2,8,16,128]{3,2,1,0:T(8,128)(2,1)} %copy-done.5, bf16[2,8,16,128]{3,2,1,0:T(8,128)(2,1)} %copy-done.4), custom_call_target="tpu_custom_call" | custom-call | tf_op jit(solution)/shard_map/choose/pallas_call | solution.py:129
  28.8 1.1 %collective-permute-start.8 = (bf16[4,8,16,128]{3,2,1,0:T(8,128)(2,1)}, bf16[4,8,16,128]{3,2,1,0:T(8,128)(2,1)S(1)}, u32[]{:S(2)}, u32[]{:S(2)}) collective-permute-start(bf16[4,8,16,128]{3,2,1,0:T(8,128)(2,1)} %choose.1.rest_0_), channel_id=1, source_target_pairs={{0,3},{1,0},{2,1},{3,2},{4,7},{5,4},{6,5},{7,6},{8,11},{9,8},{10,9... | collective-permute-start | bytes 393224 | tf_op jit(solution)/shard_map/ppermute | solution.py:221
  29.9 0.6 %collective-permute-start.7 = (bf16[4,8,16,128]{3,2,1,0:T(8,128)(2,1)}, bf16[4,8,16,128]{3,2,1,0:T(8,128)(2,1)S(1)}, u32[]{:S(2)}, u32[]{:S(2)}) collective-permute-start(bf16[4,8,16,128]{3,2,1,0:T(8,128)(2,1)} %choose.1.rest_0_), channel_id=1, source_target_pairs={{0,2},{1,3},{2,0},{3,1},{4,6},{5,7},{6,4},{7,5},{8,10},{9,11},{10,... | collective-permute-start | bytes 393224 | tf_op jit(solution)/shard_map/ppermute | solution.py:221
  30.5 0.0 collective-permute-start.6
  30.5 5.0 %halfway.1.half_ref = bf16[4,2048,128]{2,1,0:T(8,128)(2,1)} custom-call(s32[2]{0:T(128)} %copy-done.1, s32[2,4]{1,0:T(2,128)} %bitcast.8, s32[8]{0:T(128)} %map_ref.3, bf16[4,64,2048]{2,1,0:T(8,128)(2,1)} %tau_ref.1, bf16[2,8,16,128]{3,2,1,0:T(8,128)(2,1)} %copy-done.3, bf16[2,8,16,128]{3,2,1,0:T(8,128)(2,1)} %copy-done.6, ...), custom_call_target="tpu_custom_call" | custom-call | tf_op jit(solution)/shard_map/halfway/pallas_call | solution.py:167
  35.5 0.0 collective-permute-done.8.rest_3_
  35.5 0.0 copy-start.7
  35.5 2.2 %collective-permute-done.7.rest_2_ = bf16[4,8,16,128]{3,2,1,0:T(8,128)(2,1)S(1)} collective-permute-done((bf16[4,8,16,128]{3,2,1,0:T(8,128)(2,1)}, bf16[4,8,16,128]{3,2,1,0:T(8,128)(2,1)S(1)}, u32[]{:S(2)}, u32[]{:S(2)}) %collective-permute-start.7) | collective-permute-done | bytes 131104 | tf_op jit(solution)/shard_map/ppermute | solution.py:221
  37.7 0.0 copy-start.8
  37.7 0.0 collective-permute-done.6.rest_1_
  37.7 0.0 copy-done.7
  37.7 0.6 %copy-done.8 = bf16[4,8,16,128]{3,2,1,0:T(8,128)(2,1)} copy-done((bf16[4,8,16,128]{3,2,1,0:T(8,128)(2,1)}, bf16[4,8,16,128]{3,2,1,0:T(8,128)(2,1)S(1)}, u32[]{:S(2)}) %copy-start.8) | copy-done | bytes 131096
  38.4 0.0 copy-start.9
  38.4 0.6 %copy-done.9 = bf16[4,8,16,128]{3,2,1,0:T(8,128)(2,1)} copy-done((bf16[4,8,16,128]{3,2,1,0:T(8,128)(2,1)}, bf16[4,8,16,128]{3,2,1,0:T(8,128)(2,1)S(1)}, u32[]{:S(2)}) %copy-start.9) | copy-done | bytes 131096
  39.0 4.6 %loops.1 = bf16[4,8,16,16,128]{4,3,2,1,0:T(8,128)(2,1)} custom-call(s32[2]{0:T(128)} %copy-done.1, bf16[4,2048,128]{2,1,0:T(8,128)(2,1)} %halfway.1.half_ref, bf16[4,8,16,128]{3,2,1,0:T(8,128)(2,1)} %choose.1.rest_0_, bf16[4,8,16,128]{3,2,1,0:T(8,128)(2,1)} %copy-done.9, bf16[4,8,16,128]{3,2,1,0:T(8,128)(2,1)} %copy-done.8, bf16[4,8,16,128]{3,2,1,0:T(8,128)(2,1)} %copy-done.7), custom_call_target="tpu_custom_call" | custom-call | tf_op jit(solution)/shard_map/loops/pallas_call | solution.py:207
  (1 shorter events, 0.0 us)
Async XLA Ops:
  0.1 26.3 %copy-start.1 = (s32[2]{0:T(128)}, s32[2]{0:T(128)S(1)}, u32[]{:S(2)}) copy-start(s32[2]{0:T(128)S(1)} %pad_add_fusion.pos_ref.place_ref) | copy-start | bytes 28
  0.1 1.1 %copy-start = (bf16[2,512,3,128]{3,1,2,0:T(8,128)(2,1)S(1)}, bf16[2,512,3,128]{3,1,2,0:T(8,128)(2,1)}, u32[]{:S(2)}) copy-start(bf16[2,512,3,128]{3,1,2,0:T(8,128)(2,1)} %param.5) | copy-start | bytes 2359300
  1.2 0.7 %copy-start.2 = (s32[8,3]{0,1:T(4,128)S(1)}, s32[8,3]{0,1:T(4,128)}, u32[]{:S(2)}) copy-start(s32[8,3]{0,1:T(4,128)} %param.6) | copy-start | bytes 292
  8.9 4.5 %collective-permute-start = (bf16[2,8,16,128]{3,2,1,0:T(8,128)(2,1)S(1)}, bf16[2,8,16,128]{3,2,1,0:T(8,128)(2,1)S(1)}, u32[]{:S(2)}, u32[]{:S(2)}) collective-permute-start(bf16[2,8,16,128]{3,2,1,0:T(8,128)(2,1)S(1)} %get-tuple-element.10), channel_id=1, source_target_pairs={{0,1},{1,2},{2,3},{3,0},{4,5},{5,6},{6,7},{7,4},{8,9},{9,10},{10,1... | collective-permute-start | bytes 196616 | tf_op jit(solution)/shard_map/ppermute | solution.py:221
  9.5 5.0 %collective-permute-start.1 = (bf16[2,8,16,128]{3,2,1,0:T(8,128)(2,1)S(1)}, bf16[2,8,16,128]{3,2,1,0:T(8,128)(2,1)S(1)}, u32[]{:S(2)}, u32[]{:S(2)}) collective-permute-start(bf16[2,8,16,128]{3,2,1,0:T(8,128)(2,1)S(1)} %get-tuple-element.11), channel_id=1, source_target_pairs={{0,2},{1,3},{2,0},{3,1},{4,6},{5,7},{6,4},{7,5},{8,10},{9,11},{10,... | collective-permute-start | bytes 196616 | tf_op jit(solution)/shard_map/ppermute | solution.py:221
  12.0 3.3 %collective-permute-start.2 = (bf16[2,8,16,128]{3,2,1,0:T(8,128)(2,1)S(1)}, bf16[2,8,16,128]{3,2,1,0:T(8,128)(2,1)S(1)}, u32[]{:S(2)}, u32[]{:S(2)}) collective-permute-start(bf16[2,8,16,128]{3,2,1,0:T(8,128)(2,1)S(1)} %get-tuple-element.12), channel_id=1, source_target_pairs={{0,3},{1,0},{2,1},{3,2},{4,7},{5,4},{6,5},{7,6},{8,11},{9,8},{10,9... | collective-permute-start | bytes 196616 | tf_op jit(solution)/shard_map/ppermute | solution.py:221
  15.3 11.1 %copy-start.3 = (bf16[2,8,16,128]{3,2,1,0:T(8,128)(2,1)}, bf16[2,8,16,128]{3,2,1,0:T(8,128)(2,1)S(1)}, u32[]{:S(2)}) copy-start(bf16[2,8,16,128]{3,2,1,0:T(8,128)(2,1)S(1)} %add_convert_fusion.rest_0_) | copy-start | bytes 196612
  15.4 6.2 %collective-permute-start.5 = (bf16[2,8,16,128]{3,2,1,0:T(8,128)(2,1)S(1)}, bf16[2,8,16,128]{3,2,1,0:T(8,128)(2,1)S(1)}, u32[]{:S(2)}, u32[]{:S(2)}) collective-permute-start(bf16[2,8,16,128]{3,2,1,0:T(8,128)(2,1)S(1)} %add_convert_fusion.rest_0_), channel_id=1, source_target_pairs={{0,12},{4,0},{8,4},{12,8},{1,13},{5,1},{9,5},{13,9},{2,14},{6,2},{... | collective-permute-start | bytes 196616 | tf_op jit(solution)/shard_map/ppermute | solution.py:221
  19.0 7.4 %collective-permute-start.4 = (bf16[2,8,16,128]{3,2,1,0:T(8,128)(2,1)S(1)}, bf16[2,8,16,128]{3,2,1,0:T(8,128)(2,1)S(1)}, u32[]{:S(2)}, u32[]{:S(2)}) collective-permute-start(bf16[2,8,16,128]{3,2,1,0:T(8,128)(2,1)S(1)} %add_convert_fusion.rest_0_), channel_id=1, source_target_pairs={{0,8},{4,12},{8,0},{12,4},{1,9},{5,13},{9,1},{13,5},{2,10},{6,14},... | collective-permute-start | bytes 196616 | tf_op jit(solution)/shard_map/ppermute | solution.py:221
  19.0 7.4 %collective-permute-start.3 = (bf16[2,8,16,128]{3,2,1,0:T(8,128)(2,1)S(1)}, bf16[2,8,16,128]{3,2,1,0:T(8,128)(2,1)S(1)}, u32[]{:S(2)}, u32[]{:S(2)}) collective-permute-start(bf16[2,8,16,128]{3,2,1,0:T(8,128)(2,1)S(1)} %add_convert_fusion.rest_0_), channel_id=1, source_target_pairs={{0,4},{4,8},{8,12},{12,0},{1,5},{5,9},{9,13},{13,1},{2,6},{6,10},{... | collective-permute-start | bytes 196616 | tf_op jit(solution)/shard_map/ppermute | solution.py:221
  21.6 4.9 %copy-start.4 = (bf16[2,8,16,128]{3,2,1,0:T(8,128)(2,1)}, bf16[2,8,16,128]{3,2,1,0:T(8,128)(2,1)S(1)}, u32[]{:S(2)}) copy-start(bf16[2,8,16,128]{3,2,1,0:T(8,128)(2,1)S(1)} %collective-permute-done.5.rest_3_) | copy-start | bytes 196612
  26.4 0.6 %copy-start.5 = (bf16[2,8,16,128]{3,2,1,0:T(8,128)(2,1)}, bf16[2,8,16,128]{3,2,1,0:T(8,128)(2,1)S(1)}, u32[]{:S(2)}) copy-start(bf16[2,8,16,128]{3,2,1,0:T(8,128)(2,1)S(1)} %collective-permute-done.4.rest_2_) | copy-start | bytes 196612
  26.4 0.6 %copy-start.6 = (bf16[2,8,16,128]{3,2,1,0:T(8,128)(2,1)}, bf16[2,8,16,128]{3,2,1,0:T(8,128)(2,1)S(1)}, u32[]{:S(2)}) copy-start(bf16[2,8,16,128]{3,2,1,0:T(8,128)(2,1)S(1)} %collective-permute-done.3.rest_1_) | copy-start | bytes 196612
  28.8 6.7 %collective-permute-start.8 = (bf16[4,8,16,128]{3,2,1,0:T(8,128)(2,1)}, bf16[4,8,16,128]{3,2,1,0:T(8,128)(2,1)S(1)}, u32[]{:S(2)}, u32[]{:S(2)}) collective-permute-start(bf16[4,8,16,128]{3,2,1,0:T(8,128)(2,1)} %choose.1.rest_0_), channel_id=1, source_target_pairs={{0,3},{1,0},{2,1},{3,2},{4,7},{5,4},{6,5},{7,6},{8,11},{9,8},{10,9... | collective-permute-start | bytes 393224 | tf_op jit(solution)/shard_map/ppermute | solution.py:221
  29.9 7.8 %collective-permute-start.7 = (bf16[4,8,16,128]{3,2,1,0:T(8,128)(2,1)}, bf16[4,8,16,128]{3,2,1,0:T(8,128)(2,1)S(1)}, u32[]{:S(2)}, u32[]{:S(2)}) collective-permute-start(bf16[4,8,16,128]{3,2,1,0:T(8,128)(2,1)} %choose.1.rest_0_), channel_id=1, source_target_pairs={{0,2},{1,3},{2,0},{3,1},{4,6},{5,7},{6,4},{7,5},{8,10},{9,11},{10,... | collective-permute-start | bytes 393224 | tf_op jit(solution)/shard_map/ppermute | solution.py:221
  30.5 7.2 %collective-permute-start.6 = (bf16[4,8,16,128]{3,2,1,0:T(8,128)(2,1)}, bf16[4,8,16,128]{3,2,1,0:T(8,128)(2,1)S(1)}, u32[]{:S(2)}, u32[]{:S(2)}) collective-permute-start(bf16[4,8,16,128]{3,2,1,0:T(8,128)(2,1)} %choose.1.rest_0_), channel_id=1, source_target_pairs={{0,1},{1,2},{2,3},{3,0},{4,5},{5,6},{6,7},{7,4},{8,9},{9,10},{10,1... | collective-permute-start | bytes 393224 | tf_op jit(solution)/shard_map/ppermute | solution.py:221
  35.5 2.3 %copy-start.7 = (bf16[4,8,16,128]{3,2,1,0:T(8,128)(2,1)}, bf16[4,8,16,128]{3,2,1,0:T(8,128)(2,1)S(1)}, u32[]{:S(2)}) copy-start(bf16[4,8,16,128]{3,2,1,0:T(8,128)(2,1)S(1)} %collective-permute-done.8.rest_3_) | copy-start | bytes 393220
  37.7 0.6 %copy-start.8 = (bf16[4,8,16,128]{3,2,1,0:T(8,128)(2,1)}, bf16[4,8,16,128]{3,2,1,0:T(8,128)(2,1)S(1)}, u32[]{:S(2)}) copy-start(bf16[4,8,16,128]{3,2,1,0:T(8,128)(2,1)S(1)} %collective-permute-done.7.rest_2_) | copy-start | bytes 393220
  38.4 0.6 %copy-start.9 = (bf16[4,8,16,128]{3,2,1,0:T(8,128)(2,1)}, bf16[4,8,16,128]{3,2,1,0:T(8,128)(2,1)S(1)}, u32[]{:S(2)}) copy-start(bf16[4,8,16,128]{3,2,1,0:T(8,128)(2,1)S(1)} %collective-permute-done.6.rest_1_) | copy-start | bytes 393220

commit v2 on v0

v2 whole, which is shorter than its diff:
```python
import jax
import jax.numpy as jnp
from jax import lax
from jax.experimental import pallas as pl
from jax.experimental.pallas import tpu as pltpu
from jax.sharding import PartitionSpec as P


LAT = 32
TURN = 6.283185307179586
SPINS = 16
SMEM = pl.BlockSpec(memory_space=pltpu.SMEM)
VMEM = pl.BlockSpec(memory_space=pltpu.VMEM)
HBM = pl.BlockSpec(memory_space=pltpu.HBM)
ANY = pl.BlockSpec(memory_space=pl.ANY)


def params(mib):
    return pltpu.CompilerParams(vmem_limit_bytes=mib * 1024 * 1024)


def in_hbm(value):
    return pltpu.with_memory_space_constraint(value, pltpu.HBM)


def swapped(value, first, second):
    half = value.shape[1] // 2
    lane = lax.broadcasted_iota(jnp.int32, value.shape, 1)
    sign = jnp.where(lane < half, first, second).astype(jnp.float32)
    return pltpu.roll(value.astype(jnp.float32), half, 1) * sign


def elementals_kernel(place_hbm, mom_hbm, x_hbm, keep_ref, give_ref, *scratch):
    x_ref, place_ref, mom_ref, table_ref, plain_ref, phased_ref, part_ref, small_sems, sems = scratch
    slots, colours, sites, width = x_ref.shape
    half = width // 2
    moms = mom_ref.shape[1]
    spaces, _, _, rows, _ = keep_ref.shape
    spins = half // (rows * spaces)
    mom_copy = pltpu.make_async_copy(mom_hbm, mom_ref, small_sems.at[0])
    mom_copy.start()
    place_copy = pltpu.make_async_copy(place_hbm, place_ref, small_sems.at[1])
    place_copy.start()
    copies = [pltpu.make_async_copy(x_hbm.at[s], x_ref.at[s], sems.at[s]) for s in range(slots)]
    for copy in copies:
        copy.start()
    row = lax.broadcasted_iota(jnp.int32, (moms, sites), 0)
    site = lax.broadcasted_iota(jnp.int32, (moms, sites), 1)
    place_copy.wait()
    space = place_ref[0]
    spin = place_ref[1]
    site = site + (space * spins + spin) * sites
    coords = (site % LAT, site // LAT % LAT, site // (LAT * LAT))
    mom_copy.wait()
    wave = jnp.zeros((moms, sites), jnp.int32)
    for d in range(3):
        value = jnp.zeros((moms, sites), jnp.int32)
        for m in range(moms):
            value = jnp.where(row == m, mom_ref[d, m], value)
        wave = wave + value * coords[d]
    angle = (wave & (LAT - 1)).astype(jnp.float32) * (TURN / LAT)
    table_ref[0] = jnp.cos(angle)
    table_ref[1] = jnp.sin(angle)
    tiles = sites // width
    pieces = [(c, t) for c in range(colours) for t in range(tiles)]
    for s in range(slots):
        copies[s].wait()
        lefts = []
        for c, t in pieces:
            left = x_ref[s, c, t * width : (t + 1) * width].T
            lefts.append(left)
            plain_ref[s, c, t] = left.astype(jnp.float32)
        left = jnp.concatenate(lefts, axis=1)
        for p in range(moms // 2):
            for i in range(2):
                m = 2 * p + i
                for t in range(tiles):
                    at = slice(t * width, (t + 1) * width)
                    cosine = jnp.broadcast_to(table_ref[0, m : m + 1, at], (half, width))
                    sine = jnp.broadcast_to(table_ref[1, m : m + 1, at], (half, width))
                    for c in range(colours):
                        real = plain_ref[s, c, t, :half]
                        imag = plain_ref[s, c, t, half:]
                        base = i * width
                        phased_ref[s, p, c, t, base : base + half] = (
                            cosine * real - sine * imag
                        ).astype(jnp.bfloat16)
                        phased_ref[s, p, c, t, base + half : base + width] = (
                            sine * real + cosine * imag
                        ).astype(jnp.bfloat16)
            right = jnp.concatenate([phased_ref[s, p, c, t] for c, t in pieces], axis=1)
            products = lax.dot_general(
                left, right, (((1,), (1,)), ((), ())), preferred_element_type=jnp.float32
            )
            for i in range(2):
                block = products[:, i * width : (i + 1) * width]
                value = block[:half] + swapped(block[half:], 1.0, -1.0)
                for r in range(half // rows):
                    part_ref[r // spins, r % spins, s, 2 * p + i] = value[r * rows : (r + 1) * rows]
    for j in range(spaces):
        at = lax.rem(space + j, spaces)
        keep_ref[j] = part_ref[at, spin]
        for i in range(1, spins):
            give_ref[i - 1, j] = part_ref[at, lax.rem(spin + i, spins)]


def elementals(place, mom_t, x, spaces, spins):
    slots, colours, sites, width = x.shape
    moms = mom_t.shape[1]
    shape = (slots, moms, width // 2 // (spaces * spins), width)
    return pl.pallas_call(
        elementals_kernel,
        out_shape=[
            jax.ShapeDtypeStruct((spaces,) + shape, jnp.float32),
            jax.ShapeDtypeStruct((spins - 1, spaces) + shape, jnp.float32),
        ],
        in_specs=[ANY, ANY, ANY],
        out_specs=[VMEM, VMEM],
        scratch_shapes=[
            pltpu.VMEM(x.shape, x.dtype),
            pltpu.SMEM(place.shape, jnp.int32),
            pltpu.SMEM(mom_t.shape, jnp.int32),
            pltpu.VMEM((2, moms, sites), jnp.float32),
            pltpu.VMEM((slots, colours, sites // width, width, width), jnp.float32),
            pltpu.VMEM((slots, moms // 2, colours, sites // width, 2 * width, width), jnp.bfloat16),
            pltpu.VMEM((spaces, spins) + shape, jnp.float32),
            pltpu.SemaphoreType.DMA((2,)),
            pltpu.SemaphoreType.DMA((slots,)),
        ],
        compiler_params=params(24),
        name="elementals",
    )(place, in_hbm(mom_t), in_hbm(x))


def halfway_kernel(sink_ref, tau_ref, out_ref, right_ref, turn_ref):
    pairs, vectors, _ = tau_ref.shape
    _, moms, rows, width = sink_ref.shape
    count = moms * rows

    def step(k, carry):
        right_ref[:vectors] = tau_ref[k]
        for g in range(SPINS):
            at = slice(g * width, (g + 1) * width)
            right_ref[vectors:, at] = swapped(tau_ref[k, :, at], -1.0, 1.0).astype(jnp.bfloat16)
        product = jnp.dot(
            sink_ref[k].reshape(count, width),
            right_ref[...],
            preferred_element_type=jnp.float32,
        )
        for g in range(SPINS):
            turn_ref[pl.ds(g, count, stride=SPINS), :] = product[:, g * width : (g + 1) * width]
        out_ref[k] = turn_ref[...].astype(jnp.bfloat16)
        return carry

    lax.fori_loop(0, pairs, step, 0)


def halfway(sink_rows, perambulators):
    pairs, vectors, wide = perambulators.shape
    _, moms, rows, width = sink_rows.shape
    count = moms * rows * SPINS
    return pl.pallas_call(
        halfway_kernel,
        out_shape=jax.ShapeDtypeStruct((pairs, count, width), jnp.bfloat16),
        in_specs=[VMEM, VMEM],
        out_specs=VMEM,
        scratch_shapes=[
            pltpu.VMEM((2 * vectors, wide), jnp.bfloat16),
            pltpu.VMEM((count, width), jnp.float32),
        ],
        compiler_params=params(12),
        cost_estimate=pl.CostEstimate(
            flops=4 * pairs * moms * rows * vectors * wide, bytes_accessed=4 * 2**20, transcendentals=0
        ),
        name="halfway",
    )(sink_rows, perambulators)


def loops_kernel(place_hbm, half_ref, *rest):
    sources = rest[:-5]
    out_hbm, place_ref, full_ref, stage_ref, sems = rest[-5:]
    pairs, moms, rows, spinors, width = stage_ref.shape
    spaces, spins = full_ref.shape[2:4]
    vectors = width // 2
    count = rows * spinors
    place_copy = pltpu.make_async_copy(place_hbm, place_ref, sems.at[pairs * moms // 2])
    place_copy.start()
    place_copy.wait()
    space = place_ref[0]
    spin = place_ref[1]
    for j in range(spaces):
        for i in range(spins):
            full_ref[
                :, :, lax.rem(space + spaces - j, spaces), lax.rem(spin + spins - i, spins)
            ] = sources[j * spins + i][...]
    copies = []
    zeros = jnp.zeros((width, width), jnp.bfloat16)
    for k in range(pairs):
        for m in range(0, moms, 2):
            rights = []
            for i in range(2):
                source = full_ref[k, m + i].reshape(vectors, width)
                turned = swapped(source, -1.0, 1.0).astype(jnp.bfloat16)
                rights.append(jnp.concatenate([source, turned], axis=0))
            right = jnp.concatenate(
                [
                    jnp.concatenate([rights[0], zeros], axis=1),
                    jnp.concatenate([zeros, rights[1]], axis=1),
                ],
                axis=0,
            )
            left = jnp.concatenate(
                [half_ref[k, (m + i) * count : (m + i + 1) * count] for i in range(2)], axis=1
            )
            product = lax.dot_general(
                left, right, (((1,), (1,)), ((), ())), preferred_element_type=jnp.float32
            ).astype(jnp.bfloat16)
            for i in range(2):
                stage_ref[k, m + i] = product[:, i * width : (i + 1) * width].reshape(
                    rows, spinors, width
                )
            at = pl.ds(m, 2)
            copies.append(
                pltpu.make_async_copy(
                    stage_ref.at[k, at], out_hbm.at[k, at], sems.at[k * moms // 2 + m // 2]
                )
            )
            copies[-1].start()
    for copy in copies:
        copy.wait()


def loops(place, half, sources):
    pairs, _, width = half.shape
    spaces, spins = len(sources), len(sources[0])
    _, moms, rows, _ = sources[0][0].shape
    shape = (pairs, moms, rows, SPINS, width)
    return pl.pallas_call(
        loops_kernel,
        out_shape=jax.ShapeDtypeStruct(shape, jnp.bfloat16),
        in_specs=[ANY, VMEM] + [VMEM] * (spaces * spins),
        out_specs=HBM,
        scratch_shapes=[
            pltpu.SMEM(place.shape, jnp.int32),
            pltpu.VMEM((pairs, moms, spaces, spins, rows, width), jnp.bfloat16),
            pltpu.VMEM(shape, jnp.bfloat16),
            pltpu.SemaphoreType.DMA((pairs * moms // 2 + 1,)),
        ],
        compiler_params=params(16),
        name="loops",
    )(place, half, *[part for group in sources for part in group])


def shifted(value, axis, by):
    size = lax.axis_size(axis)
    return lax.ppermute(value, axis, [(i, (i + by) % size) for i in range(size)])


def around(value, axis):
    parts = [value]
    for j in range(1, lax.axis_size(axis)):
        parts.append(shifted(value, axis, j))
    return parts


def selected(index, candidates):
    flag = index[:, None, None, None]
    result = jnp.broadcast_to(candidates[0], (index.shape[0],) + candidates[0].shape)
    for n in range(1, len(candidates)):
        result = jnp.where(flag == n, candidates[n], result)
    return result


def per_device(eigenvectors, momenta, time_pairs, slot_map, perambulators):
    spaces = lax.axis_size("space")
    spins = lax.axis_size("spin")
    members = lax.axis_size("tm")
    slots = eigenvectors.shape[0]
    place = jnp.stack([lax.axis_index("space"), lax.axis_index("spin")]).astype(jnp.int32)
    times = slot_map.shape[0]
    named = time_pairs[:, :, None] == lax.iota(jnp.int32, times)
    slot = jnp.sum(jnp.where(named, slot_map, 0), axis=-1)
    back = (lax.axis_index("tm") + members - slot // slots) % members
    index = back * slots + slot % slots

    keep, give = elementals(
        place, momenta.T, jnp.transpose(eigenvectors, (0, 2, 1, 3)), spaces, spins
    )
    total = keep
    for i in range(1, spins):
        total = total + shifted(give[i - 1], "spin", i)
    row_share = total[0]
    for j in range(1, spaces):
        row_share = row_share + shifted(total[j].astype(jnp.bfloat16), "space", j).astype(
            jnp.float32
        )
    row_share = row_share.astype(jnp.bfloat16)
    arrived = around(row_share, "tm")
    candidates = [part[s] for part in arrived for s in range(slots)]
    source_share = selected(index[:, 1], candidates)
    sink_rows = selected(index[:, 0], candidates)
    far = around(source_share, "space")
    sources = [around(part, "spin") for part in far]
    half = halfway(sink_rows, perambulators)
    return loops(place, half, sources)


def solution(mesh):
    placed = (
        P(("cfg", "tm"), ("space", "spin"), None, None),
        P(),
        P(("cfg", "tm"), None),
        P(),
        P(("cfg", "tm"), None, None),
    )

    return jax.shard_map(
        per_device,
        mesh=mesh,
        in_specs=placed,
        out_specs=P(("cfg", "tm"), None, ("space", "spin"), None, None),
        check_vma=False,
    )
```

time: 156 us -> 30.6 us (0.20)
  other arithmetic: 52.9 us -> 1.3 us
  local copies, waits for them, and re-layouts: 42.6 us -> 0.04 us
  blocking collectives: 20.8 us -> 0 us
  matrix products: 19.3 us -> 0 us
  between operations: 13.6 us -> 0.09 us
  starting transfers between devices: 0.01 us -> 11.1 us
  Pallas kernels: 0 us -> 8.81 us
  waiting for transfers between devices: 5.82 us -> 9.17 us
    sin x16 -> x0, other arithmetic: 31 us -> none  [elemental(): sines = jnp.sin(angles)[:, None, None]]
    all_gather x2 -> x0, blocking collectives: 20.8 us -> none  [the longest x1 13.9 us: per_device(): lax.all_gather(part, 'tm', axis=0, tiled=True)]
    another operation x18 -> x0, local copies, waits for them, and re-layouts: 20.5 us -> none  [the longest x16 18 us: elemental(): jnp.stack([upper_rows, lower_rows], axis=2)]
    dot_general x20 -> x0, matrix products: 19.3 us -> none  [the longest x16 14.7 us: elemental(): lax.dot_general(conj_left, phased, (((0,), (0,)), ((), ())), preferred_el...]
    another operation x43 -> x1, other arithmetic: 13.7 us -> 0.07 us  [per_device(): jnp.stack([lax.axis_index('space'), lax.axis_index('spin')])]
    reshape x6 -> x0, local copies, waits for them, and re-layouts: 13.2 us -> none  [the longest x1 4.43 us: contract(): parts = perambulators.reshape(pair_count, vectors, 16, 2, vectors)]
    ppermute x0 -> x8, starting transfers between devices: none -> 11.1 us  [shifted(): lax.ppermute(value, axis, [(i, (i + by) % size) for i in range(size)])]
    ppermute x0 -> x8, waiting for transfers between devices: none -> 9.17 us  [shifted(): lax.ppermute(value, axis, [(i, (i + by) % size) for i in range(size)])]
  transfers between devices with their start and end apart: 1 -> 8, of which waited for: 1 -> 6; matrix products, arithmetic and copies ran while one was open for 12% -> 3% of each run, Pallas kernels for 0% -> 8%
where the time goes in v2:
time: 30.6 us; the launch traced here: 30.5 us
  starting transfers between devices  11.1 us (36%)
  waiting for transfers between devices  9.17 us (30%)
  Pallas kernels  8.81 us (29%)
  other arithmetic  1.3 us (4%)
    ppermute x8, starting transfers between devices, shifted(): lax.ppermute(value, axis, [(i, (i + by) % size) for i in range(size)])  11.1 us
    ppermute x8, waiting for transfers between devices, shifted(): lax.ppermute(value, axis, [(i, (i + by) % size) for i in range(size)])  9.17 us
    pallas_call x1, Pallas kernels, elementals(): pl.pallas_call(elementals_kernel, out_shape=[jax.ShapeDtypeStruct((spaces...  4.08 us
    pallas_call x1, Pallas kernels, halfway(): pl.pallas_call(halfway_kernel, out_shape=jax.ShapeDtypeStruct((pairs, cou...  2.39 us
    pallas_call x1, Pallas kernels, loops(): pl.pallas_call(loops_kernel, out_shape=jax.ShapeDtypeStruct(shape, jnp.bf...  2.35 us
    reduce_sum x1, other arithmetic, per_device(): slot = jnp.sum(jnp.where(named, slot_map, 0), axis=-1)  0.9 us
  transfers between devices with their start and end apart: 8, of which 6 were waited for; matrix products, arithmetic and copies ran while one was open for 3% of the time, Pallas kernels for 8%

profile of v2, /device:TPU:0, one launch (start us, length us, event | category | flops | bytes accessed | tf_op | source)
XLA Modules:
  0.0 30.5 jit_solution(4416680837993239248)
XLA Ops:
  0.0 0.0 copy-start
  0.0 0.1 pad_add_fusion.place_hbm
  0.1 4.1 %elementals.1 = (f32[2,2,8,16,128]{4,3,2,1,0:T(8,128)S(1)}, f32[1,2,2,8,16,128]{5,4,3,2,1,0:T(8,128)S(1)}) custom-call(s32[2]{0:T(128)S(1)} %pad_add_fusion.place_hbm, s32[3,8]{1,0:T(4,128)} %bitcast.59, bf16[2,3,512,128]{3,2,1,0:T(8,128)(2,1)} %bitcast.58), custom_call_target="tpu_custom_call" | custom-call | tf_op jit(solution)/shard_map/elementals/pallas_call | solution.py:111
  4.2 0.6 %collective-permute-start = (f32[2,2,8,16,128]{4,3,2,1,0:T(8,128)S(1)}, f32[2,2,8,16,128]{4,3,2,1,0:T(8,128)S(1)}, u32[]{:S(2)}, u32[]{:S(2)}) collective-permute-start(f32[2,2,8,16,128]{4,3,2,1,0:T(8,128)S(1)} %bitcast.57), channel_id=1, source_target_pairs={{0,1},{1,0},{2,3},{3,2},{4,5},{5,4},{6,7},{7,6},{8,9},{9,8},{10,11... | collective-permute-start | bytes 786440 | tf_op jit(solution)/shard_map/ppermute | solution.py:256
  4.7 0.9 %select_reduce_fusion = s32[4,2]{0,1:T(2,128)S(1)} fusion(s32[8]{0:T(128)} %param.8, s32[4,2]{0,1:T(2,128)} %param.7), kind=kLoop, calls=%fused_computation.15 | loop fusion | flops 184 | bytes 96 | tf_op jit(solution)/shard_map/reduce_sum | solution.py:282
  5.7 0.2 collective-permute-done
  5.9 2.9 %collective-permute-start.1 = (bf16[2,8,16,128]{3,2,1,0:T(8,128)(2,1)S(1)}, bf16[2,8,16,128]{3,2,1,0:T(8,128)(2,1)S(1)}, u32[]{:S(2)}, u32[]{:S(2)}) collective-permute-start(bf16[2,8,16,128]{3,2,1,0:T(8,128)(2,1)S(1)} %fusion.2), channel_id=1, source_target_pairs={{0,2},{2,0},{1,3},{3,1},{4,6},{6,4},{5,7},{7,5},{8,10},{10,8},{9,1... | collective-permute-start | bytes 196616 | tf_op jit(solution)/shard_map/ppermute | solution.py:256
  8.9 2.4 %collective-permute-done.1 = bf16[2,8,16,128]{3,2,1,0:T(8,128)(2,1)S(1)} collective-permute-done((bf16[2,8,16,128]{3,2,1,0:T(8,128)(2,1)S(1)}, bf16[2,8,16,128]{3,2,1,0:T(8,128)(2,1)S(1)}, u32[]{:S(2)}, u32[]{:S(2)}) %collective-permute-start.1) | collective-permute-done | bytes 65568 | tf_op jit(solution)/shard_map/ppermute | solution.py:256
  11.3 2.0 %collective-permute-start.4 = (bf16[2,8,16,128]{3,2,1,0:T(8,128)(2,1)S(1)}, bf16[2,8,16,128]{3,2,1,0:T(8,128)(2,1)S(1)}, u32[]{:S(2)}, u32[]{:S(2)}) collective-permute-start(bf16[2,8,16,128]{3,2,1,0:T(8,128)(2,1)S(1)} %fusion.1), channel_id=1, source_target_pairs={{0,4},{4,8},{8,12},{12,0},{1,5},{5,9},{9,13},{13,1},{2,6},{6,10},{... | collective-permute-start | bytes 196616 | tf_op jit(solution)/shard_map/ppermute | solution.py:256
  13.3 2.6 %collective-permute-start.3 = (bf16[2,8,16,128]{3,2,1,0:T(8,128)(2,1)S(1)}, bf16[2,8,16,128]{3,2,1,0:T(8,128)(2,1)S(1)}, u32[]{:S(2)}, u32[]{:S(2)}) collective-permute-start(bf16[2,8,16,128]{3,2,1,0:T(8,128)(2,1)S(1)} %fusion.1), channel_id=1, source_target_pairs={{0,8},{4,12},{8,0},{12,4},{1,9},{5,13},{9,1},{13,5},{2,10},{6,14},... | collective-permute-start | bytes 196616 | tf_op jit(solution)/shard_map/ppermute | solution.py:256
  15.9 1.3 %collective-permute-start.2 = (bf16[2,8,16,128]{3,2,1,0:T(8,128)(2,1)S(1)}, bf16[2,8,16,128]{3,2,1,0:T(8,128)(2,1)S(1)}, u32[]{:S(2)}, u32[]{:S(2)}) collective-permute-start(bf16[2,8,16,128]{3,2,1,0:T(8,128)(2,1)S(1)} %fusion.1), channel_id=1, source_target_pairs={{0,12},{4,0},{8,4},{12,8},{1,13},{5,1},{9,5},{13,9},{2,14},{6,2},{... | collective-permute-start | bytes 196616 | tf_op jit(solution)/shard_map/ppermute | solution.py:256
  17.2 1.1 %collective-permute-done.4 = bf16[2,8,16,128]{3,2,1,0:T(8,128)(2,1)S(1)} collective-permute-done((bf16[2,8,16,128]{3,2,1,0:T(8,128)(2,1)S(1)}, bf16[2,8,16,128]{3,2,1,0:T(8,128)(2,1)S(1)}, u32[]{:S(2)}, u32[]{:S(2)}) %collective-permute-start.4) | collective-permute-done | bytes 65568 | tf_op jit(solution)/shard_map/ppermute | solution.py:256
  18.3 1.8 %collective-permute-done.3 = bf16[2,8,16,128]{3,2,1,0:T(8,128)(2,1)S(1)} collective-permute-done((bf16[2,8,16,128]{3,2,1,0:T(8,128)(2,1)S(1)}, bf16[2,8,16,128]{3,2,1,0:T(8,128)(2,1)S(1)}, u32[]{:S(2)}, u32[]{:S(2)}) %collective-permute-start.3) | collective-permute-done | bytes 65568 | tf_op jit(solution)/shard_map/ppermute | solution.py:256
  20.1 0.3 collective-permute-done.2
  20.4 0.1 select_select_fusion.rest_0_
  20.6 1.7 %collective-permute-start.6 = (bf16[4,8,16,128]{3,2,1,0:T(8,128)(2,1)S(1)}, bf16[4,8,16,128]{3,2,1,0:T(8,128)(2,1)S(1)}, u32[]{:S(2)}, u32[]{:S(2)}) collective-permute-start(bf16[4,8,16,128]{3,2,1,0:T(8,128)(2,1)S(1)} %select_select_fusion.rest_0_), channel_id=1, source_target_pairs={{0,2},{2,0},{1,3},{3,1},{4,6},{6,4},{5,7},{7,5},{8,10},{10,8},{9,1... | collective-permute-start | bytes 393224 | tf_op jit(solution)/shard_map/ppermute | solution.py:256
  22.2 0.0 collective-permute-start.5
  22.2 3.4 %collective-permute-done.6.rest_2_ = bf16[4,8,16,128]{3,2,1,0:T(8,128)(2,1)S(1)} collective-permute-done((bf16[4,8,16,128]{3,2,1,0:T(8,128)(2,1)S(1)}, bf16[4,8,16,128]{3,2,1,0:T(8,128)(2,1)S(1)}, u32[]{:S(2)}, u32[]{:S(2)}) %collective-permute-start.6) | collective-permute-done | bytes 131104 | tf_op jit(solution)/shard_map/ppermute | solution.py:256
  25.6 0.0 collective-permute-start.7
  25.6 0.1 select_select_fusion.1.sink_ref
  25.7 0.0 copy-done
  25.7 2.4 %halfway.1.half_ref = bf16[4,2048,128]{2,1,0:T(8,128)(2,1)S(1)} custom-call(bf16[4,8,16,128]{3,2,1,0:T(8,128)(2,1)S(1)} %select_select_fusion.1.sink_ref, bf16[4,64,2048]{2,1,0:T(8,128)(2,1)S(1)} %copy-done), custom_call_target="tpu_custom_call" | custom-call | flops 268435456 | bytes 4194304 | tf_op jit(solution)/shard_map/halfway/pallas_call | solution.py:162
  28.1 0.0 collective-permute-done.5.rest_1_
  28.1 0.0 collective-permute-done.7.rest_3_
  28.1 2.3 %loops.1 = bf16[4,8,16,16,128]{4,3,2,1,0:T(8,128)(2,1)} custom-call(s32[2]{0:T(128)S(1)} %pad_add_fusion.place_hbm, bf16[4,2048,128]{2,1,0:T(8,128)(2,1)S(1)} %halfway.1.half_ref, bf16[4,8,16,128]{3,2,1,0:T(8,128)(2,1)S(1)} %select_select_fusion.rest_0_, bf16[4,8,16,128]{3,2,1,0:T(8,128)(2,1)S(1)} %collective-permute-done.5.rest_1_, ...), custom_call_target="tpu_custom_call" | custom-call | tf_op jit(solution)/shard_map/loops/pallas_call | solution.py:238
  (9 shorter events, 0.1 us)
Async XLA Ops:
  0.0 25.7 %copy-start = (bf16[4,64,2048]{2,1,0:T(8,128)(2,1)S(1)}, bf16[4,64,2048]{2,1,0:T(8,128)(2,1)}, u32[]{:S(2)}) copy-start(bf16[4,64,2048]{2,1,0:T(8,128)(2,1)} %tau_ref.1) | copy-start | bytes 3145732
  4.2 1.7 %collective-permute-start = (f32[2,2,8,16,128]{4,3,2,1,0:T(8,128)S(1)}, f32[2,2,8,16,128]{4,3,2,1,0:T(8,128)S(1)}, u32[]{:S(2)}, u32[]{:S(2)}) collective-permute-start(f32[2,2,8,16,128]{4,3,2,1,0:T(8,128)S(1)} %bitcast.57), channel_id=1, source_target_pairs={{0,1},{1,0},{2,3},{3,2},{4,5},{5,4},{6,7},{7,6},{8,9},{9,8},{10,11... | collective-permute-start | bytes 786440 | tf_op jit(solution)/shard_map/ppermute | solution.py:256
  5.9 5.3 %collective-permute-start.1 = (bf16[2,8,16,128]{3,2,1,0:T(8,128)(2,1)S(1)}, bf16[2,8,16,128]{3,2,1,0:T(8,128)(2,1)S(1)}, u32[]{:S(2)}, u32[]{:S(2)}) collective-permute-start(bf16[2,8,16,128]{3,2,1,0:T(8,128)(2,1)S(1)} %fusion.2), channel_id=1, source_target_pairs={{0,2},{2,0},{1,3},{3,1},{4,6},{6,4},{5,7},{7,5},{8,10},{10,8},{9,1... | collective-permute-start | bytes 196616 | tf_op jit(solution)/shard_map/ppermute | solution.py:256
  11.3 7.1 %collective-permute-start.4 = (bf16[2,8,16,128]{3,2,1,0:T(8,128)(2,1)S(1)}, bf16[2,8,16,128]{3,2,1,0:T(8,128)(2,1)S(1)}, u32[]{:S(2)}, u32[]{:S(2)}) collective-permute-start(bf16[2,8,16,128]{3,2,1,0:T(8,128)(2,1)S(1)} %fusion.1), channel_id=1, source_target_pairs={{0,4},{4,8},{8,12},{12,0},{1,5},{5,9},{9,13},{13,1},{2,6},{6,10},{... | collective-permute-start | bytes 196616 | tf_op jit(solution)/shard_map/ppermute | solution.py:256
  13.3 6.8 %collective-permute-start.3 = (bf16[2,8,16,128]{3,2,1,0:T(8,128)(2,1)S(1)}, bf16[2,8,16,128]{3,2,1,0:T(8,128)(2,1)S(1)}, u32[]{:S(2)}, u32[]{:S(2)}) collective-permute-start(bf16[2,8,16,128]{3,2,1,0:T(8,128)(2,1)S(1)} %fusion.1), channel_id=1, source_target_pairs={{0,8},{4,12},{8,0},{12,4},{1,9},{5,13},{9,1},{13,5},{2,10},{6,14},... | collective-permute-start | bytes 196616 | tf_op jit(solution)/shard_map/ppermute | solution.py:256
  15.9 4.5 %collective-permute-start.2 = (bf16[2,8,16,128]{3,2,1,0:T(8,128)(2,1)S(1)}, bf16[2,8,16,128]{3,2,1,0:T(8,128)(2,1)S(1)}, u32[]{:S(2)}, u32[]{:S(2)}) collective-permute-start(bf16[2,8,16,128]{3,2,1,0:T(8,128)(2,1)S(1)} %fusion.1), channel_id=1, source_target_pairs={{0,12},{4,0},{8,4},{12,8},{1,13},{5,1},{9,5},{13,9},{2,14},{6,2},{... | collective-permute-start | bytes 196616 | tf_op jit(solution)/shard_map/ppermute | solution.py:256
  20.6 5.0 %collective-permute-start.6 = (bf16[4,8,16,128]{3,2,1,0:T(8,128)(2,1)S(1)}, bf16[4,8,16,128]{3,2,1,0:T(8,128)(2,1)S(1)}, u32[]{:S(2)}, u32[]{:S(2)}) collective-permute-start(bf16[4,8,16,128]{3,2,1,0:T(8,128)(2,1)S(1)} %select_select_fusion.rest_0_), channel_id=1, source_target_pairs={{0,2},{2,0},{1,3},{3,1},{4,6},{6,4},{5,7},{7,5},{8,10},{10,8},{9,1... | collective-permute-start | bytes 393224 | tf_op jit(solution)/shard_map/ppermute | solution.py:256
  22.2 5.9 %collective-permute-start.5 = (bf16[4,8,16,128]{3,2,1,0:T(8,128)(2,1)S(1)}, bf16[4,8,16,128]{3,2,1,0:T(8,128)(2,1)S(1)}, u32[]{:S(2)}, u32[]{:S(2)}) collective-permute-start(bf16[4,8,16,128]{3,2,1,0:T(8,128)(2,1)S(1)} %select_select_fusion.rest_0_), channel_id=1, source_target_pairs={{0,1},{1,0},{2,3},{3,2},{4,5},{5,4},{6,7},{7,6},{8,9},{9,8},{10,11... | collective-permute-start | bytes 393224 | tf_op jit(solution)/shard_map/ppermute | solution.py:256
  25.6 2.5 %collective-permute-start.7 = (bf16[4,8,16,128]{3,2,1,0:T(8,128)(2,1)S(1)}, bf16[4,8,16,128]{3,2,1,0:T(8,128)(2,1)S(1)}, u32[]{:S(2)}, u32[]{:S(2)}) collective-permute-start(bf16[4,8,16,128]{3,2,1,0:T(8,128)(2,1)S(1)} %collective-permute-done.6.rest_2_), channel_id=1, source_target_pairs={{0,1},{1,0},{2,3},{3,2},{4,5},{5,4},{6,7},{7,6},{8,9},{9,8},{10,11... | collective-permute-start | bytes 393224 | tf_op jit(solution)/shard_map/ppermute | solution.py:256

commit v3 on v2

v3 whole, which is shorter than its diff:
```python
import jax
import jax.numpy as jnp
from jax import lax
from jax.experimental import pallas as pl
from jax.experimental.pallas import tpu as pltpu
from jax.sharding import PartitionSpec as P


LAT = 32
TURN = 6.283185307179586
SPINS = 16
SMEM = pl.BlockSpec(memory_space=pltpu.SMEM)
VMEM = pl.BlockSpec(memory_space=pltpu.VMEM)
HBM = pl.BlockSpec(memory_space=pltpu.HBM)
ANY = pl.BlockSpec(memory_space=pl.ANY)


def params(mib):
    return pltpu.CompilerParams(vmem_limit_bytes=mib * 1024 * 1024)


def in_hbm(value):
    return pltpu.with_memory_space_constraint(value, pltpu.HBM)


def swapped(value, first, second):
    half = value.shape[1] // 2
    lane = lax.broadcasted_iota(jnp.int32, value.shape, 1)
    sign = jnp.where(lane < half, first, second).astype(jnp.float32)
    return pltpu.roll(value.astype(jnp.float32), half, 1) * sign


def turn_and_sum(lefts, table_ref, first, phased_ref, sum_ref):
    slots, colours, _, tiles, _, width = phased_ref.shape
    half = width // 2
    spaces, _, count, rows, _ = sum_ref.shape
    for s in range(slots):
        totals = [None] * (count // 2)
        for c in range(colours):
            left = [lefts(s, c, t) for t in range(tiles)]
            for t in range(tiles):
                at = slice(t * width, (t + 1) * width)
                real = left[t][:half].astype(jnp.float32)
                imag = left[t][half:].astype(jnp.float32)
                for m in range(count):
                    row = slice(first + m, first + m + 1)
                    cosine = jnp.broadcast_to(table_ref[0, row, at], (half, width))
                    sine = jnp.broadcast_to(table_ref[1, row, at], (half, width))
                    top = m % 2 * width
                    phased_ref[s, c, m // 2, t, top : top + half] = (
                        cosine * real - sine * imag
                    ).astype(jnp.bfloat16)
                    phased_ref[s, c, m // 2, t, top + half : top + width] = (
                        sine * real + cosine * imag
                    ).astype(jnp.bfloat16)
            left = jnp.concatenate(left, axis=1)
            for p in range(count // 2):
                right = jnp.concatenate([phased_ref[s, c, p, t] for t in range(tiles)], axis=1)
                product = lax.dot_general(
                    left, right, (((1,), (1,)), ((), ())), preferred_element_type=jnp.float32
                )
                totals[p] = product if totals[p] is None else totals[p] + product
        for m in range(count):
            block = totals[m // 2][:, m % 2 * width : (m % 2 + 1) * width]
            value = block[:half] + swapped(block[half:], 1.0, -1.0)
            for r in range(spaces):
                sum_ref[r, s, m] = value[r * rows : (r + 1) * rows]


def given_kernel(place_hbm, mom_hbm, x_hbm, out_ref, table_ref, turned_ref, *scratch):
    x_ref, place_ref, mom_ref, phased_ref, sum_ref, sems = scratch
    _, _, sites, width = x_ref.shape
    spaces, _, count, _, _ = out_ref.shape
    moms = mom_ref.shape[1]
    spins = moms // count
    x_copy = pltpu.make_async_copy(x_hbm, x_ref, sems.at[0])
    mom_copy = pltpu.make_async_copy(mom_hbm, mom_ref, sems.at[1])
    place_copy = pltpu.make_async_copy(place_hbm, place_ref, sems.at[2])
    mom_copy.start()
    place_copy.start()
    x_copy.start()
    row = lax.broadcasted_iota(jnp.int32, (moms, sites), 0)
    site = lax.broadcasted_iota(jnp.int32, (moms, sites), 1)
    place_copy.wait()
    space = place_ref[0]
    spin = place_ref[1]
    site = site + (space * spins + spin) * sites
    coords = (site % LAT, site // LAT % LAT, site // (LAT * LAT))
    mom_copy.wait()
    wave = jnp.zeros((moms, sites), jnp.int32)
    for d in range(3):
        value = jnp.zeros((moms, sites), jnp.int32)
        for m in range(moms):
            value = jnp.where(
                row == m, mom_ref[d, lax.rem(spin + m // count, spins) * count + m % count], value
            )
        wave = wave + value * coords[d]
    angle = (wave & (LAT - 1)).astype(jnp.float32) * (TURN / LAT)
    table_ref[0] = jnp.cos(angle)
    table_ref[1] = jnp.sin(angle)
    x_copy.wait()

    def lefts(s, c, t):
        value = x_ref[s, c, t * width : (t + 1) * width].T
        turned_ref[s, c, t] = value
        return value

    turn_and_sum(lefts, table_ref, count, phased_ref, sum_ref)
    for j in range(spaces):
        out_ref[j] = sum_ref[lax.rem(space + j, spaces)]


def given(place, mom_t, x, spaces, spins):
    slots, colours, sites, width = x.shape
    moms = mom_t.shape[1]
    count = moms // spins
    shape = (spaces, slots, count, width // 2 // spaces, width)
    tiles = sites // width
    return pl.pallas_call(
        given_kernel,
        out_shape=[
            jax.ShapeDtypeStruct(shape, jnp.float32),
            jax.ShapeDtypeStruct((2, moms, sites), jnp.float32),
            jax.ShapeDtypeStruct((slots, colours, tiles, width, width), x.dtype),
        ],
        in_specs=[ANY, ANY, ANY],
        out_specs=[VMEM] * 3,
        scratch_shapes=[
            pltpu.VMEM(x.shape, x.dtype),
            pltpu.SMEM(place.shape, jnp.int32),
            pltpu.SMEM(mom_t.shape, jnp.int32),
            pltpu.VMEM((slots, colours, count // 2, tiles, 2 * width, width), jnp.bfloat16),
            pltpu.VMEM(shape, jnp.float32),
            pltpu.SemaphoreType.DMA((3,)),
        ],
        compiler_params=params(20),
        name="given",
    )(place, in_hbm(mom_t), in_hbm(x))


def kept_kernel(place_hbm, table_ref, turned_ref, out_ref, place_ref, phased_ref, sum_ref, sem):
    spaces = out_ref.shape[0]
    place_copy = pltpu.make_async_copy(place_hbm, place_ref, sem)
    place_copy.start()
    turn_and_sum(lambda s, c, t: turned_ref[s, c, t], table_ref, 0, phased_ref, sum_ref)
    place_copy.wait()
    for j in range(spaces):
        out_ref[j] = sum_ref[lax.rem(place_ref[0] + j, spaces)]


def kept(place, table, turned, spaces, spins):
    slots, colours, tiles, width, _ = turned.shape
    count = table.shape[1] // spins
    shape = (spaces, slots, count, width // 2 // spaces, width)
    return pl.pallas_call(
        kept_kernel,
        out_shape=jax.ShapeDtypeStruct(shape, jnp.float32),
        in_specs=[ANY, VMEM, VMEM],
        out_specs=VMEM,
        scratch_shapes=[
            pltpu.SMEM(place.shape, jnp.int32),
            pltpu.VMEM((slots, colours, count // 2, tiles, 2 * width, width), jnp.bfloat16),
            pltpu.VMEM(shape, jnp.float32),
            pltpu.SemaphoreType.DMA,
        ],
        compiler_params=params(20),
        name="kept",
    )(place, table, turned)


def doubled_kernel(tau_ref, out_ref):
    pairs, vectors, wide = tau_ref.shape
    width = 2 * vectors
    for k in range(pairs):
        out_ref[k, :vectors] = tau_ref[k]
        for g in range(wide // width):
            at = slice(g * width, (g + 1) * width)
            out_ref[k, vectors:, at] = swapped(tau_ref[k, :, at], -1.0, 1.0).astype(jnp.bfloat16)


def doubled(perambulators):
    pairs, vectors, wide = perambulators.shape
    return pl.pallas_call(
        doubled_kernel,
        out_shape=jax.ShapeDtypeStruct((pairs, 2 * vectors, wide), perambulators.dtype),
        in_specs=[VMEM],
        out_specs=VMEM,
        compiler_params=params(8),
        name="doubled",
    )(perambulators)


def halfway_kernel(right_ref, *rest):
    sinks, out_ref, turn_ref = rest[:-2], rest[-2], rest[-1]
    pairs, count, rows, width = sinks[0].shape
    lines = len(sinks) * count * rows

    def step(k, carry):
        left = jnp.concatenate([sink[k].reshape(count * rows, width) for sink in sinks], axis=0)
        product = jnp.dot(left, right_ref[k], preferred_element_type=jnp.float32)
        for g in range(SPINS):
            turn_ref[pl.ds(g, lines, stride=SPINS), :] = product[:, g * width : (g + 1) * width]
        out_ref[k] = turn_ref[...].astype(jnp.bfloat16)
        return carry

    lax.fori_loop(0, pairs, step, 0)


def halfway(right, sinks):
    pairs, count, rows, width = sinks[0].shape
    lines = len(sinks) * count * rows * SPINS
    return pl.pallas_call(
        halfway_kernel,
        out_shape=jax.ShapeDtypeStruct((pairs, lines, width), jnp.bfloat16),
        in_specs=[VMEM] * (1 + len(sinks)),
        out_specs=VMEM,
        scratch_shapes=[pltpu.VMEM((lines, width), jnp.float32)],
        compiler_params=params(8),
        name="halfway",
    )(right, *sinks)


def loops_kernel(place_hbm, half_ref, *rest):
    sources = rest[:-5]
    out_hbm, place_ref, full_ref, stage_ref, sems = rest[-5:]
    pairs, moms, rows, spinors, width = stage_ref.shape
    _, _, spaces, _, _ = full_ref.shape
    spins = len(sources) // spaces
    part = moms // spins
    vectors = width // 2
    count = rows * spinors
    place_copy = pltpu.make_async_copy(place_hbm, place_ref, sems.at[pairs * moms // 2])
    place_copy.start()
    place_copy.wait()
    space = place_ref[0]
    spin = place_ref[1]
    for i in range(spins):
        for j in range(spaces):
            full_ref[:, i * part : (i + 1) * part, lax.rem(space + spaces - j, spaces)] = sources[
                i * spaces + j
            ][...]
    copies = []
    zeros = jnp.zeros((width, width), jnp.bfloat16)
    for k in range(pairs):
        for m in range(0, moms, 2):
            rights = []
            for i in range(2):
                source = full_ref[k, m + i].reshape(vectors, width)
                turned = swapped(source, -1.0, 1.0).astype(jnp.bfloat16)
                rights.append(jnp.concatenate([source, turned], axis=0))
            right = jnp.concatenate(
                [
                    jnp.concatenate([rights[0], zeros], axis=1),
                    jnp.concatenate([zeros, rights[1]], axis=1),
                ],
                axis=0,
            )
            left = jnp.concatenate(
                [half_ref[k, (m + i) * count : (m + i + 1) * count] for i in range(2)], axis=1
            )
            product = lax.dot_general(
                left, right, (((1,), (1,)), ((), ())), preferred_element_type=jnp.float32
            ).astype(jnp.bfloat16)
            for i in range(2):
                stage_ref[k, m + i] = product[:, i * width : (i + 1) * width].reshape(
                    rows, spinors, width
                )
            first = lax.rem(spin + spins - m // part, spins) * part + m % part
            copies.append(
                pltpu.make_async_copy(
                    stage_ref.at[k, pl.ds(m, 2)],
                    out_hbm.at[k, pl.ds(first, 2)],
                    sems.at[k * moms // 2 + m // 2],
                )
            )
            copies[-1].start()
    for copy in copies:
        copy.wait()


def loops(place, half, sources):
    pairs, lines, width = half.shape
    spins, spaces = len(sources), len(sources[0])
    _, part, block, _ = sources[0][0].shape
    moms = spins * part
    shape = (pairs, moms, lines // (moms * SPINS), SPINS, width)
    return pl.pallas_call(
        loops_kernel,
        out_shape=jax.ShapeDtypeStruct(shape, jnp.bfloat16),
        in_specs=[ANY, VMEM] + [VMEM] * (spaces * spins),
        out_specs=HBM,
        scratch_shapes=[
            pltpu.SMEM(place.shape, jnp.int32),
            pltpu.VMEM((pairs, moms, spaces, block, width), jnp.bfloat16),
            pltpu.VMEM(shape, jnp.bfloat16),
            pltpu.SemaphoreType.DMA((pairs * moms // 2 + 1,)),
        ],
        compiler_params=params(16),
        name="loops",
    )(place, half, *[block for group in sources for block in group])


def shifted(value, axis, by):
    size = lax.axis_size(axis)
    return lax.ppermute(value, axis, [(i, (i + by) % size) for i in range(size)])


def around(value, axis):
    parts = [value]
    for j in range(1, lax.axis_size(axis)):
        parts.append(shifted(value, axis, j))
    return parts


def across(value, axis):
    size = lax.axis_size(axis)
    parts = [value]
    for j in range(1, size):
        parts.append(lax.ppermute(value, axis, [(i, i ^ j) for i in range(size)]))
    return parts


def selected(index, candidates):
    flag = index[:, None, None, None]
    result = jnp.broadcast_to(candidates[0], (index.shape[0],) + candidates[0].shape)
    for n in range(1, len(candidates)):
        result = jnp.where(flag == n, candidates[n], result)
    return result


def per_device(eigenvectors, momenta, time_pairs, slot_map, perambulators):
    spaces = lax.axis_size("space")
    spins = lax.axis_size("spin")
    slots = eigenvectors.shape[0]
    place = jnp.stack([lax.axis_index("space"), lax.axis_index("spin")]).astype(jnp.int32)
    times = slot_map.shape[0]
    named = time_pairs[:, :, None] == lax.iota(jnp.int32, times)
    slot = jnp.sum(jnp.where(named, slot_map, 0), axis=-1)
    index = (lax.axis_index("tm") ^ slot // slots) * slots + slot % slots

    spin = lax.axis_index("spin")
    x = jnp.transpose(eigenvectors, (0, 2, 1, 3))
    send, table, turned = given(place, momenta.T, x, spaces, spins)
    received = shifted(send, "spin", 1)
    total = kept(place, table, turned, spaces, spins)
    total = total + received
    row_share = total[0]
    for j in range(1, spaces):
        value = shifted(total[j].astype(jnp.bfloat16), "space", j)
        row_share = row_share + value.astype(jnp.float32)
    row_share = row_share.astype(jnp.bfloat16)
    arrived = across(row_share, "tm")
    candidates = [value[s] for value in arrived for s in range(slots)]
    source_share = selected(index[:, 1], candidates)
    sink_share = selected(index[:, 0], candidates)
    rows = sink_share.shape[2] // spins
    sinks = []
    for i in range(spins):
        block = lax.dynamic_slice_in_dim(sink_share, (spin + i) % spins * rows, rows, axis=2)
        if i:
            block = shifted(block, "spin", i)
        sinks.append(block)
    right = doubled(perambulators)
    half = halfway(right, sinks)
    far = around(source_share, "space")
    near = [around(value, "spin") for value in far]
    sources = [[group[i] for group in near] for i in range(spins)]
    return loops(place, half, sources)


def solution(mesh):
    placed = (
        P(("cfg", "tm"), ("space", "spin"), None, None),
        P(),
        P(("cfg", "tm"), None),
        P(),
        P(("cfg", "tm"), None, None),
    )

    members = mesh.shape["tm"]
    order = [j for j in range(1, members) if j & (j + 1) == 0][::-1]
    order += [j for j in range(1, members) if j not in order]
    return jax.shard_map(
        per_device,
        mesh=mesh,
        in_specs=placed,
        out_specs=P(("cfg", "tm"), None, ("space", "spin"), None, None),
        check_vma=False,
    )
```

time: 30.6 us -> 32.8 us (1.072)
  waiting for transfers between devices: 9.17 us -> 12.6 us
  starting transfers between devices: 11.1 us -> 9.79 us
    ppermute x0 -> x3, waiting for transfers between devices: none -> 6.04 us  [across(): parts.append(lax.ppermute(value, axis, [(i, i ^ j) for i in range(size)]))]
    ppermute x8 -> x6, starting transfers between devices: 11.1 us -> 5.32 us  [shifted(): lax.ppermute(value, axis, [(i, (i + by) % size) for i in range(size)])]
    ppermute x0 -> x3, starting transfers between devices: none -> 4.48 us  [across(): parts.append(lax.ppermute(value, axis, [(i, i ^ j) for i in range(size)]))]
    ppermute x8 -> x6, waiting for transfers between devices: 9.17 us -> 6.51 us  [shifted(): lax.ppermute(value, axis, [(i, (i + by) % size) for i in range(size)])]
    pallas_call x2 -> x4, Pallas kernels: 6.46 us -> 6.47 us  [the longest x1 2.82 us: given(): pl.pallas_call(given_kernel, out_shape=[jax.ShapeDtypeStruct(shape, jnp.f...]
  transfers between devices with their start and end apart: 8 -> 9, of which waited for: 6 -> 5; matrix products, arithmetic and copies ran while one was open for 3% -> 3% of each run, Pallas kernels for 8% -> 11%
where the time goes in v3:
time: 32.8 us; the launch traced here: 32.7 us
  waiting for transfers between devices  12.6 us (38%)
  starting transfers between devices  9.79 us (30%)
  Pallas kernels  8.83 us (27%)
  other arithmetic  1.29 us (4%)
    ppermute x6, waiting for transfers between devices, shifted(): lax.ppermute(value, axis, [(i, (i + by) % size) for i in range(size)])  6.51 us
    ppermute x3, waiting for transfers between devices, across(): parts.append(lax.ppermute(value, axis, [(i, i ^ j) for i in range(size)]))  6.04 us
    ppermute x6, starting transfers between devices, shifted(): lax.ppermute(value, axis, [(i, (i + by) % size) for i in range(size)])  5.32 us
    ppermute x3, starting transfers between devices, across(): parts.append(lax.ppermute(value, axis, [(i, i ^ j) for i in range(size)]))  4.48 us
    pallas_call x1, Pallas kernels, given(): pl.pallas_call(given_kernel, out_shape=[jax.ShapeDtypeStruct(shape, jnp.f...  2.82 us
    pallas_call x1, Pallas kernels, loops(): pl.pallas_call(loops_kernel, out_shape=jax.ShapeDtypeStruct(shape, jnp.bf...  2.36 us
    pallas_call x1, Pallas kernels, halfway(): pl.pallas_call(halfway_kernel, out_shape=jax.ShapeDtypeStruct((pairs, lin...  1.95 us
    pallas_call x1, Pallas kernels, kept(): pl.pallas_call(kept_kernel, out_shape=jax.ShapeDtypeStruct(shape, jnp.flo...  1.32 us
  transfers between devices with their start and end apart: 9, of which 5 were waited for; matrix products, arithmetic and copies ran while one was open for 3% of the time, Pallas kernels for 11%

profile of v3, /device:TPU:0, one launch (start us, length us, event | category | flops | bytes accessed | tf_op | source)
XLA Modules:
  0.0 32.7 jit_solution(3459980857028910462)
XLA Ops:
  0.0 0.1 pad_add_fusion.place_hbm
  0.1 2.8 %given.1 = (f32[2,2,4,32,128]{4,3,2,1,0:T(8,128)S(1)}, f32[2,8,512]{2,1,0:T(8,128)S(1)}, bf16[2,3,4,128,128]{4,3,2,1,0:T(8,128)(2,1)S(1)}) custom-call(s32[2]{0:T(128)S(1)} %pad_add_fusion.place_hbm, s32[3,8]{1,0:T(4,128)} %bitcast.57, bf16[2,3,512,128]{3,2,1,0:T(8,128)(2,1)} %bitcast.56), custom_call_target="tpu_custom_call" | custom-call | tf_op jit(solution)/shard_map/given/pallas_call | solution.py:119
  2.9 0.0 copy-start
  2.9 0.6 %collective-permute-start = (f32[2,2,4,32,128]{4,3,2,1,0:T(8,128)S(1)}, f32[2,2,4,32,128]{4,3,2,1,0:T(8,128)S(1)}, u32[]{:S(2)}, u32[]{:S(2)}) collective-permute-start(f32[2,2,4,32,128]{4,3,2,1,0:T(8,128)S(1)} %get-tuple-element.10), channel_id=1, source_target_pairs={{0,1},{1,0},{2,3},{3,2},{4,5},{5,4},{6,7},{7,6},{8,9},{9,8},{10,11... | collective-permute-start | bytes 786440 | tf_op jit(solution)/shard_map/ppermute | solution.py:305
  3.5 0.9 %select_reduce_fusion = s32[4,2]{0,1:T(2,128)S(1)} fusion(s32[8]{0:T(128)} %param.8, s32[4,2]{0,1:T(2,128)} %param.7), kind=kLoop, calls=%fused_computation.15 | loop fusion | flops 184 | bytes 96 | tf_op jit(solution)/shard_map/reduce_sum | solution.py:338
  4.4 1.3 %kept.1 = f32[2,2,4,32,128]{4,3,2,1,0:T(8,128)S(1)} custom-call(s32[2]{0:T(128)S(1)} %pad_add_fusion.place_hbm, f32[2,8,512]{2,1,0:T(8,128)S(1)} %get-tuple-element.8.table_ref, bf16[2,3,4,128,128]{4,3,2,1,0:T(8,128)(2,1)S(1)} %get-tuple-element.9.turned_ref), custom_call_target="tpu_custom_call" | custom-call | tf_op jit(solution)/shard_map/kept/pallas_call | solution.py:155
  5.7 0.0 collective-permute-done
  5.8 2.6 %collective-permute-start.1 = (bf16[2,4,32,128]{3,2,1,0:T(8,128)(2,1)S(1)}, bf16[2,4,32,128]{3,2,1,0:T(8,128)(2,1)S(1)}, u32[]{:S(2)}, u32[]{:S(2)}) collective-permute-start(bf16[2,4,32,128]{3,2,1,0:T(8,128)(2,1)S(1)} %fusion.2), channel_id=1, source_target_pairs={{0,2},{2,0},{1,3},{3,1},{4,6},{6,4},{5,7},{7,5},{8,10},{10,8},{9,1... | collective-permute-start | bytes 196616 | tf_op jit(solution)/shard_map/ppermute | solution.py:305
  8.5 2.6 %collective-permute-done.1 = bf16[2,4,32,128]{3,2,1,0:T(8,128)(2,1)S(1)} collective-permute-done((bf16[2,4,32,128]{3,2,1,0:T(8,128)(2,1)S(1)}, bf16[2,4,32,128]{3,2,1,0:T(8,128)(2,1)S(1)}, u32[]{:S(2)}, u32[]{:S(2)}) %collective-permute-start.1) | collective-permute-done | bytes 65568 | tf_op jit(solution)/shard_map/ppermute | solution.py:305
  11.1 1.9 %collective-permute-start.4 = (bf16[2,4,32,128]{3,2,1,0:T(8,128)(2,1)S(1)}, bf16[2,4,32,128]{3,2,1,0:T(8,128)(2,1)S(1)}, u32[]{:S(2)}, u32[]{:S(2)}) collective-permute-start(bf16[2,4,32,128]{3,2,1,0:T(8,128)(2,1)S(1)} %fusion.1), channel_id=1, source_target_pairs={{0,4},{4,0},{8,12},{12,8},{1,5},{5,1},{9,13},{13,9},{2,6},{6,2},{1... | collective-permute-start | bytes 196616 | tf_op jit(solution)/shard_map/ppermute | solution.py:319
  13.0 2.6 %collective-permute-start.3 = (bf16[2,4,32,128]{3,2,1,0:T(8,128)(2,1)S(1)}, bf16[2,4,32,128]{3,2,1,0:T(8,128)(2,1)S(1)}, u32[]{:S(2)}, u32[]{:S(2)}) collective-permute-start(bf16[2,4,32,128]{3,2,1,0:T(8,128)(2,1)S(1)} %fusion.1), channel_id=1, source_target_pairs={{0,8},{4,12},{8,0},{12,4},{1,9},{5,13},{9,1},{13,5},{2,10},{6,14},... | collective-permute-start | bytes 196616 | tf_op jit(solution)/shard_map/ppermute | solution.py:319
  15.6 0.0 collective-permute-start.2
  15.6 0.0 collective-permute-done.4
  15.6 4.4 %collective-permute-done.3 = bf16[2,4,32,128]{3,2,1,0:T(8,128)(2,1)S(1)} collective-permute-done((bf16[2,4,32,128]{3,2,1,0:T(8,128)(2,1)S(1)}, bf16[2,4,32,128]{3,2,1,0:T(8,128)(2,1)S(1)}, u32[]{:S(2)}, u32[]{:S(2)}) %collective-permute-start.3) | collective-permute-done | bytes 65568 | tf_op jit(solution)/shard_map/ppermute | solution.py:319
  20.0 1.7 %collective-permute-done.2 = bf16[2,4,32,128]{3,2,1,0:T(8,128)(2,1)S(1)} collective-permute-done((bf16[2,4,32,128]{3,2,1,0:T(8,128)(2,1)S(1)}, bf16[2,4,32,128]{3,2,1,0:T(8,128)(2,1)S(1)}, u32[]{:S(2)}, u32[]{:S(2)}) %collective-permute-start.2) | collective-permute-done | bytes 65568 | tf_op jit(solution)/shard_map/ppermute | solution.py:319
  21.7 0.1 select_select_fusion.rest_0_
  21.8 1.6 %collective-permute-start.6 = (bf16[4,4,32,128]{3,2,1,0:T(8,128)(2,1)S(1)}, bf16[4,4,32,128]{3,2,1,0:T(8,128)(2,1)S(1)}, u32[]{:S(2)}, u32[]{:S(2)}) collective-permute-start(bf16[4,4,32,128]{3,2,1,0:T(8,128)(2,1)S(1)} %select_select_fusion.rest_0_), channel_id=1, source_target_pairs={{0,2},{2,0},{1,3},{3,1},{4,6},{6,4},{5,7},{7,5},{8,10},{10,8},{9,1... | collective-permute-start | bytes 393224 | tf_op jit(solution)/shard_map/ppermute | solution.py:305
  23.4 0.0 collective-permute-start.7
  23.4 0.1 select_select_fusion.1
  23.5 3.4 %collective-permute-done.6.rest_1_ = bf16[4,4,32,128]{3,2,1,0:T(8,128)(2,1)S(1)} collective-permute-done((bf16[4,4,32,128]{3,2,1,0:T(8,128)(2,1)S(1)}, bf16[4,4,32,128]{3,2,1,0:T(8,128)(2,1)S(1)}, u32[]{:S(2)}, u32[]{:S(2)}) %collective-permute-start.6) | collective-permute-done | bytes 131104 | tf_op jit(solution)/shard_map/ppermute | solution.py:305
  26.8 0.0 collective-permute-start.8
  26.9 0.6 %collective-permute-start.5 = (bf16[4,4,16,128]{3,2,1,0:T(8,128)(2,1)S(1)}, bf16[4,4,16,128]{3,2,1,0:T(8,128)(2,1)S(1)}, u32[]{:S(2)}, u32[]{:S(2)}) collective-permute-start(bf16[4,4,16,128]{3,2,1,0:T(8,128)(2,1)S(1)} %get-tuple-element.11), channel_id=1, source_target_pairs={{0,1},{1,0},{2,3},{3,2},{4,5},{5,4},{6,7},{7,6},{8,9},{9,8},{10,11... | collective-permute-start | bytes 196616 | tf_op jit(solution)/shard_map/ppermute | solution.py:305
  27.4 0.0 copy-done
  27.4 0.4 %doubled.1.right_ref = bf16[4,128,2048]{2,1,0:T(8,128)(2,1)S(1)} custom-call(bf16[4,64,2048]{2,1,0:T(8,128)(2,1)S(1)} %copy-done), custom_call_target="tpu_custom_call" | custom-call | tf_op jit(solution)/shard_map/doubled/pallas_call | solution.py:183
  27.8 0.5 %collective-permute-done.5.rest_1_ = bf16[4,4,16,128]{3,2,1,0:T(8,128)(2,1)S(1)} collective-permute-done((bf16[4,4,16,128]{3,2,1,0:T(8,128)(2,1)S(1)}, bf16[4,4,16,128]{3,2,1,0:T(8,128)(2,1)S(1)}, u32[]{:S(2)}, u32[]{:S(2)}) %collective-permute-start.5) | collective-permute-done | bytes 65568 | tf_op jit(solution)/shard_map/ppermute | solution.py:305
  28.3 1.9 %halfway.1.half_ref = bf16[4,2048,128]{2,1,0:T(8,128)(2,1)S(1)} custom-call(bf16[4,128,2048]{2,1,0:T(8,128)(2,1)S(1)} %doubled.1.right_ref, bf16[4,4,16,128]{3,2,1,0:T(8,128)(2,1)S(1)} %get-tuple-element.12.rest_0_, bf16[4,4,16,128]{3,2,1,0:T(8,128)(2,1)S(1)} %collective-permute-done.5.rest_1_), custom_call_target="tpu_custom_call" | custom-call | tf_op jit(solution)/shard_map/halfway/pallas_call | solution.py:212
  30.3 0.0 collective-permute-done.7.rest_2_
  30.3 0.0 collective-permute-done.8.rest_3_
  30.3 2.4 %loops.1 = bf16[4,8,16,16,128]{4,3,2,1,0:T(8,128)(2,1)} custom-call(s32[2]{0:T(128)S(1)} %pad_add_fusion.place_hbm, bf16[4,2048,128]{2,1,0:T(8,128)(2,1)S(1)} %halfway.1.half_ref, bf16[4,4,32,128]{3,2,1,0:T(8,128)(2,1)S(1)} %select_select_fusion.rest_0_, bf16[4,4,32,128]{3,2,1,0:T(8,128)(2,1)S(1)} %collective-permute-done.6.rest_1_, ...), custom_call_target="tpu_custom_call" | custom-call | tf_op jit(solution)/shard_map/loops/pallas_call | solution.py:287
  (10 shorter events, 0.1 us)
Async XLA Ops:
  2.9 24.5 %copy-start = (bf16[4,64,2048]{2,1,0:T(8,128)(2,1)S(1)}, bf16[4,64,2048]{2,1,0:T(8,128)(2,1)}, u32[]{:S(2)}) copy-start(bf16[4,64,2048]{2,1,0:T(8,128)(2,1)} %tau_ref.1) | copy-start | bytes 3145732
  2.9 2.8 %collective-permute-start = (f32[2,2,4,32,128]{4,3,2,1,0:T(8,128)S(1)}, f32[2,2,4,32,128]{4,3,2,1,0:T(8,128)S(1)}, u32[]{:S(2)}, u32[]{:S(2)}) collective-permute-start(f32[2,2,4,32,128]{4,3,2,1,0:T(8,128)S(1)} %get-tuple-element.10), channel_id=1, source_target_pairs={{0,1},{1,0},{2,3},{3,2},{4,5},{5,4},{6,7},{7,6},{8,9},{9,8},{10,11... | collective-permute-start | bytes 786440 | tf_op jit(solution)/shard_map/ppermute | solution.py:305
  5.8 5.3 %collective-permute-start.1 = (bf16[2,4,32,128]{3,2,1,0:T(8,128)(2,1)S(1)}, bf16[2,4,32,128]{3,2,1,0:T(8,128)(2,1)S(1)}, u32[]{:S(2)}, u32[]{:S(2)}) collective-permute-start(bf16[2,4,32,128]{3,2,1,0:T(8,128)(2,1)S(1)} %fusion.2), channel_id=1, source_target_pairs={{0,2},{2,0},{1,3},{3,1},{4,6},{6,4},{5,7},{7,5},{8,10},{10,8},{9,1... | collective-permute-start | bytes 196616 | tf_op jit(solution)/shard_map/ppermute | solution.py:305
  11.1 4.5 %collective-permute-start.4 = (bf16[2,4,32,128]{3,2,1,0:T(8,128)(2,1)S(1)}, bf16[2,4,32,128]{3,2,1,0:T(8,128)(2,1)S(1)}, u32[]{:S(2)}, u32[]{:S(2)}) collective-permute-start(bf16[2,4,32,128]{3,2,1,0:T(8,128)(2,1)S(1)} %fusion.1), channel_id=1, source_target_pairs={{0,4},{4,0},{8,12},{12,8},{1,5},{5,1},{9,13},{13,9},{2,6},{6,2},{1... | collective-permute-start | bytes 196616 | tf_op jit(solution)/shard_map/ppermute | solution.py:319
  13.0 7.0 %collective-permute-start.3 = (bf16[2,4,32,128]{3,2,1,0:T(8,128)(2,1)S(1)}, bf16[2,4,32,128]{3,2,1,0:T(8,128)(2,1)S(1)}, u32[]{:S(2)}, u32[]{:S(2)}) collective-permute-start(bf16[2,4,32,128]{3,2,1,0:T(8,128)(2,1)S(1)} %fusion.1), channel_id=1, source_target_pairs={{0,8},{4,12},{8,0},{12,4},{1,9},{5,13},{9,1},{13,5},{2,10},{6,14},... | collective-permute-start | bytes 196616 | tf_op jit(solution)/shard_map/ppermute | solution.py:319
  15.6 6.1 %collective-permute-start.2 = (bf16[2,4,32,128]{3,2,1,0:T(8,128)(2,1)S(1)}, bf16[2,4,32,128]{3,2,1,0:T(8,128)(2,1)S(1)}, u32[]{:S(2)}, u32[]{:S(2)}) collective-permute-start(bf16[2,4,32,128]{3,2,1,0:T(8,128)(2,1)S(1)} %fusion.1), channel_id=1, source_target_pairs={{0,12},{4,8},{8,4},{12,0},{1,13},{5,9},{9,5},{13,1},{2,14},{6,10},... | collective-permute-start | bytes 196616 | tf_op jit(solution)/shard_map/ppermute | solution.py:319
  21.8 5.0 %collective-permute-start.6 = (bf16[4,4,32,128]{3,2,1,0:T(8,128)(2,1)S(1)}, bf16[4,4,32,128]{3,2,1,0:T(8,128)(2,1)S(1)}, u32[]{:S(2)}, u32[]{:S(2)}) collective-permute-start(bf16[4,4,32,128]{3,2,1,0:T(8,128)(2,1)S(1)} %select_select_fusion.rest_0_), channel_id=1, source_target_pairs={{0,2},{2,0},{1,3},{3,1},{4,6},{6,4},{5,7},{7,5},{8,10},{10,8},{9,1... | collective-permute-start | bytes 393224 | tf_op jit(solution)/shard_map/ppermute | solution.py:305
  23.4 6.9 %collective-permute-start.7 = (bf16[4,4,32,128]{3,2,1,0:T(8,128)(2,1)S(1)}, bf16[4,4,32,128]{3,2,1,0:T(8,128)(2,1)S(1)}, u32[]{:S(2)}, u32[]{:S(2)}) collective-permute-start(bf16[4,4,32,128]{3,2,1,0:T(8,128)(2,1)S(1)} %select_select_fusion.rest_0_), channel_id=1, source_target_pairs={{0,1},{1,0},{2,3},{3,2},{4,5},{5,4},{6,7},{7,6},{8,9},{9,8},{10,11... | collective-permute-start | bytes 393224 | tf_op jit(solution)/shard_map/ppermute | solution.py:305
  26.8 3.5 %collective-permute-start.8 = (bf16[4,4,32,128]{3,2,1,0:T(8,128)(2,1)S(1)}, bf16[4,4,32,128]{3,2,1,0:T(8,128)(2,1)S(1)}, u32[]{:S(2)}, u32[]{:S(2)}) collective-permute-start(bf16[4,4,32,128]{3,2,1,0:T(8,128)(2,1)S(1)} %collective-permute-done.6.rest_1_), channel_id=1, source_target_pairs={{0,1},{1,0},{2,3},{3,2},{4,5},{5,4},{6,7},{7,6},{8,9},{9,8},{10,11... | collective-permute-start | bytes 393224 | tf_op jit(solution)/shard_map/ppermute | solution.py:305
  26.9 1.5 %collective-permute-start.5 = (bf16[4,4,16,128]{3,2,1,0:T(8,128)(2,1)S(1)}, bf16[4,4,16,128]{3,2,1,0:T(8,128)(2,1)S(1)}, u32[]{:S(2)}, u32[]{:S(2)}) collective-permute-start(bf16[4,4,16,128]{3,2,1,0:T(8,128)(2,1)S(1)} %get-tuple-element.11), channel_id=1, source_target_pairs={{0,1},{1,0},{2,3},{3,2},{4,5},{5,4},{6,7},{7,6},{8,9},{9,8},{10,11... | collective-permute-start | bytes 196616 | tf_op jit(solution)/shard_map/ppermute | solution.py:305

commit v4 on v3

--- a/solution.py
+++ b/solution.py
@@ -1,3 +1,5 @@
+import functools
+
 import jax
 import jax.numpy as jnp
 from jax import lax
@@ -220,34 +222,37 @@
     )(right, *sinks)
 
 
-def loops_kernel(place_hbm, half_ref, *rest):
-    sources = rest[:-5]
-    out_hbm, place_ref, full_ref, stage_ref, sems = rest[-5:]
+def loops_kernel(place_hbm, space_ref, half_ref, *rest, spaces):
+    sources = rest[:-4]
+    out_hbm, place_ref, stage_ref, sems = rest[-4:]
     pairs, moms, rows, spinors, width = stage_ref.shape
-    _, _, spaces, _, _ = full_ref.shape
     spins = len(sources) // spaces
     part = moms // spins
-    vectors = width // 2
+    block = sources[0].shape[2]
     count = rows * spinors
-    place_copy = pltpu.make_async_copy(place_hbm, place_ref, sems.at[pairs * moms // 2])
+    place_copy = pltpu.make_async_copy(place_hbm, place_ref, sems.at[1])
     place_copy.start()
-    place_copy.wait()
-    space = place_ref[0]
-    spin = place_ref[1]
-    for i in range(spins):
-        for j in range(spaces):
-            full_ref[:, i * part : (i + 1) * part, lax.rem(space + spaces - j, spaces)] = sources[
-                i * spaces + j
-            ][...]
-    copies = []
+    here = [
+        jnp.broadcast_to(space_ref[...], (block, width)) == space for space in range(spaces)
+    ]
     zeros = jnp.zeros((width, width), jnp.bfloat16)
     for k in range(pairs):
         for m in range(0, moms, 2):
             rights = []
             for i in range(2):
-                source = full_ref[k, m + i].reshape(vectors, width)
-                turned = swapped(source, -1.0, 1.0).astype(jnp.bfloat16)
-                rights.append(jnp.concatenate([source, turned], axis=0))
+                given_blocks = [
+                    sources[(m + i) // part * spaces + j][k, (m + i) % part].astype(jnp.float32)
+                    for j in range(spaces)
+                ]
+                ordered = []
+                for r in range(spaces):
+                    value = given_blocks[0]
+                    for j in range(1, spaces):
+                        value = jnp.where(here[(r + j) % spaces], given_blocks[j], value)
+                    ordered.append(value)
+                source = jnp.concatenate(ordered, axis=0)
+                turned = swapped(source, -1.0, 1.0)
+                rights.append(jnp.concatenate([source, turned], axis=0).astype(jnp.bfloat16))
             right = jnp.concatenate(
                 [
                     jnp.concatenate([rights[0], zeros], axis=1),
@@ -265,39 +270,38 @@
                 stage_ref[k, m + i] = product[:, i * width : (i + 1) * width].reshape(
                     rows, spinors, width
                 )
-            first = lax.rem(spin + spins - m // part, spins) * part + m % part
-            copies.append(
+            if k == 0 and m == 0:
+                place_copy.wait()
+                spin = place_ref[1]
+            if (m + 2) % part == 0:
+                owner = lax.rem(spin + spins - m // part, spins)
                 pltpu.make_async_copy(
-                    stage_ref.at[k, pl.ds(m, 2)],
-                    out_hbm.at[k, pl.ds(first, 2)],
-                    sems.at[k * moms // 2 + m // 2],
-                )
-            )
-            copies[-1].start()
-    for copy in copies:
-        copy.wait()
-
-
-def loops(place, half, sources):
+                    stage_ref.at[k, pl.ds(m + 2 - part, part)],
+                    out_hbm.at[k, pl.ds(owner * part, part)],
+                    sems.at[0],
+                ).start()
+    pltpu.make_async_copy(stage_ref, out_hbm, sems.at[0]).wait()
+
+
+def loops(place, space_row, half, sources):
     pairs, lines, width = half.shape
     spins, spaces = len(sources), len(sources[0])
-    _, part, block, _ = sources[0][0].shape
+    _, part, _, _ = sources[0][0].shape
     moms = spins * part
     shape = (pairs, moms, lines // (moms * SPINS), SPINS, width)
     return pl.pallas_call(
-        loops_kernel,
+        functools.partial(loops_kernel, spaces=spaces),
         out_shape=jax.ShapeDtypeStruct(shape, jnp.bfloat16),
-        in_specs=[ANY, VMEM] + [VMEM] * (spaces * spins),
+        in_specs=[ANY, VMEM, VMEM] + [VMEM] * (spaces * spins),
         out_specs=HBM,
         scratch_shapes=[
             pltpu.SMEM(place.shape, jnp.int32),
-            pltpu.VMEM((pairs, moms, spaces, block, width), jnp.bfloat16),
             pltpu.VMEM(shape, jnp.bfloat16),
-            pltpu.SemaphoreType.DMA((pairs * moms // 2 + 1,)),
+            pltpu.SemaphoreType.DMA((2,)),
         ],
         compiler_params=params(16),
         name="loops",
-    )(place, half, *[block for group in sources for block in group])
+    )(place, space_row, half, *[block for group in sources for block in group])
 
 
 def shifted(value, axis, by):
@@ -312,12 +316,25 @@
     return parts
 
 
-def across(value, axis):
-    size = lax.axis_size(axis)
+def targets(size):
+    ring = [0, *range(1, size, 2), *reversed(range(2, size, 2))]
+    place = {member: n for n, member in enumerate(ring)}
+    return [[ring[(place[i] + j) % size] for i in range(size)] for j in range(1, size)]
+
+
+def exchanged(value, axis):
     parts = [value]
-    for j in range(1, size):
-        parts.append(lax.ppermute(value, axis, [(i, i ^ j) for i in range(size)]))
+    for to in targets(lax.axis_size(axis)):
+        parts.append(lax.ppermute(value, axis, list(enumerate(to))))
     return parts
+
+
+def arrivals(size):
+    table = [[0] * size for _ in range(size)]
+    for n, to in enumerate(targets(size)):
+        for sender, receiver in enumerate(to):
+            table[receiver][sender] = n + 1
+    return table
 
 
 def selected(index, candidates):
@@ -336,7 +353,13 @@
     times = slot_map.shape[0]
     named = time_pairs[:, :, None] == lax.iota(jnp.int32, times)
     slot = jnp.sum(jnp.where(named, slot_map, 0), axis=-1)
-    index = (lax.axis_index("tm") ^ slot // slots) * slots + slot % slots
+    members = lax.axis_size("tm")
+    table = jnp.array(arrivals(members), jnp.int32)
+    row = jnp.sum(
+        jnp.where((lax.iota(jnp.int32, members) == lax.axis_index("tm"))[:, None], table, 0), 0
+    )
+    held = (slot // slots)[..., None] == lax.iota(jnp.int32, members)
+    index = jnp.sum(jnp.where(held, row, 0), axis=-1) * slots + slot % slots
 
     spin = lax.axis_index("spin")
     x = jnp.transpose(eigenvectors, (0, 2, 1, 3))
@@ -349,7 +372,7 @@
         value = shifted(total[j].astype(jnp.bfloat16), "space", j)
         row_share = row_share + value.astype(jnp.float32)
     row_share = row_share.astype(jnp.bfloat16)
-    arrived = across(row_share, "tm")
+    arrived = exchanged(row_share, "tm")
     candidates = [value[s] for value in arrived for s in range(slots)]
     source_share = selected(index[:, 1], candidates)
     sink_share = selected(index[:, 0], candidates)
@@ -365,7 +388,8 @@
     far = around(source_share, "space")
     near = [around(value, "spin") for value in far]
     sources = [[group[i] for group in near] for i in range(spins)]
-    return loops(place, half, sources)
+    space_row = jnp.full((1, perambulators.shape[1] * 2), lax.axis_index("space"), jnp.int32)
+    return loops(place, space_row, half, sources)
 
 
 def solution(mesh):
@@ -377,9 +401,6 @@
         P(("cfg", "tm"), None, None),
     )
 
-    members = mesh.shape["tm"]
-    order = [j for j in range(1, members) if j & (j + 1) == 0][::-1]
-    order += [j for j in range(1, members) if j not in order]
     return jax.shard_map(
         per_device,
         mesh=mesh,

time: 32.8 us -> 32.1 us (0.979)
  waiting for transfers between devices: 12.6 us -> 9.52 us
  starting transfers between devices: 9.79 us -> 11.3 us
  other arithmetic: 1.29 us -> 2.28 us
    ppermute x3, waiting for transfers between devices: 6.04 us -> 3.03 us  [exchanged(): parts.append(lax.ppermute(value, axis, list(enumerate(to))))]
    ppermute x3, starting transfers between devices: 4.48 us -> 5.93 us  [exchanged(): parts.append(lax.ppermute(value, axis, list(enumerate(to))))]
    reduce_sum x0 -> x2, other arithmetic: none -> 0.98 us  [the longest x1 0.77 us: per_device(): jnp.sum(jnp.where((lax.iota(jnp.int32, members) == lax.axis_index('tm'))[...]
  transfers between devices with their start and end apart: 9 -> 9, of which waited for: 5 -> 5; matrix products, arithmetic and copies ran while one was open for 3% -> 6% of each run, Pallas kernels for 11% -> 11%
where the time goes in v4:
time: 32.1 us; the launch traced here: 32 us
  starting transfers between devices  11.3 us (35%)
  waiting for transfers between devices  9.52 us (30%)
  Pallas kernels  8.67 us (27%)
  other arithmetic  2.28 us (7%)
    ppermute x6, waiting for transfers between devices, shifted(): lax.ppermute(value, axis, [(i, (i + by) % size) for i in range(size)])  6.49 us
    ppermute x3, starting transfers between devices, exchanged(): parts.append(lax.ppermute(value, axis, list(enumerate(to))))  5.93 us
    ppermute x6, starting transfers between devices, shifted(): lax.ppermute(value, axis, [(i, (i + by) % size) for i in range(size)])  5.33 us
    ppermute x3, waiting for transfers between devices, exchanged(): parts.append(lax.ppermute(value, axis, list(enumerate(to))))  3.03 us
    pallas_call x1, Pallas kernels, given(): pl.pallas_call(given_kernel, out_shape=[jax.ShapeDtypeStruct(shape, jnp.f...  2.82 us
    pallas_call x1, Pallas kernels, loops(): pl.pallas_call(functools.partial(loops_kernel, spaces=spaces), out_shape=...  2.19 us
    pallas_call x1, Pallas kernels, halfway(): pl.pallas_call(halfway_kernel, out_shape=jax.ShapeDtypeStruct((pairs, lin...  1.95 us
    pallas_call x1, Pallas kernels, kept(): pl.pallas_call(kept_kernel, out_shape=jax.ShapeDtypeStruct(shape, jnp.flo...  1.33 us
  transfers between devices with their start and end apart: 9, of which 5 were waited for; matrix products, arithmetic and copies ran while one was open for 6% of the time, Pallas kernels for 11%

profile of v4, /device:TPU:0, one launch (start us, length us, event | category | flops | bytes accessed | tf_op | source)
XLA Modules:
  0.0 32.0 jit_solution(6174027657925133155)
XLA Ops:
  0.0 0.1 pad_add_fusion.place_hbm
  0.1 2.8 %given.1 = (f32[2,2,4,32,128]{4,3,2,1,0:T(8,128)S(1)}, f32[2,8,512]{2,1,0:T(8,128)S(1)}, bf16[2,3,4,128,128]{4,3,2,1,0:T(8,128)(2,1)S(1)}) custom-call(s32[2]{0:T(128)S(1)} %pad_add_fusion.place_hbm, s32[3,8]{1,0:T(4,128)} %bitcast.57, bf16[2,3,512,128]{3,2,1,0:T(8,128)(2,1)} %bitcast.56), custom_call_target="tpu_custom_call" | custom-call | tf_op jit(solution)/shard_map/given/pallas_call | solution.py:121
  2.9 0.0 copy-start
  2.9 0.6 %collective-permute-start = (f32[2,2,4,32,128]{4,3,2,1,0:T(8,128)S(1)}, f32[2,2,4,32,128]{4,3,2,1,0:T(8,128)S(1)}, u32[]{:S(2)}, u32[]{:S(2)}) collective-permute-start(f32[2,2,4,32,128]{4,3,2,1,0:T(8,128)S(1)} %get-tuple-element.10), channel_id=1, source_target_pairs={{0,1},{1,0},{2,3},{3,2},{4,5},{5,4},{6,7},{7,6},{8,9},{9,8},{10,11... | collective-permute-start | bytes 786440 | tf_op jit(solution)/shard_map/ppermute | solution.py:309
  3.5 0.9 %select_reduce_fusion.1 = s32[4,2]{0,1:T(2,128)S(1)} fusion(s32[8]{0:T(128)} %param.9, s32[4,2]{0,1:T(2,128)} %param.8), kind=kLoop, calls=%fused_computation.17 | loop fusion | flops 184 | bytes 96 | tf_op jit(solution)/shard_map/reduce_sum | solution.py:355
  4.4 0.8 %select_reduce_fusion.2 = s32[4]{0:T(128)S(1)} fusion(s32[4,4]{1,0:T(4,128)} %constant.68.clone, pred[4]{0:T(512)(128)(4,1)S(1)} %iota_compare_fusion.2), kind=kLoop, calls=%fused_computation.19 | loop fusion | flops 28 | bytes 84 | tf_op jit(solution)/shard_map/reduce_sum | solution.py:358
  5.2 0.2 select_reduce_fusion
  5.4 1.3 %kept.1 = f32[2,2,4,32,128]{4,3,2,1,0:T(8,128)S(1)} custom-call(s32[2]{0:T(128)S(1)} %pad_add_fusion.place_hbm, f32[2,8,512]{2,1,0:T(8,128)S(1)} %get-tuple-element.8.table_ref, bf16[2,3,4,128,128]{4,3,2,1,0:T(8,128)(2,1)S(1)} %get-tuple-element.9.turned_ref), custom_call_target="tpu_custom_call" | custom-call | tf_op jit(solution)/shard_map/kept/pallas_call | solution.py:157
  6.7 0.0 collective-permute-done
  6.8 2.6 %collective-permute-start.1 = (bf16[2,4,32,128]{3,2,1,0:T(8,128)(2,1)S(1)}, bf16[2,4,32,128]{3,2,1,0:T(8,128)(2,1)S(1)}, u32[]{:S(2)}, u32[]{:S(2)}) collective-permute-start(bf16[2,4,32,128]{3,2,1,0:T(8,128)(2,1)S(1)} %fusion.2), channel_id=1, source_target_pairs={{0,2},{2,0},{1,3},{3,1},{4,6},{6,4},{5,7},{7,5},{8,10},{10,8},{9,1... | collective-permute-start | bytes 196616 | tf_op jit(solution)/shard_map/ppermute | solution.py:309
  9.5 2.6 %collective-permute-done.1 = bf16[2,4,32,128]{3,2,1,0:T(8,128)(2,1)S(1)} collective-permute-done((bf16[2,4,32,128]{3,2,1,0:T(8,128)(2,1)S(1)}, bf16[2,4,32,128]{3,2,1,0:T(8,128)(2,1)S(1)}, u32[]{:S(2)}, u32[]{:S(2)}) %collective-permute-start.1) | collective-permute-done | bytes 65568 | tf_op jit(solution)/shard_map/ppermute | solution.py:309
  12.1 1.9 %collective-permute-start.4 = (bf16[2,4,32,128]{3,2,1,0:T(8,128)(2,1)S(1)}, bf16[2,4,32,128]{3,2,1,0:T(8,128)(2,1)S(1)}, u32[]{:S(2)}, u32[]{:S(2)}) collective-permute-start(bf16[2,4,32,128]{3,2,1,0:T(8,128)(2,1)S(1)} %fusion.1), channel_id=1, source_target_pairs={{0,4},{4,12},{8,0},{12,8},{1,5},{5,13},{9,1},{13,9},{2,6},{6,14},{... | collective-permute-start | bytes 196616 | tf_op jit(solution)/shard_map/ppermute | solution.py:328
  14.0 2.5 %collective-permute-start.3 = (bf16[2,4,32,128]{3,2,1,0:T(8,128)(2,1)S(1)}, bf16[2,4,32,128]{3,2,1,0:T(8,128)(2,1)S(1)}, u32[]{:S(2)}, u32[]{:S(2)}) collective-permute-start(bf16[2,4,32,128]{3,2,1,0:T(8,128)(2,1)S(1)} %fusion.1), channel_id=1, source_target_pairs={{0,12},{4,8},{8,4},{12,0},{1,13},{5,9},{9,5},{13,1},{2,14},{6,10},... | collective-permute-start | bytes 196616 | tf_op jit(solution)/shard_map/ppermute | solution.py:328
  16.5 1.6 %collective-permute-start.2 = (bf16[2,4,32,128]{3,2,1,0:T(8,128)(2,1)S(1)}, bf16[2,4,32,128]{3,2,1,0:T(8,128)(2,1)S(1)}, u32[]{:S(2)}, u32[]{:S(2)}) collective-permute-start(bf16[2,4,32,128]{3,2,1,0:T(8,128)(2,1)S(1)} %fusion.1), channel_id=1, source_target_pairs={{0,8},{4,0},{8,12},{12,4},{1,9},{5,1},{9,13},{13,5},{2,10},{6,2},{... | collective-permute-start | bytes 196616 | tf_op jit(solution)/shard_map/ppermute | solution.py:328
  18.1 0.0 collective-permute-done.4
  18.1 2.5 %collective-permute-done.3 = bf16[2,4,32,128]{3,2,1,0:T(8,128)(2,1)S(1)} collective-permute-done((bf16[2,4,32,128]{3,2,1,0:T(8,128)(2,1)S(1)}, bf16[2,4,32,128]{3,2,1,0:T(8,128)(2,1)S(1)}, u32[]{:S(2)}, u32[]{:S(2)}) %collective-permute-start.3) | collective-permute-done | bytes 65568 | tf_op jit(solution)/shard_map/ppermute | solution.py:328
  20.6 0.5 %collective-permute-done.2 = bf16[2,4,32,128]{3,2,1,0:T(8,128)(2,1)S(1)} collective-permute-done((bf16[2,4,32,128]{3,2,1,0:T(8,128)(2,1)S(1)}, bf16[2,4,32,128]{3,2,1,0:T(8,128)(2,1)S(1)}, u32[]{:S(2)}, u32[]{:S(2)}) %collective-permute-start.2) | collective-permute-done | bytes 65568 | tf_op jit(solution)/shard_map/ppermute | solution.py:328
  21.1 0.1 select_select_fusion.rest_0_
  21.3 1.6 %collective-permute-start.6 = (bf16[4,4,32,128]{3,2,1,0:T(8,128)(2,1)S(1)}, bf16[4,4,32,128]{3,2,1,0:T(8,128)(2,1)S(1)}, u32[]{:S(2)}, u32[]{:S(2)}) collective-permute-start(bf16[4,4,32,128]{3,2,1,0:T(8,128)(2,1)S(1)} %select_select_fusion.rest_0_), channel_id=1, source_target_pairs={{0,2},{2,0},{1,3},{3,1},{4,6},{6,4},{5,7},{7,5},{8,10},{10,8},{9,1... | collective-permute-start | bytes 393224 | tf_op jit(solution)/shard_map/ppermute | solution.py:309
  22.8 0.0 collective-permute-start.7
  22.8 0.1 select_select_fusion.1
  22.9 3.3 %collective-permute-done.6.rest_1_ = bf16[4,4,32,128]{3,2,1,0:T(8,128)(2,1)S(1)} collective-permute-done((bf16[4,4,32,128]{3,2,1,0:T(8,128)(2,1)S(1)}, bf16[4,4,32,128]{3,2,1,0:T(8,128)(2,1)S(1)}, u32[]{:S(2)}, u32[]{:S(2)}) %collective-permute-start.6) | collective-permute-done | bytes 131104 | tf_op jit(solution)/shard_map/ppermute | solution.py:309
  26.3 0.0 collective-permute-start.8
  26.3 0.6 %collective-permute-start.5 = (bf16[4,4,16,128]{3,2,1,0:T(8,128)(2,1)S(1)}, bf16[4,4,16,128]{3,2,1,0:T(8,128)(2,1)S(1)}, u32[]{:S(2)}, u32[]{:S(2)}) collective-permute-start(bf16[4,4,16,128]{3,2,1,0:T(8,128)(2,1)S(1)} %get-tuple-element.11), channel_id=1, source_target_pairs={{0,1},{1,0},{2,3},{3,2},{4,5},{5,4},{6,7},{7,6},{8,9},{9,8},{10,11... | collective-permute-start | bytes 196616 | tf_op jit(solution)/shard_map/ppermute | solution.py:309
  26.9 0.0 copy-done
  26.9 0.4 %doubled.1.right_ref = bf16[4,128,2048]{2,1,0:T(8,128)(2,1)S(1)} custom-call(bf16[4,64,2048]{2,1,0:T(8,128)(2,1)S(1)} %copy-done), custom_call_target="tpu_custom_call" | custom-call | tf_op jit(solution)/shard_map/doubled/pallas_call | solution.py:185
  27.3 0.5 %collective-permute-done.5.rest_1_ = bf16[4,4,16,128]{3,2,1,0:T(8,128)(2,1)S(1)} collective-permute-done((bf16[4,4,16,128]{3,2,1,0:T(8,128)(2,1)S(1)}, bf16[4,4,16,128]{3,2,1,0:T(8,128)(2,1)S(1)}, u32[]{:S(2)}, u32[]{:S(2)}) %collective-permute-start.5) | collective-permute-done | bytes 65568 | tf_op jit(solution)/shard_map/ppermute | solution.py:309
  27.8 1.9 %halfway.1.half_ref = bf16[4,2048,128]{2,1,0:T(8,128)(2,1)S(1)} custom-call(bf16[4,128,2048]{2,1,0:T(8,128)(2,1)S(1)} %doubled.1.right_ref, bf16[4,4,16,128]{3,2,1,0:T(8,128)(2,1)S(1)} %get-tuple-element.12.rest_0_, bf16[4,4,16,128]{3,2,1,0:T(8,128)(2,1)S(1)} %collective-permute-done.5.rest_1_), custom_call_target="tpu_custom_call" | custom-call | tf_op jit(solution)/shard_map/halfway/pallas_call | solution.py:214
  29.7 0.0 collective-permute-done.7.rest_2_
  29.7 0.0 collective-permute-done.8.rest_3_
  29.8 2.2 %loops.1 = bf16[4,8,16,16,128]{4,3,2,1,0:T(8,128)(2,1)} custom-call(s32[2]{0:T(128)S(1)} %pad_add_fusion.place_hbm, s32[1,128]{1,0:T(1,128)S(1)} %broadcast_in_dim.142.space_ref, bf16[4,2048,128]{2,1,0:T(8,128)(2,1)S(1)} %halfway.1.half_ref, bf16[4,4,32,128]{3,2,1,0:T(8,128)(2,1)S(1)} %select_select_fusion.rest_0_, ...), custom_call_target="tpu_custom_call" | custom-call | tf_op jit(solution)/shard_map/loops/pallas_call | solution.py:292
  (13 shorter events, 0.1 us)
Async XLA Ops:
  2.9 24.0 %copy-start = (bf16[4,64,2048]{2,1,0:T(8,128)(2,1)S(1)}, bf16[4,64,2048]{2,1,0:T(8,128)(2,1)}, u32[]{:S(2)}) copy-start(bf16[4,64,2048]{2,1,0:T(8,128)(2,1)} %tau_ref.1) | copy-start | bytes 3145732
  2.9 3.8 %collective-permute-start = (f32[2,2,4,32,128]{4,3,2,1,0:T(8,128)S(1)}, f32[2,2,4,32,128]{4,3,2,1,0:T(8,128)S(1)}, u32[]{:S(2)}, u32[]{:S(2)}) collective-permute-start(f32[2,2,4,32,128]{4,3,2,1,0:T(8,128)S(1)} %get-tuple-element.10), channel_id=1, source_target_pairs={{0,1},{1,0},{2,3},{3,2},{4,5},{5,4},{6,7},{7,6},{8,9},{9,8},{10,11... | collective-permute-start | bytes 786440 | tf_op jit(solution)/shard_map/ppermute | solution.py:309
  6.8 5.3 %collective-permute-start.1 = (bf16[2,4,32,128]{3,2,1,0:T(8,128)(2,1)S(1)}, bf16[2,4,32,128]{3,2,1,0:T(8,128)(2,1)S(1)}, u32[]{:S(2)}, u32[]{:S(2)}) collective-permute-start(bf16[2,4,32,128]{3,2,1,0:T(8,128)(2,1)S(1)} %fusion.2), channel_id=1, source_target_pairs={{0,2},{2,0},{1,3},{3,1},{4,6},{6,4},{5,7},{7,5},{8,10},{10,8},{9,1... | collective-permute-start | bytes 196616 | tf_op jit(solution)/shard_map/ppermute | solution.py:309
  12.1 5.9 %collective-permute-start.4 = (bf16[2,4,32,128]{3,2,1,0:T(8,128)(2,1)S(1)}, bf16[2,4,32,128]{3,2,1,0:T(8,128)(2,1)S(1)}, u32[]{:S(2)}, u32[]{:S(2)}) collective-permute-start(bf16[2,4,32,128]{3,2,1,0:T(8,128)(2,1)S(1)} %fusion.1), channel_id=1, source_target_pairs={{0,4},{4,12},{8,0},{12,8},{1,5},{5,13},{9,1},{13,9},{2,6},{6,14},{... | collective-permute-start | bytes 196616 | tf_op jit(solution)/shard_map/ppermute | solution.py:328
  14.0 6.6 %collective-permute-start.3 = (bf16[2,4,32,128]{3,2,1,0:T(8,128)(2,1)S(1)}, bf16[2,4,32,128]{3,2,1,0:T(8,128)(2,1)S(1)}, u32[]{:S(2)}, u32[]{:S(2)}) collective-permute-start(bf16[2,4,32,128]{3,2,1,0:T(8,128)(2,1)S(1)} %fusion.1), channel_id=1, source_target_pairs={{0,12},{4,8},{8,4},{12,0},{1,13},{5,9},{9,5},{13,1},{2,14},{6,10},... | collective-permute-start | bytes 196616 | tf_op jit(solution)/shard_map/ppermute | solution.py:328
  16.5 4.6 %collective-permute-start.2 = (bf16[2,4,32,128]{3,2,1,0:T(8,128)(2,1)S(1)}, bf16[2,4,32,128]{3,2,1,0:T(8,128)(2,1)S(1)}, u32[]{:S(2)}, u32[]{:S(2)}) collective-permute-start(bf16[2,4,32,128]{3,2,1,0:T(8,128)(2,1)S(1)} %fusion.1), channel_id=1, source_target_pairs={{0,8},{4,0},{8,12},{12,4},{1,9},{5,1},{9,13},{13,5},{2,10},{6,2},{... | collective-permute-start | bytes 196616 | tf_op jit(solution)/shard_map/ppermute | solution.py:328
  21.3 5.0 %collective-permute-start.6 = (bf16[4,4,32,128]{3,2,1,0:T(8,128)(2,1)S(1)}, bf16[4,4,32,128]{3,2,1,0:T(8,128)(2,1)S(1)}, u32[]{:S(2)}, u32[]{:S(2)}) collective-permute-start(bf16[4,4,32,128]{3,2,1,0:T(8,128)(2,1)S(1)} %select_select_fusion.rest_0_), channel_id=1, source_target_pairs={{0,2},{2,0},{1,3},{3,1},{4,6},{6,4},{5,7},{7,5},{8,10},{10,8},{9,1... | collective-permute-start | bytes 393224 | tf_op jit(solution)/shard_map/ppermute | solution.py:309
  22.8 6.9 %collective-permute-start.7 = (bf16[4,4,32,128]{3,2,1,0:T(8,128)(2,1)S(1)}, bf16[4,4,32,128]{3,2,1,0:T(8,128)(2,1)S(1)}, u32[]{:S(2)}, u32[]{:S(2)}) collective-permute-start(bf16[4,4,32,128]{3,2,1,0:T(8,128)(2,1)S(1)} %select_select_fusion.rest_0_), channel_id=1, source_target_pairs={{0,1},{1,0},{2,3},{3,2},{4,5},{5,4},{6,7},{7,6},{8,9},{9,8},{10,11... | collective-permute-start | bytes 393224 | tf_op jit(solution)/shard_map/ppermute | solution.py:309
  26.3 3.5 %collective-permute-start.8 = (bf16[4,4,32,128]{3,2,1,0:T(8,128)(2,1)S(1)}, bf16[4,4,32,128]{3,2,1,0:T(8,128)(2,1)S(1)}, u32[]{:S(2)}, u32[]{:S(2)}) collective-permute-start(bf16[4,4,32,128]{3,2,1,0:T(8,128)(2,1)S(1)} %collective-permute-done.6.rest_1_), channel_id=1, source_target_pairs={{0,1},{1,0},{2,3},{3,2},{4,5},{5,4},{6,7},{7,6},{8,9},{9,8},{10,11... | collective-permute-start | bytes 393224 | tf_op jit(solution)/shard_map/ppermute | solution.py:309
  26.3 1.5 %collective-permute-start.5 = (bf16[4,4,16,128]{3,2,1,0:T(8,128)(2,1)S(1)}, bf16[4,4,16,128]{3,2,1,0:T(8,128)(2,1)S(1)}, u32[]{:S(2)}, u32[]{:S(2)}) collective-permute-start(bf16[4,4,16,128]{3,2,1,0:T(8,128)(2,1)S(1)} %get-tuple-element.11), channel_id=1, source_target_pairs={{0,1},{1,0},{2,3},{3,2},{4,5},{5,4},{6,7},{7,6},{8,9},{9,8},{10,11... | collective-permute-start | bytes 196616 | tf_op jit(solution)/shard_map/ppermute | solution.py:309

commit v5 on v4

--- a/solution.py
+++ b/solution.py
@@ -222,33 +222,26 @@
     )(right, *sinks)
 
 
-def loops_kernel(place_hbm, space_ref, half_ref, *rest, spaces):
-    sources = rest[:-4]
-    out_hbm, place_ref, stage_ref, sems = rest[-4:]
-    pairs, moms, rows, spinors, width = stage_ref.shape
-    spins = len(sources) // spaces
-    part = moms // spins
+def loops_kernel(place_ref, half_ref, *rest, spaces, spins, back):
+    sources = rest[:spaces]
+    out_hbm, stage_ref, sem = rest[-3:]
+    pairs, part, rows, spinors, width = stage_ref.shape
     block = sources[0].shape[2]
     count = rows * spinors
-    place_copy = pltpu.make_async_copy(place_hbm, place_ref, sems.at[1])
-    place_copy.start()
-    here = [
-        jnp.broadcast_to(space_ref[...], (block, width)) == space for space in range(spaces)
-    ]
+    where = jnp.broadcast_to(place_ref[:1, :], (block, width))
+    here = [where == space for space in range(spaces)]
+    owner = lax.rem(place_ref[1, 0] + spins - back, spins)
     zeros = jnp.zeros((width, width), jnp.bfloat16)
     for k in range(pairs):
-        for m in range(0, moms, 2):
+        for m in range(0, part, 2):
             rights = []
             for i in range(2):
-                given_blocks = [
-                    sources[(m + i) // part * spaces + j][k, (m + i) % part].astype(jnp.float32)
-                    for j in range(spaces)
-                ]
+                blocks = [source[k, m + i].astype(jnp.float32) for source in sources]
                 ordered = []
                 for r in range(spaces):
-                    value = given_blocks[0]
+                    value = blocks[0]
                     for j in range(1, spaces):
-                        value = jnp.where(here[(r + j) % spaces], given_blocks[j], value)
+                        value = jnp.where(here[(r + j) % spaces], blocks[j], value)
                     ordered.append(value)
                 source = jnp.concatenate(ordered, axis=0)
                 turned = swapped(source, -1.0, 1.0)
@@ -260,8 +253,9 @@
                 ],
                 axis=0,
             )
+            first = (back * part + m) * count
             left = jnp.concatenate(
-                [half_ref[k, (m + i) * count : (m + i + 1) * count] for i in range(2)], axis=1
+                [half_ref[k, first + i * count : first + (i + 1) * count] for i in range(2)], axis=1
             )
             product = lax.dot_general(
                 left, right, (((1,), (1,)), ((), ())), preferred_element_type=jnp.float32
@@ -270,38 +264,30 @@
                 stage_ref[k, m + i] = product[:, i * width : (i + 1) * width].reshape(
                     rows, spinors, width
                 )
-            if k == 0 and m == 0:
-                place_copy.wait()
-                spin = place_ref[1]
-            if (m + 2) % part == 0:
-                owner = lax.rem(spin + spins - m // part, spins)
-                pltpu.make_async_copy(
-                    stage_ref.at[k, pl.ds(m + 2 - part, part)],
-                    out_hbm.at[k, pl.ds(owner * part, part)],
-                    sems.at[0],
-                ).start()
-    pltpu.make_async_copy(stage_ref, out_hbm, sems.at[0]).wait()
-
-
-def loops(place, space_row, half, sources):
+            pltpu.make_async_copy(
+                stage_ref.at[k, pl.ds(m, 2)], out_hbm.at[k, pl.ds(owner * part + m, 2)], sem
+            ).start()
+    pltpu.make_async_copy(stage_ref, out_hbm.at[:, pl.ds(owner * part, part)], sem).wait()
+
+
+def loops(place_rows, half, sources, back, spins, before):
     pairs, lines, width = half.shape
-    spins, spaces = len(sources), len(sources[0])
-    _, part, _, _ = sources[0][0].shape
-    moms = spins * part
-    shape = (pairs, moms, lines // (moms * SPINS), SPINS, width)
-    return pl.pallas_call(
-        functools.partial(loops_kernel, spaces=spaces),
-        out_shape=jax.ShapeDtypeStruct(shape, jnp.bfloat16),
-        in_specs=[ANY, VMEM, VMEM] + [VMEM] * (spaces * spins),
+    spaces = len(sources)
+    _, part, _, _ = sources[0].shape
+    rows = lines // (spins * part * SPINS)
+    operands = [place_rows, half, *sources] + ([] if before is None else [before])
+    return pl.pallas_call(
+        functools.partial(loops_kernel, spaces=spaces, spins=spins, back=back),
+        out_shape=jax.ShapeDtypeStruct((pairs, spins * part, rows, SPINS, width), jnp.bfloat16),
+        in_specs=[VMEM] * (2 + spaces) + ([] if before is None else [HBM]),
         out_specs=HBM,
         scratch_shapes=[
-            pltpu.SMEM(place.shape, jnp.int32),
-            pltpu.VMEM(shape, jnp.bfloat16),
-            pltpu.SemaphoreType.DMA((2,)),
+            pltpu.VMEM((pairs, part, rows, SPINS, width), jnp.bfloat16),
+            pltpu.SemaphoreType.DMA,
         ],
+        input_output_aliases={} if before is None else {2 + spaces: 0},
         compiler_params=params(16),
-        name="loops",
-    )(place, space_row, half, *[block for group in sources for block in group])
+    )(*operands)
 
 
 def shifted(value, axis, by):
@@ -350,6 +336,7 @@
     spins = lax.axis_size("spin")
     slots = eigenvectors.shape[0]
     place = jnp.stack([lax.axis_index("space"), lax.axis_index("spin")]).astype(jnp.int32)
+    place_rows = jnp.broadcast_to(place[:, None], (2, 2 * perambulators.shape[1]))
     times = slot_map.shape[0]
     named = time_pairs[:, :, None] == lax.iota(jnp.int32, times)
     slot = jnp.sum(jnp.where(named, slot_map, 0), axis=-1)
@@ -387,9 +374,11 @@
     half = halfway(right, sinks)
     far = around(source_share, "space")
     near = [around(value, "spin") for value in far]
-    sources = [[group[i] for group in near] for i in range(spins)]
-    space_row = jnp.full((1, perambulators.shape[1] * 2), lax.axis_index("space"), jnp.int32)
-    return loops(place, space_row, half, sources)
+    result = None
+    for back in range(spins):
+        sources = [group[back] for group in near]
+        result = loops(place_rows, half, sources, back, spins, result)
+    return result
 
 
 def solution(mesh):

time: 32.1 us -> 32.6 us (1.016)
  Pallas kernels: 8.67 us -> 9.08 us
    pallas_call x1 -> x2, Pallas kernels: 2.19 us -> 2.6 us  [loops(): pl.pallas_call(functools.partial(loops_kernel, spaces=spaces, spins=spins...]
  transfers between devices with their start and end apart: 9 -> 9, of which waited for: 5 -> 5; matrix products, arithmetic and copies ran while one was open for 6% -> 7% of each run, Pallas kernels for 11% -> 15%
where the time goes in v5:
time: 32.6 us; the launch traced here: 32.4 us
  starting transfers between devices  11.3 us (35%)
  waiting for transfers between devices  9.52 us (29%)
  Pallas kernels  9.08 us (28%)
  other arithmetic  2.28 us (7%)
    ppermute x6, waiting for transfers between devices, shifted(): lax.ppermute(value, axis, [(i, (i + by) % size) for i in range(size)])  6.49 us
    ppermute x3, starting transfers between devices, exchanged(): parts.append(lax.ppermute(value, axis, list(enumerate(to))))  5.93 us
    ppermute x6, starting transfers between devices, shifted(): lax.ppermute(value, axis, [(i, (i + by) % size) for i in range(size)])  5.33 us
    ppermute x3, waiting for transfers between devices, exchanged(): parts.append(lax.ppermute(value, axis, list(enumerate(to))))  3.03 us
    pallas_call x1, Pallas kernels, given(): pl.pallas_call(given_kernel, out_shape=[jax.ShapeDtypeStruct(shape, jnp.f...  2.82 us
    pallas_call x2, Pallas kernels, loops(): pl.pallas_call(functools.partial(loops_kernel, spaces=spaces, spins=spins...  2.6 us
    pallas_call x1, Pallas kernels, halfway(): pl.pallas_call(halfway_kernel, out_shape=jax.ShapeDtypeStruct((pairs, lin...  1.95 us
    pallas_call x1, Pallas kernels, kept(): pl.pallas_call(kept_kernel, out_shape=jax.ShapeDtypeStruct(shape, jnp.flo...  1.33 us
  transfers between devices with their start and end apart: 9, of which 5 were waited for; matrix products, arithmetic and copies ran while one was open for 7% of the time, Pallas kernels for 15%

profile of v5, /device:TPU:0, one launch (start us, length us, event | category | flops | bytes accessed | tf_op | source)
XLA Modules:
  0.0 32.4 jit_solution(5328124039112621515)
XLA Ops:
  0.0 0.1 pad_add_fusion.place_hbm
  0.1 2.8 %given.1 = (f32[2,2,4,32,128]{4,3,2,1,0:T(8,128)S(1)}, f32[2,8,512]{2,1,0:T(8,128)S(1)}, bf16[2,3,4,128,128]{4,3,2,1,0:T(8,128)(2,1)S(1)}) custom-call(s32[2]{0:T(128)S(1)} %pad_add_fusion.place_hbm, s32[3,8]{1,0:T(4,128)} %bitcast.57, bf16[2,3,512,128]{3,2,1,0:T(8,128)(2,1)} %bitcast.56), custom_call_target="tpu_custom_call" | custom-call | tf_op jit(solution)/shard_map/given/pallas_call | solution.py:121
  2.9 0.0 copy-start
  2.9 0.6 %collective-permute-start = (f32[2,2,4,32,128]{4,3,2,1,0:T(8,128)S(1)}, f32[2,2,4,32,128]{4,3,2,1,0:T(8,128)S(1)}, u32[]{:S(2)}, u32[]{:S(2)}) collective-permute-start(f32[2,2,4,32,128]{4,3,2,1,0:T(8,128)S(1)} %get-tuple-element.10), channel_id=1, source_target_pairs={{0,1},{1,0},{2,3},{3,2},{4,5},{5,4},{6,7},{7,6},{8,9},{9,8},{10,11... | collective-permute-start | bytes 786440 | tf_op jit(solution)/shard_map/ppermute | solution.py:295
  3.5 0.9 %select_reduce_fusion.1 = s32[4,2]{0,1:T(2,128)S(1)} fusion(s32[8]{0:T(128)} %param.9, s32[4,2]{0,1:T(2,128)} %param.8), kind=kLoop, calls=%fused_computation.17 | loop fusion | flops 184 | bytes 96 | tf_op jit(solution)/shard_map/reduce_sum | solution.py:342
  4.4 0.8 %select_reduce_fusion.2 = s32[4]{0:T(128)S(1)} fusion(s32[4,4]{1,0:T(4,128)} %constant.68.clone, pred[4]{0:T(512)(128)(4,1)S(1)} %iota_compare_fusion.2), kind=kLoop, calls=%fused_computation.19 | loop fusion | flops 28 | bytes 84 | tf_op jit(solution)/shard_map/reduce_sum | solution.py:345
  5.2 0.2 select_reduce_fusion
  5.4 1.3 %kept.1 = f32[2,2,4,32,128]{4,3,2,1,0:T(8,128)S(1)} custom-call(s32[2]{0:T(128)S(1)} %pad_add_fusion.place_hbm, f32[2,8,512]{2,1,0:T(8,128)S(1)} %get-tuple-element.8.table_ref, bf16[2,3,4,128,128]{4,3,2,1,0:T(8,128)(2,1)S(1)} %get-tuple-element.9.turned_ref), custom_call_target="tpu_custom_call" | custom-call | tf_op jit(solution)/shard_map/kept/pallas_call | solution.py:157
  6.7 0.0 collective-permute-done
  6.8 2.6 %collective-permute-start.1 = (bf16[2,4,32,128]{3,2,1,0:T(8,128)(2,1)S(1)}, bf16[2,4,32,128]{3,2,1,0:T(8,128)(2,1)S(1)}, u32[]{:S(2)}, u32[]{:S(2)}) collective-permute-start(bf16[2,4,32,128]{3,2,1,0:T(8,128)(2,1)S(1)} %fusion.2), channel_id=1, source_target_pairs={{0,2},{2,0},{1,3},{3,1},{4,6},{6,4},{5,7},{7,5},{8,10},{10,8},{9,1... | collective-permute-start | bytes 196616 | tf_op jit(solution)/shard_map/ppermute | solution.py:295
  9.5 2.6 %collective-permute-done.1 = bf16[2,4,32,128]{3,2,1,0:T(8,128)(2,1)S(1)} collective-permute-done((bf16[2,4,32,128]{3,2,1,0:T(8,128)(2,1)S(1)}, bf16[2,4,32,128]{3,2,1,0:T(8,128)(2,1)S(1)}, u32[]{:S(2)}, u32[]{:S(2)}) %collective-permute-start.1) | collective-permute-done | bytes 65568 | tf_op jit(solution)/shard_map/ppermute | solution.py:295
  12.1 1.9 %collective-permute-start.4 = (bf16[2,4,32,128]{3,2,1,0:T(8,128)(2,1)S(1)}, bf16[2,4,32,128]{3,2,1,0:T(8,128)(2,1)S(1)}, u32[]{:S(2)}, u32[]{:S(2)}) collective-permute-start(bf16[2,4,32,128]{3,2,1,0:T(8,128)(2,1)S(1)} %fusion.1), channel_id=1, source_target_pairs={{0,4},{4,12},{8,0},{12,8},{1,5},{5,13},{9,1},{13,9},{2,6},{6,14},{... | collective-permute-start | bytes 196616 | tf_op jit(solution)/shard_map/ppermute | solution.py:314
  14.0 2.5 %collective-permute-start.3 = (bf16[2,4,32,128]{3,2,1,0:T(8,128)(2,1)S(1)}, bf16[2,4,32,128]{3,2,1,0:T(8,128)(2,1)S(1)}, u32[]{:S(2)}, u32[]{:S(2)}) collective-permute-start(bf16[2,4,32,128]{3,2,1,0:T(8,128)(2,1)S(1)} %fusion.1), channel_id=1, source_target_pairs={{0,12},{4,8},{8,4},{12,0},{1,13},{5,9},{9,5},{13,1},{2,14},{6,10},... | collective-permute-start | bytes 196616 | tf_op jit(solution)/shard_map/ppermute | solution.py:314
  16.5 1.6 %collective-permute-start.2 = (bf16[2,4,32,128]{3,2,1,0:T(8,128)(2,1)S(1)}, bf16[2,4,32,128]{3,2,1,0:T(8,128)(2,1)S(1)}, u32[]{:S(2)}, u32[]{:S(2)}) collective-permute-start(bf16[2,4,32,128]{3,2,1,0:T(8,128)(2,1)S(1)} %fusion.1), channel_id=1, source_target_pairs={{0,8},{4,0},{8,12},{12,4},{1,9},{5,1},{9,13},{13,5},{2,10},{6,2},{... | collective-permute-start | bytes 196616 | tf_op jit(solution)/shard_map/ppermute | solution.py:314
  18.1 0.0 collective-permute-done.4
  18.1 2.5 %collective-permute-done.3 = bf16[2,4,32,128]{3,2,1,0:T(8,128)(2,1)S(1)} collective-permute-done((bf16[2,4,32,128]{3,2,1,0:T(8,128)(2,1)S(1)}, bf16[2,4,32,128]{3,2,1,0:T(8,128)(2,1)S(1)}, u32[]{:S(2)}, u32[]{:S(2)}) %collective-permute-start.3) | collective-permute-done | bytes 65568 | tf_op jit(solution)/shard_map/ppermute | solution.py:314
  20.6 0.5 %collective-permute-done.2 = bf16[2,4,32,128]{3,2,1,0:T(8,128)(2,1)S(1)} collective-permute-done((bf16[2,4,32,128]{3,2,1,0:T(8,128)(2,1)S(1)}, bf16[2,4,32,128]{3,2,1,0:T(8,128)(2,1)S(1)}, u32[]{:S(2)}, u32[]{:S(2)}) %collective-permute-start.2) | collective-permute-done | bytes 65568 | tf_op jit(solution)/shard_map/ppermute | solution.py:314
  21.1 0.1 select_select_fusion.rest_0_
  21.3 1.6 %collective-permute-start.7 = (bf16[4,4,32,128]{3,2,1,0:T(8,128)(2,1)S(1)}, bf16[4,4,32,128]{3,2,1,0:T(8,128)(2,1)S(1)}, u32[]{:S(2)}, u32[]{:S(2)}) collective-permute-start(bf16[4,4,32,128]{3,2,1,0:T(8,128)(2,1)S(1)} %select_select_fusion.rest_0_), channel_id=1, source_target_pairs={{0,2},{2,0},{1,3},{3,1},{4,6},{6,4},{5,7},{7,5},{8,10},{10,8},{9,1... | collective-permute-start | bytes 393224 | tf_op jit(solution)/shard_map/ppermute | solution.py:295
  22.8 0.0 collective-permute-start.6
  22.8 0.1 select_select_fusion.1
  22.9 3.3 %collective-permute-done.7.rest_1_ = bf16[4,4,32,128]{3,2,1,0:T(8,128)(2,1)S(1)} collective-permute-done((bf16[4,4,32,128]{3,2,1,0:T(8,128)(2,1)S(1)}, bf16[4,4,32,128]{3,2,1,0:T(8,128)(2,1)S(1)}, u32[]{:S(2)}, u32[]{:S(2)}) %collective-permute-start.7) | collective-permute-done | bytes 131104 | tf_op jit(solution)/shard_map/ppermute | solution.py:295
  26.3 0.0 collective-permute-start.8
  26.3 0.6 %collective-permute-start.5 = (bf16[4,4,16,128]{3,2,1,0:T(8,128)(2,1)S(1)}, bf16[4,4,16,128]{3,2,1,0:T(8,128)(2,1)S(1)}, u32[]{:S(2)}, u32[]{:S(2)}) collective-permute-start(bf16[4,4,16,128]{3,2,1,0:T(8,128)(2,1)S(1)} %get-tuple-element.11), channel_id=1, source_target_pairs={{0,1},{1,0},{2,3},{3,2},{4,5},{5,4},{6,7},{7,6},{8,9},{9,8},{10,11... | collective-permute-start | bytes 196616 | tf_op jit(solution)/shard_map/ppermute | solution.py:295
  26.9 0.0 copy-done
  26.9 0.4 %doubled.1.right_ref = bf16[4,128,2048]{2,1,0:T(8,128)(2,1)S(1)} custom-call(bf16[4,64,2048]{2,1,0:T(8,128)(2,1)S(1)} %copy-done), custom_call_target="tpu_custom_call" | custom-call | tf_op jit(solution)/shard_map/doubled/pallas_call | solution.py:185
  27.3 0.5 %collective-permute-done.5.rest_1_ = bf16[4,4,16,128]{3,2,1,0:T(8,128)(2,1)S(1)} collective-permute-done((bf16[4,4,16,128]{3,2,1,0:T(8,128)(2,1)S(1)}, bf16[4,4,16,128]{3,2,1,0:T(8,128)(2,1)S(1)}, u32[]{:S(2)}, u32[]{:S(2)}) %collective-permute-start.5) | collective-permute-done | bytes 65568 | tf_op jit(solution)/shard_map/ppermute | solution.py:295
  27.8 2.0 %halfway.1.half_ref = bf16[4,2048,128]{2,1,0:T(8,128)(2,1)S(1)} custom-call(bf16[4,128,2048]{2,1,0:T(8,128)(2,1)S(1)} %doubled.1.right_ref, bf16[4,4,16,128]{3,2,1,0:T(8,128)(2,1)S(1)} %get-tuple-element.12.rest_0_, bf16[4,4,16,128]{3,2,1,0:T(8,128)(2,1)S(1)} %collective-permute-done.5.rest_1_), custom_call_target="tpu_custom_call" | custom-call | tf_op jit(solution)/shard_map/halfway/pallas_call | solution.py:214
  29.7 0.1 broadcast_in_dim.145.place_ref
  29.8 1.3 %shard_map.64.rest_2_ = bf16[4,8,16,16,128]{4,3,2,1,0:T(8,128)(2,1)} custom-call(s32[2,128]{1,0:T(2,128)S(1)} %broadcast_in_dim.145.place_ref, bf16[4,2048,128]{2,1,0:T(8,128)(2,1)S(1)} %halfway.1.half_ref, bf16[4,4,32,128]{3,2,1,0:T(8,128)(2,1)S(1)} %select_select_fusion.rest_0_, bf16[4,4,32,128]{3,2,1,0:T(8,128)(2,1)S(1)} %collective-permute-done.7.rest_1_), custom_call_target="tpu_custom_call" | custom-call | tf_op jit(solution)/shard_map/pallas_call | solution.py:279
  31.1 0.0 collective-permute-done.6.rest_0_
  31.1 0.0 collective-permute-done.8.rest_1_
  31.1 1.3 %shard_map.65 = bf16[4,8,16,16,128]{4,3,2,1,0:T(8,128)(2,1)} custom-call(s32[2,128]{1,0:T(2,128)S(1)} %broadcast_in_dim.145.place_ref, bf16[4,2048,128]{2,1,0:T(8,128)(2,1)S(1)} %halfway.1.half_ref, bf16[4,4,32,128]{3,2,1,0:T(8,128)(2,1)S(1)} %collective-permute-done.6.rest_0_, ...), custom_call_target="tpu_custom_call", output_to_operand_aliasing={{}: (4, {})} | custom-call | tf_op jit(solution)/shard_map/pallas_call | solution.py:279
  (12 shorter events, 0.1 us)
Async XLA Ops:
  2.9 24.0 %copy-start = (bf16[4,64,2048]{2,1,0:T(8,128)(2,1)S(1)}, bf16[4,64,2048]{2,1,0:T(8,128)(2,1)}, u32[]{:S(2)}) copy-start(bf16[4,64,2048]{2,1,0:T(8,128)(2,1)} %tau_ref.1) | copy-start | bytes 3145732
  2.9 3.8 %collective-permute-start = (f32[2,2,4,32,128]{4,3,2,1,0:T(8,128)S(1)}, f32[2,2,4,32,128]{4,3,2,1,0:T(8,128)S(1)}, u32[]{:S(2)}, u32[]{:S(2)}) collective-permute-start(f32[2,2,4,32,128]{4,3,2,1,0:T(8,128)S(1)} %get-tuple-element.10), channel_id=1, source_target_pairs={{0,1},{1,0},{2,3},{3,2},{4,5},{5,4},{6,7},{7,6},{8,9},{9,8},{10,11... | collective-permute-start | bytes 786440 | tf_op jit(solution)/shard_map/ppermute | solution.py:295
  6.8 5.3 %collective-permute-start.1 = (bf16[2,4,32,128]{3,2,1,0:T(8,128)(2,1)S(1)}, bf16[2,4,32,128]{3,2,1,0:T(8,128)(2,1)S(1)}, u32[]{:S(2)}, u32[]{:S(2)}) collective-permute-start(bf16[2,4,32,128]{3,2,1,0:T(8,128)(2,1)S(1)} %fusion.2), channel_id=1, source_target_pairs={{0,2},{2,0},{1,3},{3,1},{4,6},{6,4},{5,7},{7,5},{8,10},{10,8},{9,1... | collective-permute-start | bytes 196616 | tf_op jit(solution)/shard_map/ppermute | solution.py:295
  12.1 5.9 %collective-permute-start.4 = (bf16[2,4,32,128]{3,2,1,0:T(8,128)(2,1)S(1)}, bf16[2,4,32,128]{3,2,1,0:T(8,128)(2,1)S(1)}, u32[]{:S(2)}, u32[]{:S(2)}) collective-permute-start(bf16[2,4,32,128]{3,2,1,0:T(8,128)(2,1)S(1)} %fusion.1), channel_id=1, source_target_pairs={{0,4},{4,12},{8,0},{12,8},{1,5},{5,13},{9,1},{13,9},{2,6},{6,14},{... | collective-permute-start | bytes 196616 | tf_op jit(solution)/shard_map/ppermute | solution.py:314
  14.0 6.6 %collective-permute-start.3 = (bf16[2,4,32,128]{3,2,1,0:T(8,128)(2,1)S(1)}, bf16[2,4,32,128]{3,2,1,0:T(8,128)(2,1)S(1)}, u32[]{:S(2)}, u32[]{:S(2)}) collective-permute-start(bf16[2,4,32,128]{3,2,1,0:T(8,128)(2,1)S(1)} %fusion.1), channel_id=1, source_target_pairs={{0,12},{4,8},{8,4},{12,0},{1,13},{5,9},{9,5},{13,1},{2,14},{6,10},... | collective-permute-start | bytes 196616 | tf_op jit(solution)/shard_map/ppermute | solution.py:314
  16.5 4.6 %collective-permute-start.2 = (bf16[2,4,32,128]{3,2,1,0:T(8,128)(2,1)S(1)}, bf16[2,4,32,128]{3,2,1,0:T(8,128)(2,1)S(1)}, u32[]{:S(2)}, u32[]{:S(2)}) collective-permute-start(bf16[2,4,32,128]{3,2,1,0:T(8,128)(2,1)S(1)} %fusion.1), channel_id=1, source_target_pairs={{0,8},{4,0},{8,12},{12,4},{1,9},{5,1},{9,13},{13,5},{2,10},{6,2},{... | collective-permute-start | bytes 196616 | tf_op jit(solution)/shard_map/ppermute | solution.py:314
  21.3 5.0 %collective-permute-start.7 = (bf16[4,4,32,128]{3,2,1,0:T(8,128)(2,1)S(1)}, bf16[4,4,32,128]{3,2,1,0:T(8,128)(2,1)S(1)}, u32[]{:S(2)}, u32[]{:S(2)}) collective-permute-start(bf16[4,4,32,128]{3,2,1,0:T(8,128)(2,1)S(1)} %select_select_fusion.rest_0_), channel_id=1, source_target_pairs={{0,2},{2,0},{1,3},{3,1},{4,6},{6,4},{5,7},{7,5},{8,10},{10,8},{9,1... | collective-permute-start | bytes 393224 | tf_op jit(solution)/shard_map/ppermute | solution.py:295
  22.8 8.3 %collective-permute-start.6 = (bf16[4,4,32,128]{3,2,1,0:T(8,128)(2,1)S(1)}, bf16[4,4,32,128]{3,2,1,0:T(8,128)(2,1)S(1)}, u32[]{:S(2)}, u32[]{:S(2)}) collective-permute-start(bf16[4,4,32,128]{3,2,1,0:T(8,128)(2,1)S(1)} %select_select_fusion.rest_0_), channel_id=1, source_target_pairs={{0,1},{1,0},{2,3},{3,2},{4,5},{5,4},{6,7},{7,6},{8,9},{9,8},{10,11... | collective-permute-start | bytes 393224 | tf_op jit(solution)/shard_map/ppermute | solution.py:295
  26.3 4.8 %collective-permute-start.8 = (bf16[4,4,32,128]{3,2,1,0:T(8,128)(2,1)S(1)}, bf16[4,4,32,128]{3,2,1,0:T(8,128)(2,1)S(1)}, u32[]{:S(2)}, u32[]{:S(2)}) collective-permute-start(bf16[4,4,32,128]{3,2,1,0:T(8,128)(2,1)S(1)} %collective-permute-done.7.rest_1_), channel_id=1, source_target_pairs={{0,1},{1,0},{2,3},{3,2},{4,5},{5,4},{6,7},{7,6},{8,9},{9,8},{10,11... | collective-permute-start | bytes 393224 | tf_op jit(solution)/shard_map/ppermute | solution.py:295
  26.3 1.5 %collective-permute-start.5 = (bf16[4,4,16,128]{3,2,1,0:T(8,128)(2,1)S(1)}, bf16[4,4,16,128]{3,2,1,0:T(8,128)(2,1)S(1)}, u32[]{:S(2)}, u32[]{:S(2)}) collective-permute-start(bf16[4,4,16,128]{3,2,1,0:T(8,128)(2,1)S(1)} %get-tuple-element.11), channel_id=1, source_target_pairs={{0,1},{1,0},{2,3},{3,2},{4,5},{5,4},{6,7},{7,6},{8,9},{9,8},{10,11... | collective-permute-start | bytes 196616 | tf_op jit(solution)/shard_map/ppermute | solution.py:295

commit v6 on v5

--- a/solution.py
+++ b/solution.py
@@ -201,8 +201,13 @@
         left = jnp.concatenate([sink[k].reshape(count * rows, width) for sink in sinks], axis=0)
         product = jnp.dot(left, right_ref[k], preferred_element_type=jnp.float32)
         for g in range(SPINS):
-            turn_ref[pl.ds(g, lines, stride=SPINS), :] = product[:, g * width : (g + 1) * width]
-        out_ref[k] = turn_ref[...].astype(jnp.bfloat16)
+            turn_ref[pl.ds(g, lines, stride=SPINS + 1), :] = product[
+                :, g * width : (g + 1) * width
+            ]
+        for n in range(lines):
+            out_ref[k, n * SPINS : (n + 1) * SPINS] = turn_ref[
+                n * (SPINS + 1) : n * (SPINS + 1) + SPINS
+            ].astype(jnp.bfloat16)
         return carry
 
     lax.fori_loop(0, pairs, step, 0)
@@ -216,7 +221,7 @@
         out_shape=jax.ShapeDtypeStruct((pairs, lines, width), jnp.bfloat16),
         in_specs=[VMEM] * (1 + len(sinks)),
         out_specs=VMEM,
-        scratch_shapes=[pltpu.VMEM((lines, width), jnp.float32)],
+        scratch_shapes=[pltpu.VMEM((lines // SPINS * (SPINS + 1) + SPINS, width), jnp.float32)],
         compiler_params=params(8),
         name="halfway",
     )(right, *sinks)

time: 32.6 us -> 31.9 us (0.979)
  Pallas kernels: 9.08 us -> 8.41 us
    pallas_call x1, Pallas kernels: 1.95 us -> 1.28 us  [halfway(): pl.pallas_call(halfway_kernel, out_shape=jax.ShapeDtypeStruct((pairs, lin...]
  transfers between devices with their start and end apart: 9 -> 9, of which waited for: 5 -> 5; matrix products, arithmetic and copies ran while one was open for 7% -> 7% of each run, Pallas kernels for 15% -> 13%
where the time goes in v6:
time: 31.9 us; the launch traced here: 31.8 us
  starting transfers between devices  11.3 us (35%)
  waiting for transfers between devices  9.52 us (30%)
  Pallas kernels  8.41 us (26%)
  other arithmetic  2.28 us (7%)
    ppermute x6, waiting for transfers between devices, shifted(): lax.ppermute(value, axis, [(i, (i + by) % size) for i in range(size)])  6.49 us
    ppermute x3, starting transfers between devices, exchanged(): parts.append(lax.ppermute(value, axis, list(enumerate(to))))  5.93 us
    ppermute x6, starting transfers between devices, shifted(): lax.ppermute(value, axis, [(i, (i + by) % size) for i in range(size)])  5.33 us
    ppermute x3, waiting for transfers between devices, exchanged(): parts.append(lax.ppermute(value, axis, list(enumerate(to))))  3.03 us
    pallas_call x1, Pallas kernels, given(): pl.pallas_call(given_kernel, out_shape=[jax.ShapeDtypeStruct(shape, jnp.f...  2.82 us
    pallas_call x2, Pallas kernels, loops(): pl.pallas_call(functools.partial(loops_kernel, spaces=spaces, spins=spins...  2.6 us
    pallas_call x1, Pallas kernels, kept(): pl.pallas_call(kept_kernel, out_shape=jax.ShapeDtypeStruct(shape, jnp.flo...  1.33 us
    pallas_call x1, Pallas kernels, halfway(): pl.pallas_call(halfway_kernel, out_shape=jax.ShapeDtypeStruct((pairs, lin...  1.28 us
  transfers between devices with their start and end apart: 9, of which 5 were waited for; matrix products, arithmetic and copies ran while one was open for 7% of the time, Pallas kernels for 13%

profile of v6, /device:TPU:0, one launch (start us, length us, event | category | flops | bytes accessed | tf_op | source)
XLA Modules:
  0.0 31.8 jit_solution(12178828195589310728)
XLA Ops:
  0.0 0.1 pad_add_fusion.place_hbm
  0.1 2.8 %given.1 = (f32[2,2,4,32,128]{4,3,2,1,0:T(8,128)S(1)}, f32[2,8,512]{2,1,0:T(8,128)S(1)}, bf16[2,3,4,128,128]{4,3,2,1,0:T(8,128)(2,1)S(1)}) custom-call(s32[2]{0:T(128)S(1)} %pad_add_fusion.place_hbm, s32[3,8]{1,0:T(4,128)} %bitcast.57, bf16[2,3,512,128]{3,2,1,0:T(8,128)(2,1)} %bitcast.56), custom_call_target="tpu_custom_call" | custom-call | tf_op jit(solution)/shard_map/given/pallas_call | solution.py:121
  2.9 0.0 copy-start
  2.9 0.6 %collective-permute-start = (f32[2,2,4,32,128]{4,3,2,1,0:T(8,128)S(1)}, f32[2,2,4,32,128]{4,3,2,1,0:T(8,128)S(1)}, u32[]{:S(2)}, u32[]{:S(2)}) collective-permute-start(f32[2,2,4,32,128]{4,3,2,1,0:T(8,128)S(1)} %get-tuple-element.10), channel_id=1, source_target_pairs={{0,1},{1,0},{2,3},{3,2},{4,5},{5,4},{6,7},{7,6},{8,9},{9,8},{10,11... | collective-permute-start | bytes 786440 | tf_op jit(solution)/shard_map/ppermute | solution.py:300
  3.5 0.9 %select_reduce_fusion.1 = s32[4,2]{0,1:T(2,128)S(1)} fusion(s32[8]{0:T(128)} %param.9, s32[4,2]{0,1:T(2,128)} %param.8), kind=kLoop, calls=%fused_computation.17 | loop fusion | flops 184 | bytes 96 | tf_op jit(solution)/shard_map/reduce_sum | solution.py:347
  4.4 0.8 %select_reduce_fusion.2 = s32[4]{0:T(128)S(1)} fusion(s32[4,4]{1,0:T(4,128)} %constant.68.clone, pred[4]{0:T(512)(128)(4,1)S(1)} %iota_compare_fusion.2), kind=kLoop, calls=%fused_computation.19 | loop fusion | flops 28 | bytes 84 | tf_op jit(solution)/shard_map/reduce_sum | solution.py:350
  5.2 0.2 select_reduce_fusion
  5.4 1.3 %kept.1 = f32[2,2,4,32,128]{4,3,2,1,0:T(8,128)S(1)} custom-call(s32[2]{0:T(128)S(1)} %pad_add_fusion.place_hbm, f32[2,8,512]{2,1,0:T(8,128)S(1)} %get-tuple-element.8.table_ref, bf16[2,3,4,128,128]{4,3,2,1,0:T(8,128)(2,1)S(1)} %get-tuple-element.9.turned_ref), custom_call_target="tpu_custom_call" | custom-call | tf_op jit(solution)/shard_map/kept/pallas_call | solution.py:157
  6.7 0.0 collective-permute-done
  6.8 2.6 %collective-permute-start.1 = (bf16[2,4,32,128]{3,2,1,0:T(8,128)(2,1)S(1)}, bf16[2,4,32,128]{3,2,1,0:T(8,128)(2,1)S(1)}, u32[]{:S(2)}, u32[]{:S(2)}) collective-permute-start(bf16[2,4,32,128]{3,2,1,0:T(8,128)(2,1)S(1)} %fusion.2), channel_id=1, source_target_pairs={{0,2},{2,0},{1,3},{3,1},{4,6},{6,4},{5,7},{7,5},{8,10},{10,8},{9,1... | collective-permute-start | bytes 196616 | tf_op jit(solution)/shard_map/ppermute | solution.py:300
  9.5 2.6 %collective-permute-done.1 = bf16[2,4,32,128]{3,2,1,0:T(8,128)(2,1)S(1)} collective-permute-done((bf16[2,4,32,128]{3,2,1,0:T(8,128)(2,1)S(1)}, bf16[2,4,32,128]{3,2,1,0:T(8,128)(2,1)S(1)}, u32[]{:S(2)}, u32[]{:S(2)}) %collective-permute-start.1) | collective-permute-done | bytes 65568 | tf_op jit(solution)/shard_map/ppermute | solution.py:300
  12.1 1.9 %collective-permute-start.4 = (bf16[2,4,32,128]{3,2,1,0:T(8,128)(2,1)S(1)}, bf16[2,4,32,128]{3,2,1,0:T(8,128)(2,1)S(1)}, u32[]{:S(2)}, u32[]{:S(2)}) collective-permute-start(bf16[2,4,32,128]{3,2,1,0:T(8,128)(2,1)S(1)} %fusion.1), channel_id=1, source_target_pairs={{0,4},{4,12},{8,0},{12,8},{1,5},{5,13},{9,1},{13,9},{2,6},{6,14},{... | collective-permute-start | bytes 196616 | tf_op jit(solution)/shard_map/ppermute | solution.py:319
  14.0 2.5 %collective-permute-start.3 = (bf16[2,4,32,128]{3,2,1,0:T(8,128)(2,1)S(1)}, bf16[2,4,32,128]{3,2,1,0:T(8,128)(2,1)S(1)}, u32[]{:S(2)}, u32[]{:S(2)}) collective-permute-start(bf16[2,4,32,128]{3,2,1,0:T(8,128)(2,1)S(1)} %fusion.1), channel_id=1, source_target_pairs={{0,12},{4,8},{8,4},{12,0},{1,13},{5,9},{9,5},{13,1},{2,14},{6,10},... | collective-permute-start | bytes 196616 | tf_op jit(solution)/shard_map/ppermute | solution.py:319
  16.5 1.6 %collective-permute-start.2 = (bf16[2,4,32,128]{3,2,1,0:T(8,128)(2,1)S(1)}, bf16[2,4,32,128]{3,2,1,0:T(8,128)(2,1)S(1)}, u32[]{:S(2)}, u32[]{:S(2)}) collective-permute-start(bf16[2,4,32,128]{3,2,1,0:T(8,128)(2,1)S(1)} %fusion.1), channel_id=1, source_target_pairs={{0,8},{4,0},{8,12},{12,4},{1,9},{5,1},{9,13},{13,5},{2,10},{6,2},{... | collective-permute-start | bytes 196616 | tf_op jit(solution)/shard_map/ppermute | solution.py:319
  18.1 0.0 collective-permute-done.4
  18.1 2.5 %collective-permute-done.3 = bf16[2,4,32,128]{3,2,1,0:T(8,128)(2,1)S(1)} collective-permute-done((bf16[2,4,32,128]{3,2,1,0:T(8,128)(2,1)S(1)}, bf16[2,4,32,128]{3,2,1,0:T(8,128)(2,1)S(1)}, u32[]{:S(2)}, u32[]{:S(2)}) %collective-permute-start.3) | collective-permute-done | bytes 65568 | tf_op jit(solution)/shard_map/ppermute | solution.py:319
  20.6 0.5 %collective-permute-done.2 = bf16[2,4,32,128]{3,2,1,0:T(8,128)(2,1)S(1)} collective-permute-done((bf16[2,4,32,128]{3,2,1,0:T(8,128)(2,1)S(1)}, bf16[2,4,32,128]{3,2,1,0:T(8,128)(2,1)S(1)}, u32[]{:S(2)}, u32[]{:S(2)}) %collective-permute-start.2) | collective-permute-done | bytes 65568 | tf_op jit(solution)/shard_map/ppermute | solution.py:319
  21.1 0.1 select_select_fusion.rest_0_
  21.3 1.6 %collective-permute-start.7 = (bf16[4,4,32,128]{3,2,1,0:T(8,128)(2,1)S(1)}, bf16[4,4,32,128]{3,2,1,0:T(8,128)(2,1)S(1)}, u32[]{:S(2)}, u32[]{:S(2)}) collective-permute-start(bf16[4,4,32,128]{3,2,1,0:T(8,128)(2,1)S(1)} %select_select_fusion.rest_0_), channel_id=1, source_target_pairs={{0,2},{2,0},{1,3},{3,1},{4,6},{6,4},{5,7},{7,5},{8,10},{10,8},{9,1... | collective-permute-start | bytes 393224 | tf_op jit(solution)/shard_map/ppermute | solution.py:300
  22.8 0.0 collective-permute-start.6
  22.8 0.1 select_select_fusion.1
  22.9 3.3 %collective-permute-done.7.rest_1_ = bf16[4,4,32,128]{3,2,1,0:T(8,128)(2,1)S(1)} collective-permute-done((bf16[4,4,32,128]{3,2,1,0:T(8,128)(2,1)S(1)}, bf16[4,4,32,128]{3,2,1,0:T(8,128)(2,1)S(1)}, u32[]{:S(2)}, u32[]{:S(2)}) %collective-permute-start.7) | collective-permute-done | bytes 131104 | tf_op jit(solution)/shard_map/ppermute | solution.py:300
  26.3 0.0 collective-permute-start.8
  26.3 0.6 %collective-permute-start.5 = (bf16[4,4,16,128]{3,2,1,0:T(8,128)(2,1)S(1)}, bf16[4,4,16,128]{3,2,1,0:T(8,128)(2,1)S(1)}, u32[]{:S(2)}, u32[]{:S(2)}) collective-permute-start(bf16[4,4,16,128]{3,2,1,0:T(8,128)(2,1)S(1)} %get-tuple-element.11), channel_id=1, source_target_pairs={{0,1},{1,0},{2,3},{3,2},{4,5},{5,4},{6,7},{7,6},{8,9},{9,8},{10,11... | collective-permute-start | bytes 196616 | tf_op jit(solution)/shard_map/ppermute | solution.py:300
  26.9 0.0 copy-done
  26.9 0.4 %doubled.1.right_ref = bf16[4,128,2048]{2,1,0:T(8,128)(2,1)S(1)} custom-call(bf16[4,64,2048]{2,1,0:T(8,128)(2,1)S(1)} %copy-done), custom_call_target="tpu_custom_call" | custom-call | tf_op jit(solution)/shard_map/doubled/pallas_call | solution.py:185
  27.3 0.5 %collective-permute-done.5.rest_1_ = bf16[4,4,16,128]{3,2,1,0:T(8,128)(2,1)S(1)} collective-permute-done((bf16[4,4,16,128]{3,2,1,0:T(8,128)(2,1)S(1)}, bf16[4,4,16,128]{3,2,1,0:T(8,128)(2,1)S(1)}, u32[]{:S(2)}, u32[]{:S(2)}) %collective-permute-start.5) | collective-permute-done | bytes 65568 | tf_op jit(solution)/shard_map/ppermute | solution.py:300
  27.8 1.3 %halfway.1.half_ref = bf16[4,2048,128]{2,1,0:T(8,128)(2,1)S(1)} custom-call(bf16[4,128,2048]{2,1,0:T(8,128)(2,1)S(1)} %doubled.1.right_ref, bf16[4,4,16,128]{3,2,1,0:T(8,128)(2,1)S(1)} %get-tuple-element.12.rest_0_, bf16[4,4,16,128]{3,2,1,0:T(8,128)(2,1)S(1)} %collective-permute-done.5.rest_1_), custom_call_target="tpu_custom_call" | custom-call | tf_op jit(solution)/shard_map/halfway/pallas_call | solution.py:219
  29.1 0.1 broadcast_in_dim.145.place_ref
  29.1 1.3 %shard_map.64.rest_2_ = bf16[4,8,16,16,128]{4,3,2,1,0:T(8,128)(2,1)} custom-call(s32[2,128]{1,0:T(2,128)S(1)} %broadcast_in_dim.145.place_ref, bf16[4,2048,128]{2,1,0:T(8,128)(2,1)S(1)} %halfway.1.half_ref, bf16[4,4,32,128]{3,2,1,0:T(8,128)(2,1)S(1)} %select_select_fusion.rest_0_, bf16[4,4,32,128]{3,2,1,0:T(8,128)(2,1)S(1)} %collective-permute-done.7.rest_1_), custom_call_target="tpu_custom_call" | custom-call | tf_op jit(solution)/shard_map/pallas_call | solution.py:284
  30.4 0.0 collective-permute-done.6.rest_0_
  30.4 0.0 collective-permute-done.8.rest_1_
  30.5 1.3 %shard_map.65 = bf16[4,8,16,16,128]{4,3,2,1,0:T(8,128)(2,1)} custom-call(s32[2,128]{1,0:T(2,128)S(1)} %broadcast_in_dim.145.place_ref, bf16[4,2048,128]{2,1,0:T(8,128)(2,1)S(1)} %halfway.1.half_ref, bf16[4,4,32,128]{3,2,1,0:T(8,128)(2,1)S(1)} %collective-permute-done.6.rest_0_, ...), custom_call_target="tpu_custom_call", output_to_operand_aliasing={{}: (4, {})} | custom-call | tf_op jit(solution)/shard_map/pallas_call | solution.py:284
  (12 shorter events, 0.1 us)
Async XLA Ops:
  2.9 24.0 %copy-start = (bf16[4,64,2048]{2,1,0:T(8,128)(2,1)S(1)}, bf16[4,64,2048]{2,1,0:T(8,128)(2,1)}, u32[]{:S(2)}) copy-start(bf16[4,64,2048]{2,1,0:T(8,128)(2,1)} %tau_ref.1) | copy-start | bytes 3145732
  2.9 3.8 %collective-permute-start = (f32[2,2,4,32,128]{4,3,2,1,0:T(8,128)S(1)}, f32[2,2,4,32,128]{4,3,2,1,0:T(8,128)S(1)}, u32[]{:S(2)}, u32[]{:S(2)}) collective-permute-start(f32[2,2,4,32,128]{4,3,2,1,0:T(8,128)S(1)} %get-tuple-element.10), channel_id=1, source_target_pairs={{0,1},{1,0},{2,3},{3,2},{4,5},{5,4},{6,7},{7,6},{8,9},{9,8},{10,11... | collective-permute-start | bytes 786440 | tf_op jit(solution)/shard_map/ppermute | solution.py:300
  6.8 5.3 %collective-permute-start.1 = (bf16[2,4,32,128]{3,2,1,0:T(8,128)(2,1)S(1)}, bf16[2,4,32,128]{3,2,1,0:T(8,128)(2,1)S(1)}, u32[]{:S(2)}, u32[]{:S(2)}) collective-permute-start(bf16[2,4,32,128]{3,2,1,0:T(8,128)(2,1)S(1)} %fusion.2), channel_id=1, source_target_pairs={{0,2},{2,0},{1,3},{3,1},{4,6},{6,4},{5,7},{7,5},{8,10},{10,8},{9,1... | collective-permute-start | bytes 196616 | tf_op jit(solution)/shard_map/ppermute | solution.py:300
  12.1 5.9 %collective-permute-start.4 = (bf16[2,4,32,128]{3,2,1,0:T(8,128)(2,1)S(1)}, bf16[2,4,32,128]{3,2,1,0:T(8,128)(2,1)S(1)}, u32[]{:S(2)}, u32[]{:S(2)}) collective-permute-start(bf16[2,4,32,128]{3,2,1,0:T(8,128)(2,1)S(1)} %fusion.1), channel_id=1, source_target_pairs={{0,4},{4,12},{8,0},{12,8},{1,5},{5,13},{9,1},{13,9},{2,6},{6,14},{... | collective-permute-start | bytes 196616 | tf_op jit(solution)/shard_map/ppermute | solution.py:319
  14.0 6.6 %collective-permute-start.3 = (bf16[2,4,32,128]{3,2,1,0:T(8,128)(2,1)S(1)}, bf16[2,4,32,128]{3,2,1,0:T(8,128)(2,1)S(1)}, u32[]{:S(2)}, u32[]{:S(2)}) collective-permute-start(bf16[2,4,32,128]{3,2,1,0:T(8,128)(2,1)S(1)} %fusion.1), channel_id=1, source_target_pairs={{0,12},{4,8},{8,4},{12,0},{1,13},{5,9},{9,5},{13,1},{2,14},{6,10},... | collective-permute-start | bytes 196616 | tf_op jit(solution)/shard_map/ppermute | solution.py:319
  16.5 4.6 %collective-permute-start.2 = (bf16[2,4,32,128]{3,2,1,0:T(8,128)(2,1)S(1)}, bf16[2,4,32,128]{3,2,1,0:T(8,128)(2,1)S(1)}, u32[]{:S(2)}, u32[]{:S(2)}) collective-permute-start(bf16[2,4,32,128]{3,2,1,0:T(8,128)(2,1)S(1)} %fusion.1), channel_id=1, source_target_pairs={{0,8},{4,0},{8,12},{12,4},{1,9},{5,1},{9,13},{13,5},{2,10},{6,2},{... | collective-permute-start | bytes 196616 | tf_op jit(solution)/shard_map/ppermute | solution.py:319
  21.3 5.0 %collective-permute-start.7 = (bf16[4,4,32,128]{3,2,1,0:T(8,128)(2,1)S(1)}, bf16[4,4,32,128]{3,2,1,0:T(8,128)(2,1)S(1)}, u32[]{:S(2)}, u32[]{:S(2)}) collective-permute-start(bf16[4,4,32,128]{3,2,1,0:T(8,128)(2,1)S(1)} %select_select_fusion.rest_0_), channel_id=1, source_target_pairs={{0,2},{2,0},{1,3},{3,1},{4,6},{6,4},{5,7},{7,5},{8,10},{10,8},{9,1... | collective-permute-start | bytes 393224 | tf_op jit(solution)/shard_map/ppermute | solution.py:300
  22.8 7.6 %collective-permute-start.6 = (bf16[4,4,32,128]{3,2,1,0:T(8,128)(2,1)S(1)}, bf16[4,4,32,128]{3,2,1,0:T(8,128)(2,1)S(1)}, u32[]{:S(2)}, u32[]{:S(2)}) collective-permute-start(bf16[4,4,32,128]{3,2,1,0:T(8,128)(2,1)S(1)} %select_select_fusion.rest_0_), channel_id=1, source_target_pairs={{0,1},{1,0},{2,3},{3,2},{4,5},{5,4},{6,7},{7,6},{8,9},{9,8},{10,11... | collective-permute-start | bytes 393224 | tf_op jit(solution)/shard_map/ppermute | solution.py:300
  26.3 4.2 %collective-permute-start.8 = (bf16[4,4,32,128]{3,2,1,0:T(8,128)(2,1)S(1)}, bf16[4,4,32,128]{3,2,1,0:T(8,128)(2,1)S(1)}, u32[]{:S(2)}, u32[]{:S(2)}) collective-permute-start(bf16[4,4,32,128]{3,2,1,0:T(8,128)(2,1)S(1)} %collective-permute-done.7.rest_1_), channel_id=1, source_target_pairs={{0,1},{1,0},{2,3},{3,2},{4,5},{5,4},{6,7},{7,6},{8,9},{9,8},{10,11... | collective-permute-start | bytes 393224 | tf_op jit(solution)/shard_map/ppermute | solution.py:300
  26.3 1.5 %collective-permute-start.5 = (bf16[4,4,16,128]{3,2,1,0:T(8,128)(2,1)S(1)}, bf16[4,4,16,128]{3,2,1,0:T(8,128)(2,1)S(1)}, u32[]{:S(2)}, u32[]{:S(2)}) collective-permute-start(bf16[4,4,16,128]{3,2,1,0:T(8,128)(2,1)S(1)} %get-tuple-element.11), channel_id=1, source_target_pairs={{0,1},{1,0},{2,3},{3,2},{4,5},{5,4},{6,7},{7,6},{8,9},{9,8},{10,11... | collective-permute-start | bytes 196616 | tf_op jit(solution)/shard_map/ppermute | solution.py:300

commit v7 on v6

--- a/solution.py
+++ b/solution.py
@@ -366,8 +366,15 @@
     row_share = row_share.astype(jnp.bfloat16)
     arrived = exchanged(row_share, "tm")
     candidates = [value[s] for value in arrived for s in range(slots)]
-    source_share = selected(index[:, 1], candidates)
-    sink_share = selected(index[:, 0], candidates)
+    early = len(candidates) - slots
+    chosen = [selected(index[:, side], candidates[:early]) for side in range(2)]
+    chosen = lax.optimization_barrier(chosen)
+    for n in range(early, len(candidates)):
+        chosen = [
+            jnp.where(index[:, side, None, None, None] == n, candidates[n], chosen[side])
+            for side in range(2)
+        ]
+    sink_share, source_share = chosen
     rows = sink_share.shape[2] // spins
     sinks = []
     for i in range(spins):

time: 31.9 us -> 32 us (level)
  no operation moved by 1% of the time
where the time goes in v7:
time: 32 us; the launch traced here: 31.8 us
  starting transfers between devices  11.2 us (35%)
  waiting for transfers between devices  9.59 us (30%)
  Pallas kernels  8.41 us (26%)
  other arithmetic  2.31 us (7%)
    ppermute x6, waiting for transfers between devices, shifted(): lax.ppermute(value, axis, [(i, (i + by) % size) for i in range(size)])  6.72 us
    ppermute x3, starting transfers between devices, exchanged(): parts.append(lax.ppermute(value, axis, list(enumerate(to))))  5.92 us
    ppermute x6, starting transfers between devices, shifted(): lax.ppermute(value, axis, [(i, (i + by) % size) for i in range(size)])  5.26 us
    ppermute x3, waiting for transfers between devices, exchanged(): parts.append(lax.ppermute(value, axis, list(enumerate(to))))  2.88 us
    pallas_call x1, Pallas kernels, given(): pl.pallas_call(given_kernel, out_shape=[jax.ShapeDtypeStruct(shape, jnp.f...  2.82 us
    pallas_call x2, Pallas kernels, loops(): pl.pallas_call(functools.partial(loops_kernel, spaces=spaces, spins=spins...  2.6 us
    pallas_call x1, Pallas kernels, kept(): pl.pallas_call(kept_kernel, out_shape=jax.ShapeDtypeStruct(shape, jnp.flo...  1.32 us
    pallas_call x1, Pallas kernels, halfway(): pl.pallas_call(halfway_kernel, out_shape=jax.ShapeDtypeStruct((pairs, lin...  1.29 us
  transfers between devices with their start and end apart: 9, of which 5 were waited for; matrix products, arithmetic and copies ran while one was open for 7% of the time, Pallas kernels for 13%

profile of v7, /device:TPU:0, one launch (start us, length us, event | category | flops | bytes accessed | tf_op | source)
XLA Modules:
  0.0 31.8 jit_solution(12836059857430759181)
XLA Ops:
  0.0 0.1 pad_add_fusion.place_hbm
  0.1 2.8 %given.1 = (f32[2,2,4,32,128]{4,3,2,1,0:T(8,128)S(1)}, f32[2,8,512]{2,1,0:T(8,128)S(1)}, bf16[2,3,4,128,128]{4,3,2,1,0:T(8,128)(2,1)S(1)}) custom-call(s32[2]{0:T(128)S(1)} %pad_add_fusion.place_hbm, s32[3,8]{1,0:T(4,128)} %bitcast.57, bf16[2,3,512,128]{3,2,1,0:T(8,128)(2,1)} %bitcast.56), custom_call_target="tpu_custom_call" | custom-call | tf_op jit(solution)/shard_map/given/pallas_call | solution.py:121
  2.9 0.6 %collective-permute-start = (f32[2,2,4,32,128]{4,3,2,1,0:T(8,128)S(1)}, f32[2,2,4,32,128]{4,3,2,1,0:T(8,128)S(1)}, u32[]{:S(2)}, u32[]{:S(2)}) collective-permute-start(f32[2,2,4,32,128]{4,3,2,1,0:T(8,128)S(1)} %get-tuple-element.12), channel_id=1, source_target_pairs={{0,1},{1,0},{2,3},{3,2},{4,5},{5,4},{6,7},{7,6},{8,9},{9,8},{10,11... | collective-permute-start | bytes 786440 | tf_op jit(solution)/shard_map/ppermute | solution.py:300
  3.5 0.9 %select_reduce_fusion.1 = s32[4,2]{0,1:T(2,128)S(1)} fusion(s32[8]{0:T(128)} %param.9, s32[4,2]{0,1:T(2,128)} %param.8), kind=kLoop, calls=%fused_computation.19 | loop fusion | flops 184 | bytes 96 | tf_op jit(solution)/shard_map/reduce_sum | solution.py:347
  4.4 0.8 %select_reduce_fusion.2 = s32[4]{0:T(128)S(1)} fusion(s32[4,4]{1,0:T(4,128)} %constant.68.clone, pred[4]{0:T(512)(128)(4,1)S(1)} %iota_compare_fusion.2), kind=kLoop, calls=%fused_computation.21 | loop fusion | flops 28 | bytes 84 | tf_op jit(solution)/shard_map/reduce_sum | solution.py:350
  5.2 0.2 select_reduce_fusion
  5.4 0.0 copy-start
  5.4 1.3 %kept.1 = f32[2,2,4,32,128]{4,3,2,1,0:T(8,128)S(1)} custom-call(s32[2]{0:T(128)S(1)} %pad_add_fusion.place_hbm, f32[2,8,512]{2,1,0:T(8,128)S(1)} %get-tuple-element.10.table_ref, bf16[2,3,4,128,128]{4,3,2,1,0:T(8,128)(2,1)S(1)} %get-tuple-element.11.turned_ref), custom_call_target="tpu_custom_call" | custom-call | tf_op jit(solution)/shard_map/kept/pallas_call | solution.py:157
  6.7 0.0 collective-permute-done
  6.8 2.6 %collective-permute-start.1 = (bf16[2,4,32,128]{3,2,1,0:T(8,128)(2,1)S(1)}, bf16[2,4,32,128]{3,2,1,0:T(8,128)(2,1)S(1)}, u32[]{:S(2)}, u32[]{:S(2)}) collective-permute-start(bf16[2,4,32,128]{3,2,1,0:T(8,128)(2,1)S(1)} %fusion.2), channel_id=1, source_target_pairs={{0,2},{2,0},{1,3},{3,1},{4,6},{6,4},{5,7},{7,5},{8,10},{10,8},{9,1... | collective-permute-start | bytes 196616 | tf_op jit(solution)/shard_map/ppermute | solution.py:300
  9.4 2.7 %collective-permute-done.1 = bf16[2,4,32,128]{3,2,1,0:T(8,128)(2,1)S(1)} collective-permute-done((bf16[2,4,32,128]{3,2,1,0:T(8,128)(2,1)S(1)}, bf16[2,4,32,128]{3,2,1,0:T(8,128)(2,1)S(1)}, u32[]{:S(2)}, u32[]{:S(2)}) %collective-permute-start.1) | collective-permute-done | bytes 65568 | tf_op jit(solution)/shard_map/ppermute | solution.py:300
  12.1 1.9 %collective-permute-start.4 = (bf16[2,4,32,128]{3,2,1,0:T(8,128)(2,1)S(1)}, bf16[2,4,32,128]{3,2,1,0:T(8,128)(2,1)S(1)}, u32[]{:S(2)}, u32[]{:S(2)}) collective-permute-start(bf16[2,4,32,128]{3,2,1,0:T(8,128)(2,1)S(1)} %fusion.1), channel_id=1, source_target_pairs={{0,4},{4,12},{8,0},{12,8},{1,5},{5,13},{9,1},{13,9},{2,6},{6,14},{... | collective-permute-start | bytes 196616 | tf_op jit(solution)/shard_map/ppermute | solution.py:319
  14.0 2.5 %collective-permute-start.3 = (bf16[2,4,32,128]{3,2,1,0:T(8,128)(2,1)S(1)}, bf16[2,4,32,128]{3,2,1,0:T(8,128)(2,1)S(1)}, u32[]{:S(2)}, u32[]{:S(2)}) collective-permute-start(bf16[2,4,32,128]{3,2,1,0:T(8,128)(2,1)S(1)} %fusion.1), channel_id=1, source_target_pairs={{0,12},{4,8},{8,4},{12,0},{1,13},{5,9},{9,5},{13,1},{2,14},{6,10},... | collective-permute-start | bytes 196616 | tf_op jit(solution)/shard_map/ppermute | solution.py:319
  16.5 1.6 %collective-permute-start.2 = (bf16[2,4,32,128]{3,2,1,0:T(8,128)(2,1)S(1)}, bf16[2,4,32,128]{3,2,1,0:T(8,128)(2,1)S(1)}, u32[]{:S(2)}, u32[]{:S(2)}) collective-permute-start(bf16[2,4,32,128]{3,2,1,0:T(8,128)(2,1)S(1)} %fusion.1), channel_id=1, source_target_pairs={{0,8},{4,0},{8,12},{12,4},{1,9},{5,1},{9,13},{13,5},{2,10},{6,2},{... | collective-permute-start | bytes 196616 | tf_op jit(solution)/shard_map/ppermute | solution.py:319
  18.1 0.0 collective-permute-done.4
  18.1 2.6 %collective-permute-done.3 = bf16[2,4,32,128]{3,2,1,0:T(8,128)(2,1)S(1)} collective-permute-done((bf16[2,4,32,128]{3,2,1,0:T(8,128)(2,1)S(1)}, bf16[2,4,32,128]{3,2,1,0:T(8,128)(2,1)S(1)}, u32[]{:S(2)}, u32[]{:S(2)}) %collective-permute-start.3) | collective-permute-done | bytes 65568 | tf_op jit(solution)/shard_map/ppermute | solution.py:319
  20.7 0.2 select_select_fusion.2
  20.8 0.3 collective-permute-done.2
  21.1 0.1 select_select_fusion
  21.2 1.6 %collective-permute-start.7 = (bf16[4,4,32,128]{3,2,1,0:T(8,128)(2,1)S(1)}, bf16[4,4,32,128]{3,2,1,0:T(8,128)(2,1)S(1)}, u32[]{:S(2)}, u32[]{:S(2)}) collective-permute-start(bf16[4,4,32,128]{3,2,1,0:T(8,128)(2,1)S(1)} %get-tuple-element.19.rest_0_), channel_id=1, source_target_pairs={{0,2},{2,0},{1,3},{3,1},{4,6},{6,4},{5,7},{7,5},{8,10},{10,8},{9,1... | collective-permute-start | bytes 393224 | tf_op jit(solution)/shard_map/ppermute | solution.py:300
  22.8 0.0 collective-permute-start.6
  22.8 3.5 %collective-permute-done.7.rest_1_ = bf16[4,4,32,128]{3,2,1,0:T(8,128)(2,1)S(1)} collective-permute-done((bf16[4,4,32,128]{3,2,1,0:T(8,128)(2,1)S(1)}, bf16[4,4,32,128]{3,2,1,0:T(8,128)(2,1)S(1)}, u32[]{:S(2)}, u32[]{:S(2)}) %collective-permute-start.7) | collective-permute-done | bytes 131104 | tf_op jit(solution)/shard_map/ppermute | solution.py:300
  26.3 0.0 collective-permute-start.8
  26.3 0.6 %collective-permute-start.5 = (bf16[4,4,16,128]{3,2,1,0:T(8,128)(2,1)S(1)}, bf16[4,4,16,128]{3,2,1,0:T(8,128)(2,1)S(1)}, u32[]{:S(2)}, u32[]{:S(2)}) collective-permute-start(bf16[4,4,16,128]{3,2,1,0:T(8,128)(2,1)S(1)} %get-tuple-element.17), channel_id=1, source_target_pairs={{0,1},{1,0},{2,3},{3,2},{4,5},{5,4},{6,7},{7,6},{8,9},{9,8},{10,11... | collective-permute-start | bytes 196616 | tf_op jit(solution)/shard_map/ppermute | solution.py:300
  26.9 0.0 copy-done
  26.9 0.4 %doubled.1.right_ref = bf16[4,128,2048]{2,1,0:T(8,128)(2,1)S(1)} custom-call(bf16[4,64,2048]{2,1,0:T(8,128)(2,1)S(1)} %copy-done), custom_call_target="tpu_custom_call" | custom-call | tf_op jit(solution)/shard_map/doubled/pallas_call | solution.py:185
  27.3 0.5 %collective-permute-done.5.rest_1_ = bf16[4,4,16,128]{3,2,1,0:T(8,128)(2,1)S(1)} collective-permute-done((bf16[4,4,16,128]{3,2,1,0:T(8,128)(2,1)S(1)}, bf16[4,4,16,128]{3,2,1,0:T(8,128)(2,1)S(1)}, u32[]{:S(2)}, u32[]{:S(2)}) %collective-permute-start.5) | collective-permute-done | bytes 65568 | tf_op jit(solution)/shard_map/ppermute | solution.py:300
  27.8 1.3 %halfway.1.half_ref = bf16[4,2048,128]{2,1,0:T(8,128)(2,1)S(1)} custom-call(bf16[4,128,2048]{2,1,0:T(8,128)(2,1)S(1)} %doubled.1.right_ref, bf16[4,4,16,128]{3,2,1,0:T(8,128)(2,1)S(1)} %get-tuple-element.18.rest_0_, bf16[4,4,16,128]{3,2,1,0:T(8,128)(2,1)S(1)} %collective-permute-done.5.rest_1_), custom_call_target="tpu_custom_call" | custom-call | tf_op jit(solution)/shard_map/halfway/pallas_call | solution.py:219
  29.1 0.1 broadcast_in_dim.145.place_ref
  29.1 1.3 %shard_map.64.rest_2_ = bf16[4,8,16,16,128]{4,3,2,1,0:T(8,128)(2,1)} custom-call(s32[2,128]{1,0:T(2,128)S(1)} %broadcast_in_dim.145.place_ref, bf16[4,2048,128]{2,1,0:T(8,128)(2,1)S(1)} %halfway.1.half_ref, bf16[4,4,32,128]{3,2,1,0:T(8,128)(2,1)S(1)} %get-tuple-element.19.rest_0_, bf16[4,4,32,128]{3,2,1,0:T(8,128)(2,1)S(1)} %collective-permute-done.7.rest_1_), custom_call_target="tpu_custom_call" | custom-call | tf_op jit(solution)/shard_map/pallas_call | solution.py:284
  30.4 0.0 collective-permute-done.6.rest_0_
  30.4 0.0 collective-permute-done.8.rest_1_
  30.5 1.3 %shard_map.65 = bf16[4,8,16,16,128]{4,3,2,1,0:T(8,128)(2,1)} custom-call(s32[2,128]{1,0:T(2,128)S(1)} %broadcast_in_dim.145.place_ref, bf16[4,2048,128]{2,1,0:T(8,128)(2,1)S(1)} %halfway.1.half_ref, bf16[4,4,32,128]{3,2,1,0:T(8,128)(2,1)S(1)} %collective-permute-done.6.rest_0_, ...), custom_call_target="tpu_custom_call", output_to_operand_aliasing={{}: (4, {})} | custom-call | tf_op jit(solution)/shard_map/pallas_call | solution.py:284
  (12 shorter events, 0.1 us)
Async XLA Ops:
  2.9 3.8 %collective-permute-start = (f32[2,2,4,32,128]{4,3,2,1,0:T(8,128)S(1)}, f32[2,2,4,32,128]{4,3,2,1,0:T(8,128)S(1)}, u32[]{:S(2)}, u32[]{:S(2)}) collective-permute-start(f32[2,2,4,32,128]{4,3,2,1,0:T(8,128)S(1)} %get-tuple-element.12), channel_id=1, source_target_pairs={{0,1},{1,0},{2,3},{3,2},{4,5},{5,4},{6,7},{7,6},{8,9},{9,8},{10,11... | collective-permute-start | bytes 786440 | tf_op jit(solution)/shard_map/ppermute | solution.py:300
  5.4 21.5 %copy-start = (bf16[4,64,2048]{2,1,0:T(8,128)(2,1)S(1)}, bf16[4,64,2048]{2,1,0:T(8,128)(2,1)}, u32[]{:S(2)}) copy-start(bf16[4,64,2048]{2,1,0:T(8,128)(2,1)} %tau_ref.1) | copy-start | bytes 3145732
  6.8 5.3 %collective-permute-start.1 = (bf16[2,4,32,128]{3,2,1,0:T(8,128)(2,1)S(1)}, bf16[2,4,32,128]{3,2,1,0:T(8,128)(2,1)S(1)}, u32[]{:S(2)}, u32[]{:S(2)}) collective-permute-start(bf16[2,4,32,128]{3,2,1,0:T(8,128)(2,1)S(1)} %fusion.2), channel_id=1, source_target_pairs={{0,2},{2,0},{1,3},{3,1},{4,6},{6,4},{5,7},{7,5},{8,10},{10,8},{9,1... | collective-permute-start | bytes 196616 | tf_op jit(solution)/shard_map/ppermute | solution.py:300
  12.1 5.9 %collective-permute-start.4 = (bf16[2,4,32,128]{3,2,1,0:T(8,128)(2,1)S(1)}, bf16[2,4,32,128]{3,2,1,0:T(8,128)(2,1)S(1)}, u32[]{:S(2)}, u32[]{:S(2)}) collective-permute-start(bf16[2,4,32,128]{3,2,1,0:T(8,128)(2,1)S(1)} %fusion.1), channel_id=1, source_target_pairs={{0,4},{4,12},{8,0},{12,8},{1,5},{5,13},{9,1},{13,9},{2,6},{6,14},{... | collective-permute-start | bytes 196616 | tf_op jit(solution)/shard_map/ppermute | solution.py:319
  14.0 6.6 %collective-permute-start.3 = (bf16[2,4,32,128]{3,2,1,0:T(8,128)(2,1)S(1)}, bf16[2,4,32,128]{3,2,1,0:T(8,128)(2,1)S(1)}, u32[]{:S(2)}, u32[]{:S(2)}) collective-permute-start(bf16[2,4,32,128]{3,2,1,0:T(8,128)(2,1)S(1)} %fusion.1), channel_id=1, source_target_pairs={{0,12},{4,8},{8,4},{12,0},{1,13},{5,9},{9,5},{13,1},{2,14},{6,10},... | collective-permute-start | bytes 196616 | tf_op jit(solution)/shard_map/ppermute | solution.py:319
  16.5 4.6 %collective-permute-start.2 = (bf16[2,4,32,128]{3,2,1,0:T(8,128)(2,1)S(1)}, bf16[2,4,32,128]{3,2,1,0:T(8,128)(2,1)S(1)}, u32[]{:S(2)}, u32[]{:S(2)}) collective-permute-start(bf16[2,4,32,128]{3,2,1,0:T(8,128)(2,1)S(1)} %fusion.1), channel_id=1, source_target_pairs={{0,8},{4,0},{8,12},{12,4},{1,9},{5,1},{9,13},{13,5},{2,10},{6,2},{... | collective-permute-start | bytes 196616 | tf_op jit(solution)/shard_map/ppermute | solution.py:319
  21.2 5.0 %collective-permute-start.7 = (bf16[4,4,32,128]{3,2,1,0:T(8,128)(2,1)S(1)}, bf16[4,4,32,128]{3,2,1,0:T(8,128)(2,1)S(1)}, u32[]{:S(2)}, u32[]{:S(2)}) collective-permute-start(bf16[4,4,32,128]{3,2,1,0:T(8,128)(2,1)S(1)} %get-tuple-element.19.rest_0_), channel_id=1, source_target_pairs={{0,2},{2,0},{1,3},{3,1},{4,6},{6,4},{5,7},{7,5},{8,10},{10,8},{9,1... | collective-permute-start | bytes 393224 | tf_op jit(solution)/shard_map/ppermute | solution.py:300
  22.8 7.6 %collective-permute-start.6 = (bf16[4,4,32,128]{3,2,1,0:T(8,128)(2,1)S(1)}, bf16[4,4,32,128]{3,2,1,0:T(8,128)(2,1)S(1)}, u32[]{:S(2)}, u32[]{:S(2)}) collective-permute-start(bf16[4,4,32,128]{3,2,1,0:T(8,128)(2,1)S(1)} %get-tuple-element.19.rest_0_), channel_id=1, source_target_pairs={{0,1},{1,0},{2,3},{3,2},{4,5},{5,4},{6,7},{7,6},{8,9},{9,8},{10,11... | collective-permute-start | bytes 393224 | tf_op jit(solution)/shard_map/ppermute | solution.py:300
  26.3 4.2 %collective-permute-start.8 = (bf16[4,4,32,128]{3,2,1,0:T(8,128)(2,1)S(1)}, bf16[4,4,32,128]{3,2,1,0:T(8,128)(2,1)S(1)}, u32[]{:S(2)}, u32[]{:S(2)}) collective-permute-start(bf16[4,4,32,128]{3,2,1,0:T(8,128)(2,1)S(1)} %collective-permute-done.7.rest_1_), channel_id=1, source_target_pairs={{0,1},{1,0},{2,3},{3,2},{4,5},{5,4},{6,7},{7,6},{8,9},{9,8},{10,11... | collective-permute-start | bytes 393224 | tf_op jit(solution)/shard_map/ppermute | solution.py:300
  26.3 1.5 %collective-permute-start.5 = (bf16[4,4,16,128]{3,2,1,0:T(8,128)(2,1)S(1)}, bf16[4,4,16,128]{3,2,1,0:T(8,128)(2,1)S(1)}, u32[]{:S(2)}, u32[]{:S(2)}) collective-permute-start(bf16[4,4,16,128]{3,2,1,0:T(8,128)(2,1)S(1)} %get-tuple-element.17), channel_id=1, source_target_pairs={{0,1},{1,0},{2,3},{3,2},{4,5},{5,4},{6,7},{7,6},{8,9},{9,8},{10,11... | collective-permute-start | bytes 196616 | tf_op jit(solution)/shard_map/ppermute | solution.py:300

commit v8 on v7

--- a/solution.py
+++ b/solution.py
@@ -32,7 +32,7 @@
     return pltpu.roll(value.astype(jnp.float32), half, 1) * sign
 
 
-def turn_and_sum(lefts, table_ref, first, phased_ref, sum_ref):
+def turn_and_sum(lefts, table_ref, first, phased_ref, sum_ref, at_block=lambda r: r):
     slots, colours, _, tiles, _, width = phased_ref.shape
     half = width // 2
     spaces, _, count, rows, _ = sum_ref.shape
@@ -66,11 +66,11 @@
             block = totals[m // 2][:, m % 2 * width : (m % 2 + 1) * width]
             value = block[:half] + swapped(block[half:], 1.0, -1.0)
             for r in range(spaces):
-                sum_ref[r, s, m] = value[r * rows : (r + 1) * rows]
+                sum_ref[at_block(r), s, m] = value[r * rows : (r + 1) * rows]
 
 
 def given_kernel(place_hbm, mom_hbm, x_hbm, out_ref, table_ref, turned_ref, *scratch):
-    x_ref, place_ref, mom_ref, phased_ref, sum_ref, sems = scratch
+    x_ref, place_ref, mom_ref, phased_ref, sems = scratch
     _, _, sites, width = x_ref.shape
     spaces, _, count, _, _ = out_ref.shape
     moms = mom_ref.shape[1]
@@ -107,9 +107,9 @@
         turned_ref[s, c, t] = value
         return value
 
-    turn_and_sum(lefts, table_ref, count, phased_ref, sum_ref)
-    for j in range(spaces):
-        out_ref[j] = sum_ref[lax.rem(space + j, spaces)]
+    turn_and_sum(
+        lefts, table_ref, count, phased_ref, out_ref, lambda r: lax.rem(r + spaces - space, spaces)
+    )
 
 
 def given(place, mom_t, x, spaces, spins):
@@ -132,7 +132,6 @@
             pltpu.SMEM(place.shape, jnp.int32),
             pltpu.SMEM(mom_t.shape, jnp.int32),
             pltpu.VMEM((slots, colours, count // 2, tiles, 2 * width, width), jnp.bfloat16),
-            pltpu.VMEM(shape, jnp.float32),
             pltpu.SemaphoreType.DMA((3,)),
         ],
         compiler_params=params(20),

time: 32 us -> 31.9 us (level)
  no operation moved by 1% of the time
where the time goes in v8:
time: 31.9 us; the launch traced here: 31.7 us
  starting transfers between devices  11.2 us (35%)
  waiting for transfers between devices  9.58 us (30%)
  Pallas kernels  8.37 us (26%)
  other arithmetic  2.31 us (7%)
    ppermute x6, waiting for transfers between devices, shifted(): lax.ppermute(value, axis, [(i, (i + by) % size) for i in range(size)])  6.71 us
    ppermute x3, starting transfers between devices, exchanged(): parts.append(lax.ppermute(value, axis, list(enumerate(to))))  5.93 us
    ppermute x6, starting transfers between devices, shifted(): lax.ppermute(value, axis, [(i, (i + by) % size) for i in range(size)])  5.27 us
    ppermute x3, waiting for transfers between devices, exchanged(): parts.append(lax.ppermute(value, axis, list(enumerate(to))))  2.87 us
    pallas_call x1, Pallas kernels, given(): pl.pallas_call(given_kernel, out_shape=[jax.ShapeDtypeStruct(shape, jnp.f...  2.79 us
    pallas_call x2, Pallas kernels, loops(): pl.pallas_call(functools.partial(loops_kernel, spaces=spaces, spins=spins...  2.6 us
    pallas_call x1, Pallas kernels, kept(): pl.pallas_call(kept_kernel, out_shape=jax.ShapeDtypeStruct(shape, jnp.flo...  1.32 us
    pallas_call x1, Pallas kernels, halfway(): pl.pallas_call(halfway_kernel, out_shape=jax.ShapeDtypeStruct((pairs, lin...  1.28 us
  transfers between devices with their start and end apart: 9, of which 5 were waited for; matrix products, arithmetic and copies ran while one was open for 7% of the time, Pallas kernels for 13%

profile of v8, /device:TPU:0, one launch (start us, length us, event | category | flops | bytes accessed | tf_op | source)
XLA Modules:
  0.0 31.7 jit_solution(14342041602250320659)
XLA Ops:
  0.0 0.1 pad_add_fusion.place_hbm
  0.1 2.8 %given.1 = (f32[2,2,4,32,128]{4,3,2,1,0:T(8,128)S(1)}, f32[2,8,512]{2,1,0:T(8,128)S(1)}, bf16[2,3,4,128,128]{4,3,2,1,0:T(8,128)(2,1)S(1)}) custom-call(s32[2]{0:T(128)S(1)} %pad_add_fusion.place_hbm, s32[3,8]{1,0:T(4,128)} %bitcast.57, bf16[2,3,512,128]{3,2,1,0:T(8,128)(2,1)} %bitcast.56), custom_call_target="tpu_custom_call" | custom-call | tf_op jit(solution)/shard_map/given/pallas_call | solution.py:121
  2.9 0.6 %collective-permute-start = (f32[2,2,4,32,128]{4,3,2,1,0:T(8,128)S(1)}, f32[2,2,4,32,128]{4,3,2,1,0:T(8,128)S(1)}, u32[]{:S(2)}, u32[]{:S(2)}) collective-permute-start(f32[2,2,4,32,128]{4,3,2,1,0:T(8,128)S(1)} %get-tuple-element.12), channel_id=1, source_target_pairs={{0,1},{1,0},{2,3},{3,2},{4,5},{5,4},{6,7},{7,6},{8,9},{9,8},{10,11... | collective-permute-start | bytes 786440 | tf_op jit(solution)/shard_map/ppermute | solution.py:299
  3.4 0.9 %select_reduce_fusion.1 = s32[4,2]{0,1:T(2,128)S(1)} fusion(s32[8]{0:T(128)} %param.9, s32[4,2]{0,1:T(2,128)} %param.8), kind=kLoop, calls=%fused_computation.19 | loop fusion | flops 184 | bytes 96 | tf_op jit(solution)/shard_map/reduce_sum | solution.py:346
  4.4 0.8 %select_reduce_fusion.2 = s32[4]{0:T(128)S(1)} fusion(s32[4,4]{1,0:T(4,128)} %constant.68.clone, pred[4]{0:T(512)(128)(4,1)S(1)} %iota_compare_fusion.2), kind=kLoop, calls=%fused_computation.21 | loop fusion | flops 28 | bytes 84 | tf_op jit(solution)/shard_map/reduce_sum | solution.py:349
  5.1 0.2 select_reduce_fusion
  5.3 0.0 copy-start
  5.3 1.3 %kept.1 = f32[2,2,4,32,128]{4,3,2,1,0:T(8,128)S(1)} custom-call(s32[2]{0:T(128)S(1)} %pad_add_fusion.place_hbm, f32[2,8,512]{2,1,0:T(8,128)S(1)} %get-tuple-element.10.table_ref, bf16[2,3,4,128,128]{4,3,2,1,0:T(8,128)(2,1)S(1)} %get-tuple-element.11.turned_ref), custom_call_target="tpu_custom_call" | custom-call | tf_op jit(solution)/shard_map/kept/pallas_call | solution.py:156
  6.7 0.0 collective-permute-done
  6.8 2.6 %collective-permute-start.1 = (bf16[2,4,32,128]{3,2,1,0:T(8,128)(2,1)S(1)}, bf16[2,4,32,128]{3,2,1,0:T(8,128)(2,1)S(1)}, u32[]{:S(2)}, u32[]{:S(2)}) collective-permute-start(bf16[2,4,32,128]{3,2,1,0:T(8,128)(2,1)S(1)} %fusion.2), channel_id=1, source_target_pairs={{0,2},{2,0},{1,3},{3,1},{4,6},{6,4},{5,7},{7,5},{8,10},{10,8},{9,1... | collective-permute-start | bytes 196616 | tf_op jit(solution)/shard_map/ppermute | solution.py:299
  9.3 2.7 %collective-permute-done.1 = bf16[2,4,32,128]{3,2,1,0:T(8,128)(2,1)S(1)} collective-permute-done((bf16[2,4,32,128]{3,2,1,0:T(8,128)(2,1)S(1)}, bf16[2,4,32,128]{3,2,1,0:T(8,128)(2,1)S(1)}, u32[]{:S(2)}, u32[]{:S(2)}) %collective-permute-start.1) | collective-permute-done | bytes 65568 | tf_op jit(solution)/shard_map/ppermute | solution.py:299
  12.1 1.9 %collective-permute-start.4 = (bf16[2,4,32,128]{3,2,1,0:T(8,128)(2,1)S(1)}, bf16[2,4,32,128]{3,2,1,0:T(8,128)(2,1)S(1)}, u32[]{:S(2)}, u32[]{:S(2)}) collective-permute-start(bf16[2,4,32,128]{3,2,1,0:T(8,128)(2,1)S(1)} %fusion.1), channel_id=1, source_target_pairs={{0,4},{4,12},{8,0},{12,8},{1,5},{5,13},{9,1},{13,9},{2,6},{6,14},{... | collective-permute-start | bytes 196616 | tf_op jit(solution)/shard_map/ppermute | solution.py:318
  14.0 2.5 %collective-permute-start.3 = (bf16[2,4,32,128]{3,2,1,0:T(8,128)(2,1)S(1)}, bf16[2,4,32,128]{3,2,1,0:T(8,128)(2,1)S(1)}, u32[]{:S(2)}, u32[]{:S(2)}) collective-permute-start(bf16[2,4,32,128]{3,2,1,0:T(8,128)(2,1)S(1)} %fusion.1), channel_id=1, source_target_pairs={{0,12},{4,8},{8,4},{12,0},{1,13},{5,9},{9,5},{13,1},{2,14},{6,10},... | collective-permute-start | bytes 196616 | tf_op jit(solution)/shard_map/ppermute | solution.py:318
  16.5 1.6 %collective-permute-start.2 = (bf16[2,4,32,128]{3,2,1,0:T(8,128)(2,1)S(1)}, bf16[2,4,32,128]{3,2,1,0:T(8,128)(2,1)S(1)}, u32[]{:S(2)}, u32[]{:S(2)}) collective-permute-start(bf16[2,4,32,128]{3,2,1,0:T(8,128)(2,1)S(1)} %fusion.1), channel_id=1, source_target_pairs={{0,8},{4,0},{8,12},{12,4},{1,9},{5,1},{9,13},{13,5},{2,10},{6,2},{... | collective-permute-start | bytes 196616 | tf_op jit(solution)/shard_map/ppermute | solution.py:318
  18.0 0.0 collective-permute-done.4
  18.0 2.6 %collective-permute-done.3 = bf16[2,4,32,128]{3,2,1,0:T(8,128)(2,1)S(1)} collective-permute-done((bf16[2,4,32,128]{3,2,1,0:T(8,128)(2,1)S(1)}, bf16[2,4,32,128]{3,2,1,0:T(8,128)(2,1)S(1)}, u32[]{:S(2)}, u32[]{:S(2)}) %collective-permute-start.3) | collective-permute-done | bytes 65568 | tf_op jit(solution)/shard_map/ppermute | solution.py:318
  20.6 0.2 select_select_fusion.2
  20.8 0.3 collective-permute-done.2
  21.1 0.1 select_select_fusion
  21.2 1.6 %collective-permute-start.7 = (bf16[4,4,32,128]{3,2,1,0:T(8,128)(2,1)S(1)}, bf16[4,4,32,128]{3,2,1,0:T(8,128)(2,1)S(1)}, u32[]{:S(2)}, u32[]{:S(2)}) collective-permute-start(bf16[4,4,32,128]{3,2,1,0:T(8,128)(2,1)S(1)} %get-tuple-element.19.rest_0_), channel_id=1, source_target_pairs={{0,2},{2,0},{1,3},{3,1},{4,6},{6,4},{5,7},{7,5},{8,10},{10,8},{9,1... | collective-permute-start | bytes 393224 | tf_op jit(solution)/shard_map/ppermute | solution.py:299
  22.8 0.0 collective-permute-start.6
  22.8 3.5 %collective-permute-done.7.rest_1_ = bf16[4,4,32,128]{3,2,1,0:T(8,128)(2,1)S(1)} collective-permute-done((bf16[4,4,32,128]{3,2,1,0:T(8,128)(2,1)S(1)}, bf16[4,4,32,128]{3,2,1,0:T(8,128)(2,1)S(1)}, u32[]{:S(2)}, u32[]{:S(2)}) %collective-permute-start.7) | collective-permute-done | bytes 131104 | tf_op jit(solution)/shard_map/ppermute | solution.py:299
  26.2 0.0 collective-permute-start.8
  26.2 0.6 %collective-permute-start.5 = (bf16[4,4,16,128]{3,2,1,0:T(8,128)(2,1)S(1)}, bf16[4,4,16,128]{3,2,1,0:T(8,128)(2,1)S(1)}, u32[]{:S(2)}, u32[]{:S(2)}) collective-permute-start(bf16[4,4,16,128]{3,2,1,0:T(8,128)(2,1)S(1)} %get-tuple-element.17), channel_id=1, source_target_pairs={{0,1},{1,0},{2,3},{3,2},{4,5},{5,4},{6,7},{7,6},{8,9},{9,8},{10,11... | collective-permute-start | bytes 196616 | tf_op jit(solution)/shard_map/ppermute | solution.py:299
  26.8 0.0 copy-done
  26.8 0.4 %doubled.1.right_ref = bf16[4,128,2048]{2,1,0:T(8,128)(2,1)S(1)} custom-call(bf16[4,64,2048]{2,1,0:T(8,128)(2,1)S(1)} %copy-done), custom_call_target="tpu_custom_call" | custom-call | tf_op jit(solution)/shard_map/doubled/pallas_call | solution.py:184
  27.2 0.5 %collective-permute-done.5.rest_1_ = bf16[4,4,16,128]{3,2,1,0:T(8,128)(2,1)S(1)} collective-permute-done((bf16[4,4,16,128]{3,2,1,0:T(8,128)(2,1)S(1)}, bf16[4,4,16,128]{3,2,1,0:T(8,128)(2,1)S(1)}, u32[]{:S(2)}, u32[]{:S(2)}) %collective-permute-start.5) | collective-permute-done | bytes 65568 | tf_op jit(solution)/shard_map/ppermute | solution.py:299
  27.7 1.3 %halfway.1.half_ref = bf16[4,2048,128]{2,1,0:T(8,128)(2,1)S(1)} custom-call(bf16[4,128,2048]{2,1,0:T(8,128)(2,1)S(1)} %doubled.1.right_ref, bf16[4,4,16,128]{3,2,1,0:T(8,128)(2,1)S(1)} %get-tuple-element.18.rest_0_, bf16[4,4,16,128]{3,2,1,0:T(8,128)(2,1)S(1)} %collective-permute-done.5.rest_1_), custom_call_target="tpu_custom_call" | custom-call | tf_op jit(solution)/shard_map/halfway/pallas_call | solution.py:218
  29.0 0.1 broadcast_in_dim.145.place_ref
  29.1 1.3 %shard_map.64.rest_2_ = bf16[4,8,16,16,128]{4,3,2,1,0:T(8,128)(2,1)} custom-call(s32[2,128]{1,0:T(2,128)S(1)} %broadcast_in_dim.145.place_ref, bf16[4,2048,128]{2,1,0:T(8,128)(2,1)S(1)} %halfway.1.half_ref, bf16[4,4,32,128]{3,2,1,0:T(8,128)(2,1)S(1)} %get-tuple-element.19.rest_0_, bf16[4,4,32,128]{3,2,1,0:T(8,128)(2,1)S(1)} %collective-permute-done.7.rest_1_), custom_call_target="tpu_custom_call" | custom-call | tf_op jit(solution)/shard_map/pallas_call | solution.py:283
  30.4 0.0 collective-permute-done.6.rest_0_
  30.4 0.0 collective-permute-done.8.rest_1_
  30.4 1.3 %shard_map.65 = bf16[4,8,16,16,128]{4,3,2,1,0:T(8,128)(2,1)} custom-call(s32[2,128]{1,0:T(2,128)S(1)} %broadcast_in_dim.145.place_ref, bf16[4,2048,128]{2,1,0:T(8,128)(2,1)S(1)} %halfway.1.half_ref, bf16[4,4,32,128]{3,2,1,0:T(8,128)(2,1)S(1)} %collective-permute-done.6.rest_0_, ...), custom_call_target="tpu_custom_call", output_to_operand_aliasing={{}: (4, {})} | custom-call | tf_op jit(solution)/shard_map/pallas_call | solution.py:283
  (12 shorter events, 0.1 us)
Async XLA Ops:
  2.9 3.8 %collective-permute-start = (f32[2,2,4,32,128]{4,3,2,1,0:T(8,128)S(1)}, f32[2,2,4,32,128]{4,3,2,1,0:T(8,128)S(1)}, u32[]{:S(2)}, u32[]{:S(2)}) collective-permute-start(f32[2,2,4,32,128]{4,3,2,1,0:T(8,128)S(1)} %get-tuple-element.12), channel_id=1, source_target_pairs={{0,1},{1,0},{2,3},{3,2},{4,5},{5,4},{6,7},{7,6},{8,9},{9,8},{10,11... | collective-permute-start | bytes 786440 | tf_op jit(solution)/shard_map/ppermute | solution.py:299
  5.3 21.5 %copy-start = (bf16[4,64,2048]{2,1,0:T(8,128)(2,1)S(1)}, bf16[4,64,2048]{2,1,0:T(8,128)(2,1)}, u32[]{:S(2)}) copy-start(bf16[4,64,2048]{2,1,0:T(8,128)(2,1)} %tau_ref.1) | copy-start | bytes 3145732
  6.8 5.3 %collective-permute-start.1 = (bf16[2,4,32,128]{3,2,1,0:T(8,128)(2,1)S(1)}, bf16[2,4,32,128]{3,2,1,0:T(8,128)(2,1)S(1)}, u32[]{:S(2)}, u32[]{:S(2)}) collective-permute-start(bf16[2,4,32,128]{3,2,1,0:T(8,128)(2,1)S(1)} %fusion.2), channel_id=1, source_target_pairs={{0,2},{2,0},{1,3},{3,1},{4,6},{6,4},{5,7},{7,5},{8,10},{10,8},{9,1... | collective-permute-start | bytes 196616 | tf_op jit(solution)/shard_map/ppermute | solution.py:299
  12.1 5.9 %collective-permute-start.4 = (bf16[2,4,32,128]{3,2,1,0:T(8,128)(2,1)S(1)}, bf16[2,4,32,128]{3,2,1,0:T(8,128)(2,1)S(1)}, u32[]{:S(2)}, u32[]{:S(2)}) collective-permute-start(bf16[2,4,32,128]{3,2,1,0:T(8,128)(2,1)S(1)} %fusion.1), channel_id=1, source_target_pairs={{0,4},{4,12},{8,0},{12,8},{1,5},{5,13},{9,1},{13,9},{2,6},{6,14},{... | collective-permute-start | bytes 196616 | tf_op jit(solution)/shard_map/ppermute | solution.py:318
  14.0 6.6 %collective-permute-start.3 = (bf16[2,4,32,128]{3,2,1,0:T(8,128)(2,1)S(1)}, bf16[2,4,32,128]{3,2,1,0:T(8,128)(2,1)S(1)}, u32[]{:S(2)}, u32[]{:S(2)}) collective-permute-start(bf16[2,4,32,128]{3,2,1,0:T(8,128)(2,1)S(1)} %fusion.1), channel_id=1, source_target_pairs={{0,12},{4,8},{8,4},{12,0},{1,13},{5,9},{9,5},{13,1},{2,14},{6,10},... | collective-permute-start | bytes 196616 | tf_op jit(solution)/shard_map/ppermute | solution.py:318
  16.5 4.6 %collective-permute-start.2 = (bf16[2,4,32,128]{3,2,1,0:T(8,128)(2,1)S(1)}, bf16[2,4,32,128]{3,2,1,0:T(8,128)(2,1)S(1)}, u32[]{:S(2)}, u32[]{:S(2)}) collective-permute-start(bf16[2,4,32,128]{3,2,1,0:T(8,128)(2,1)S(1)} %fusion.1), channel_id=1, source_target_pairs={{0,8},{4,0},{8,12},{12,4},{1,9},{5,1},{9,13},{13,5},{2,10},{6,2},{... | collective-permute-start | bytes 196616 | tf_op jit(solution)/shard_map/ppermute | solution.py:318
  21.2 5.0 %collective-permute-start.7 = (bf16[4,4,32,128]{3,2,1,0:T(8,128)(2,1)S(1)}, bf16[4,4,32,128]{3,2,1,0:T(8,128)(2,1)S(1)}, u32[]{:S(2)}, u32[]{:S(2)}) collective-permute-start(bf16[4,4,32,128]{3,2,1,0:T(8,128)(2,1)S(1)} %get-tuple-element.19.rest_0_), channel_id=1, source_target_pairs={{0,2},{2,0},{1,3},{3,1},{4,6},{6,4},{5,7},{7,5},{8,10},{10,8},{9,1... | collective-permute-start | bytes 393224 | tf_op jit(solution)/shard_map/ppermute | solution.py:299
  22.8 7.6 %collective-permute-start.6 = (bf16[4,4,32,128]{3,2,1,0:T(8,128)(2,1)S(1)}, bf16[4,4,32,128]{3,2,1,0:T(8,128)(2,1)S(1)}, u32[]{:S(2)}, u32[]{:S(2)}) collective-permute-start(bf16[4,4,32,128]{3,2,1,0:T(8,128)(2,1)S(1)} %get-tuple-element.19.rest_0_), channel_id=1, source_target_pairs={{0,1},{1,0},{2,3},{3,2},{4,5},{5,4},{6,7},{7,6},{8,9},{9,8},{10,11... | collective-permute-start | bytes 393224 | tf_op jit(solution)/shard_map/ppermute | solution.py:299
  26.2 4.2 %collective-permute-start.8 = (bf16[4,4,32,128]{3,2,1,0:T(8,128)(2,1)S(1)}, bf16[4,4,32,128]{3,2,1,0:T(8,128)(2,1)S(1)}, u32[]{:S(2)}, u32[]{:S(2)}) collective-permute-start(bf16[4,4,32,128]{3,2,1,0:T(8,128)(2,1)S(1)} %collective-permute-done.7.rest_1_), channel_id=1, source_target_pairs={{0,1},{1,0},{2,3},{3,2},{4,5},{5,4},{6,7},{7,6},{8,9},{9,8},{10,11... | collective-permute-start | bytes 393224 | tf_op jit(solution)/shard_map/ppermute | solution.py:299
  26.2 1.5 %collective-permute-start.5 = (bf16[4,4,16,128]{3,2,1,0:T(8,128)(2,1)S(1)}, bf16[4,4,16,128]{3,2,1,0:T(8,128)(2,1)S(1)}, u32[]{:S(2)}, u32[]{:S(2)}) collective-permute-start(bf16[4,4,16,128]{3,2,1,0:T(8,128)(2,1)S(1)} %get-tuple-element.17), channel_id=1, source_target_pairs={{0,1},{1,0},{2,3},{3,2},{4,5},{5,4},{6,7},{7,6},{8,9},{9,8},{10,11... | collective-permute-start | bytes 196616 | tf_op jit(solution)/shard_map/ppermute | solution.py:299
